TPU v7x, 32 devices: a 4x4x1 block of a 4x4x8 slice. The times are simulated.
32 devices in a mesh: data: 1 (over z), model: 32 (over y, x, core).
Axes of the slice: x: 4, y: 4, z: 1, core: 2. Of those that a mesh axis runs over, the one named last changes fastest.
The devices are a block of a 4x4x8 slice.
Arguments:
- x_in: bfloat16 [1, 4096, 2048], P('data')
- seg_ids: int32 [1, 4096], P('data')
- gain_one: bfloat16 [2048], replicated
- w_qkv: bfloat16 [2048, 6144], P(None, 'model')
- w_out: bfloat16 [32, 64, 2048], P('model')
- gain_two: bfloat16 [2048], replicated
- w_up: bfloat16 [2048, 8192], P(None, 'model')
- w_down: bfloat16 [8192, 2048], P('model')
- d_y: bfloat16 [1, 4096, 2048], P('data')
Outputs:
- output 1: bfloat16 [1, 4096, 2048], P('data')
- output 2: bfloat16 [1, 4096, 2048], P('data')
- output 3: bfloat16 [2048, 6144], P('data', 'model')
- output 4: bfloat16 [32, 64, 2048], P(('data', 'model'))
- output 5: bfloat16 [2048, 8192], P('data', 'model')
- output 6: bfloat16 [8192, 2048], P(('data', 'model'))
- output 7: bfloat16 [2048], P('data')
- output 8: bfloat16 [2048], P('data')
All inputs are finite; a program needn't handle non-finite values.
Results may differ from a plain program's by a relative error of at most 0.02.
Values are sent between devices in bfloat16 or wider.
A program may use at most 768 MiB of HBM per device.

v0:
```python
import jax
import jax.numpy as jnp
from jax import lax
from jax.sharding import PartitionSpec as P

LN_EPS = 1e-5


def layer_norm(x_in, gain):
    x_wide = x_in.astype(jnp.float32)
    row_mean = jnp.mean(x_wide, axis=-1, keepdims=True)
    centered = x_wide - row_mean
    row_var = jnp.mean(centered * centered, axis=-1, keepdims=True)
    return (centered * lax.rsqrt(row_var + LN_EPS) * gain.astype(jnp.float32)).astype(jnp.bfloat16)


def gelu_tanh(up_proj):
    return jax.nn.gelu(up_proj.astype(jnp.float32), approximate=True).astype(jnp.bfloat16)


def block_mask(seg_ids, start, stop):
    q_pos = jnp.arange(start, stop)
    k_pos = jnp.arange(stop)
    causal = q_pos[:, None] >= k_pos[None, :]
    same_doc = seg_ids[:, start:stop, None] == seg_ids[:, None, :stop]
    return (causal[None] & same_doc)[:, None]


def attention_forward(q_all, k_all, v_all, seg_ids, block_len):
    seq_len = q_all.shape[1]
    score_scale = q_all.shape[-1] ** -0.5
    outputs = []
    log_sums = []
    for start in range(0, seq_len, block_len):
        stop = start + block_len
        scores = jnp.einsum('bqnd,bknd->bnqk', q_all[:, start:stop], k_all[:, :stop], preferred_element_type=jnp.float32) * score_scale
        scores = jnp.where(block_mask(seg_ids, start, stop), scores, -1e30)
        row_max = jnp.max(scores, axis=-1, keepdims=True)
        exp_scores = jnp.exp(scores - row_max)
        row_sum = jnp.sum(exp_scores, axis=-1, keepdims=True)
        attn_prob = (exp_scores / row_sum).astype(jnp.bfloat16)
        outputs.append(jnp.einsum('bnqk,bknd->bqnd', attn_prob, v_all[:, :stop], preferred_element_type=jnp.float32).astype(jnp.bfloat16))
        log_sums.append(row_max + jnp.log(row_sum))
    return jnp.concatenate(outputs, axis=1), log_sums


def attention_backward(q_all, k_all, v_all, d_attn, seg_ids, log_sums, block_len):
    seq_len = q_all.shape[1]
    score_scale = q_all.shape[-1] ** -0.5
    d_q_blocks = []
    d_k_sum = jnp.zeros(k_all.shape, jnp.float32)
    d_v_sum = jnp.zeros(v_all.shape, jnp.float32)
    for index, start in enumerate(range(0, seq_len, block_len)):
        stop = start + block_len
        q_blk = q_all[:, start:stop]
        d_out_blk = d_attn[:, start:stop]
        scores = jnp.einsum('bqnd,bknd->bnqk', q_blk, k_all[:, :stop], preferred_element_type=jnp.float32) * score_scale
        scores = jnp.where(block_mask(seg_ids, start, stop), scores, -1e30)
        attn_prob = jnp.exp(scores - log_sums[index])
        d_prob = jnp.einsum('bqnd,bknd->bnqk', d_out_blk, v_all[:, :stop], preferred_element_type=jnp.float32)
        d_score = attn_prob * (d_prob - jnp.sum(attn_prob * d_prob, axis=-1, keepdims=True)) * score_scale
        d_score = d_score.astype(jnp.bfloat16)
        d_q_blocks.append(jnp.einsum('bnqk,bknd->bqnd', d_score, k_all[:, :stop], preferred_element_type=jnp.float32).astype(jnp.bfloat16))
        pad_width = ((0, 0), (0, seq_len - stop), (0, 0), (0, 0))
        d_k_blk = jnp.einsum('bnqk,bqnd->bknd', d_score, q_blk, preferred_element_type=jnp.float32)
        d_v_blk = jnp.einsum('bnqk,bqnd->bknd', attn_prob.astype(jnp.bfloat16), d_out_blk, preferred_element_type=jnp.float32)
        d_k_sum = d_k_sum + jnp.pad(d_k_blk, pad_width)
        d_v_sum = d_v_sum + jnp.pad(d_v_blk, pad_width)
    return jnp.concatenate(d_q_blocks, axis=1), d_k_sum.astype(jnp.bfloat16), d_v_sum.astype(jnp.bfloat16)


def solution(mesh):
    def local_step(x_in, seg_ids, gain_one, w_qkv, w_out, gain_two, w_up, w_down, d_y):
        rows, seq_len = x_in.shape[:2]
        n_local, head_dim = w_out.shape[:2]
        block_len = min(seq_len, 256)
        normed_one, ln_one_pull = jax.vjp(layer_norm, x_in, gain_one)
        qkv_proj = jnp.einsum('bsh,hc->bsc', normed_one, w_qkv, preferred_element_type=jnp.float32).astype(jnp.bfloat16)
        qkv_heads = qkv_proj.reshape(rows, seq_len, n_local, 3, head_dim)
        q_all = qkv_heads[:, :, :, 0]
        k_all = qkv_heads[:, :, :, 1]
        v_all = qkv_heads[:, :, :, 2]
        attn_out, log_sums = attention_forward(q_all, k_all, v_all, seg_ids, block_len)
        part_one = jnp.einsum('bsnd,ndh->bsh', attn_out, w_out, preferred_element_type=jnp.float32).astype(jnp.bfloat16)
        sum_one = lax.psum(part_one, 'model')
        resid = (x_in.astype(jnp.float32) + sum_one.astype(jnp.float32)).astype(jnp.bfloat16)
        normed_two, ln_two_pull = jax.vjp(layer_norm, resid, gain_two)
        up_proj = jnp.einsum('bsh,hf->bsf', normed_two, w_up, preferred_element_type=jnp.float32).astype(jnp.bfloat16)
        gelu_out, gelu_pull = jax.vjp(gelu_tanh, up_proj)
        part_two = jnp.einsum('bsf,fh->bsh', gelu_out, w_down, preferred_element_type=jnp.float32).astype(jnp.bfloat16)
        sum_two = lax.psum(part_two, 'model')
        y_out = (resid.astype(jnp.float32) + sum_two.astype(jnp.float32)).astype(jnp.bfloat16)
        d_w_down = jnp.einsum('bsf,bsh->fh', gelu_out, d_y, preferred_element_type=jnp.float32).astype(jnp.bfloat16)
        d_gelu = jnp.einsum('bsh,fh->bsf', d_y, w_down, preferred_element_type=jnp.float32).astype(jnp.bfloat16)
        (d_up,) = gelu_pull(d_gelu)
        d_w_up = jnp.einsum('bsh,bsf->hf', normed_two, d_up, preferred_element_type=jnp.float32).astype(jnp.bfloat16)
        d_norm_part = jnp.einsum('bsf,hf->bsh', d_up, w_up, preferred_element_type=jnp.float32).astype(jnp.bfloat16)
        d_norm_two = lax.psum(d_norm_part, 'model')
        d_resid_ln, d_gain_two = ln_two_pull(d_norm_two)
        d_resid = d_y + d_resid_ln
        d_w_out = jnp.einsum('bsnd,bsh->ndh', attn_out, d_resid, preferred_element_type=jnp.float32).astype(jnp.bfloat16)
        d_attn = jnp.einsum('bsh,ndh->bsnd', d_resid, w_out, preferred_element_type=jnp.float32).astype(jnp.bfloat16)
        d_q, d_k, d_v = attention_backward(q_all, k_all, v_all, d_attn, seg_ids, log_sums, block_len)
        d_qkv = jnp.stack([d_q, d_k, d_v], axis=3).reshape(rows, seq_len, 3 * n_local * head_dim)
        d_w_qkv = jnp.einsum('bsh,bsc->hc', normed_one, d_qkv, preferred_element_type=jnp.float32).astype(jnp.bfloat16)
        d_input_part = jnp.einsum('bsc,hc->bsh', d_qkv, w_qkv, preferred_element_type=jnp.float32).astype(jnp.bfloat16)
        d_norm_one = lax.psum(d_input_part, 'model')
        d_x_ln, d_gain_one = ln_one_pull(d_norm_one)
        d_x = d_resid + d_x_ln
        return y_out, d_x, d_w_qkv, d_w_out, d_w_up, d_w_down, d_gain_one, d_gain_two

    in_specs = (P('data'), P('data'), P(), P(None, 'model'), P('model'), P(), P(None, 'model'), P('model'), P('data'))
    out_specs = (P('data'), P('data'), P('data', 'model'), P(('data', 'model')), P('data', 'model'), P(('data', 'model')), P('data'), P('data'))
    return jax.shard_map(local_step, mesh=mesh, in_specs=in_specs, out_specs=out_specs, check_vma=False)
```

profile of v0, /device:TPU:97, one launch (start us, length us, event | category | flops | bytes accessed | tf_op | source)
XLA Modules:
  0.0 1003.2 jit_solution(13211243588628942545)
XLA Ops:
  16.3 7.0 convert_reduce_fusion.1
  23.4 3.6 copy-done.2
  27.0 6.5 fusion.16
  34.2 7.0 fusion.26
  41.2 5.6 convolution_convert_fusion.1
  84.4 8.5 convert_bitcast_fusion.3
  93.6 169.9 %all-reduce.35.cloned.1.call-done = bf16[1,4096,2048]{2,1,0:T(8,128)(2,1)} async-done(((bf16[1,4096,2048]{2,1,0:T(8,128)(2,1)}), bf16[1,4096,2048]{2,1,0:T(8,128)(2,1)}) %all-reduce.35.cloned.1.call-update) | async-done | bytes 16777232 | tf_op jit(solution)/shard_map/psum | solution.py:85
  263.5 13.5 %convert_reduce_fusion = (f32[4096]{0:T(1024)S(1)}, bf16[1,4096,2048]{2,1,0:T(8,128)(2,1)S(1)}) fusion(bf16[1,4096,2048]{2,1,0:T(8,128)(2,1)} %all-reduce.35.cloned.1.call-done, bf16[1,4096,2048]{2,1,0:T(8,128)(2,1)} %param.9), kind=kLoop, calls=%fused_computation.4 | loop fusion | flops 50327552 | bytes 50348032 | tf_op jit(solution)/shard_map/jvp()/reduce_sum | solution.py:11
  277.0 6.6 fusion.19
  283.6 9.2 fusion.27
  292.9 8.5 convolution_convert_fusion
  302.7 8.5 fusion.59
  311.2 9.8 convert_bitcast_fusion.1
  325.9 10.9 %convert_bitcast_fusion.2 = bf16[1,4096,2048]{2,1,0:T(8,128)(2,1)} fusion(bf16[256,2048]{1,0:T(8,128)(2,1)S(1)} %copy-done.104, bf16[4096,256]{1,0:T(8,128)(2,1)} %copy-done.107), kind=kOutput, calls=%fused_computation.52 | convolution fusion | flops 4313841664 | bytes 19922944 | tf_op jit(solution)/shard_map/bsf,fh->bsh/dot_general | solution.py:90
  336.8 151.5 %all-reduce.37.cloned.1.call-done = bf16[1,4096,2048]{2,1,0:T(8,128)(2,1)} async-done(((bf16[1,4096,2048]{2,1,0:T(8,128)(2,1)}), bf16[1,4096,2048]{2,1,0:T(8,128)(2,1)}) %all-reduce.37.cloned.1.call-update) | async-done | bytes 16777232 | tf_op jit(solution)/shard_map/psum | solution.py:98
  488.3 15.5 %fusion.20 = f32[4096]{0:T(1024)S(1)} fusion(bf16[1,4096,2048]{2,1,0:T(8,128)(2,1)} %all-reduce.37.cloned.1.call-done, bf16[1,4096,2048]{2,1,0:T(8,128)(2,1)} %copy-done.3, f32[2048]{0:T(1024)S(1)} %convert_element_type.727, f32[4096]{0:T(1024)S(1)} %broadcast_multiply_fusion), kind=kLoop, calls=%fused_computation.32 | loop fusion | flops 50327552 | bytes 33595392 | tf_op jit(solution)/shard_map/transpose(jvp())/reduce_sum | solution.py:14
  503.9 19.9 %fusion.14 = (bf16[2048]{0:T(1024)(128)(2,1)}, f32[4096]{0:T(1024)S(1)}) fusion(bf16[1,4096,2048]{2,1,0:T(8,128)(2,1)S(1)} %copy-done.4, bf16[1,4096,2048]{2,1,0:T(8,128)(2,1)} %copy-done.3, f32[4096]{0:T(1024)S(1)} %fusion.282, f32[4096]{0:T(1024)S(1)} %broadcast_multiply_fusion, f32[4096]{0:T(1024)S(1)} %multiply_multiply_fusion.1, ...), kind=kLoop, calls=%fused_computation.26 | loop fusion | flops 100657152 | bytes 33632256 | tf_op jit(solution)/shard_map/transpose(jvp())/reduce_sum | solution.py:14
  523.8 26.9 %fusion.24 = bf16[1,4096,2048]{2,1,0:T(8,128)(2,1)} fusion(bf16[1,4096,2048]{2,1,0:T(8,128)(2,1)} %param.17, bf16[1,4096,2048]{2,1,0:T(8,128)(2,1)} %copy-done.3, bf16[1,4096,2048]{2,1,0:T(8,128)(2,1)} %all-reduce.37.cloned.1.call-done, f32[4096]{0:T(1024)S(1)} %negate_multiply_fusion.1, f32[4096]{0:T(1024)S(1)} %multiply_multiply_fusion.1, ...), kind=kLoop, calls=%fused_computation.38 | loop fusion | flops 92274688 | bytes 67182592 | tf_op jit(solution)/shard_map/add | solution.py:100
  550.7 11.0 %fusion.51 = bf16[1,4096,1,64]{1,3,2,0:T(8,128)(2,1)S(1)} fusion(bf16[1,4096,2048]{2,1,0:T(8,128)(2,1)} %fusion.24, bf16[1,64,2048]{2,1,0:T(8,128)(2,1)S(1)} %copy-done.69), kind=kOutput, calls=%fused_computation.85 | convolution fusion | flops 1074003968 | bytes 17563648 | tf_op jit(solution)/shard_map/bsh,ndh->bsnd/dot_general | solution.py:102
  589.5 2.3 multiply_reduce_fusion.5
  593.5 2.8 multiply_reduce_fusion.4
  597.9 2.5 multiply_reduce_fusion.3
  629.3 2.3 multiply_convert_fusion.7
  666.5 8.2 convert_bitcast_fusion
  676.3 9.7 convolution_convert_fusion.2
  686.0 9.7 fusion.91
  695.8 3.8 fusion.102
  699.6 8.6 convolution_convert_fusion.3
  708.2 216.5 %all-reduce.39.cloned.1.call-done = (bf16[1,4096,2048]{2,1,0:T(8,128)(2,1)}, bf16[1,4096,2048]{2,1,0:T(8,128)(2,1)}) async-done(((bf16[1,4096,2048]{2,1,0:T(8,128)(2,1)}, bf16[1,4096,2048]{2,1,0:T(8,128)(2,1)}), (bf16[1,4096,2048]{2,1,0:T(8,128)(2,1)}, bf16[1,4096,2048]{2,1,0:T(8,128)(2,1)})) %all-reduce.39.cloned.1.call-update) | async-done | bytes 33554448 | tf_op jit(solution)/shard_map/psum | solution.py:91
  924.8 15.0 %fusion.17 = f32[4096]{0:T(1024)S(1)} fusion(bf16[1,4096,2048]{2,1,0:T(8,128)(2,1)} %get-tuple-element.13, bf16[1,4096,2048]{2,1,0:T(8,128)(2,1)} %param.9, f32[2048]{0:T(1024)S(1)} %copy-done.83, f32[4096]{0:T(1024)S(1)} %copy-done.75), kind=kLoop, calls=%fused_computation.29 | loop fusion | flops 50327552 | bytes 33595392 | tf_op jit(solution)/shard_map/transpose(jvp())/reduce_sum | solution.py:14
  939.8 29.7 %fusion.15 = (bf16[2048]{0:T(1024)(128)(2,1)}, f32[4096]{0:T(1024)S(1)}, bf16[1,4096,2048]{2,1,0:T(8,128)(2,1)}) fusion(bf16[1,4096,2048]{2,1,0:T(8,128)(2,1)} %get-tuple-element.13, bf16[1,4096,2048]{2,1,0:T(8,128)(2,1)} %param.9, f32[4096]{0:T(1024)S(1)} %copy-done.79, f32[4096]{0:T(1024)S(1)} %copy-done.75, f32[4096]{0:T(1024)S(1)} %multiply_multiply_fusion, ...), kind=kLoop, calls=%fused_computation.27 | loop fusion | flops 134211584 | bytes 83963904 | tf_op jit(solution)/shard_map/transpose(jvp())/reduce_sum | solution.py:14
  969.5 26.8 %fusion.25 = bf16[1,4096,2048]{2,1,0:T(8,128)(2,1)} fusion(bf16[1,4096,2048]{2,1,0:T(8,128)(2,1)} %fusion.24, bf16[1,4096,2048]{2,1,0:T(8,128)(2,1)} %param.9, bf16[1,4096,2048]{2,1,0:T(8,128)(2,1)} %get-tuple-element.13, f32[4096]{0:T(1024)S(1)} %negate_multiply_fusion, f32[4096]{0:T(1024)S(1)} %multiply_multiply_fusion, f32[2048]{0:T(1024)S(1)} %copy-done.83, ...), kind=kLoop, calls=%fused_computation.39 | loop fusion | flops 92274688 | bytes 67182592 | tf_op jit(solution)/shard_map/add | solution.py:109
  (427 shorter events, 149.8 us)
Async XLA Ops:
  7.2 285.7 %copy-start = (bf16[2048,256]{1,0:T(8,128)(2,1)S(1)}, bf16[2048,256]{1,0:T(8,128)(2,1)}, u32[]{:S(2)}) copy-start(bf16[2048,256]{1,0:T(8,128)(2,1)} %param.15) | copy-start | bytes 3145732
  7.2 256.3 %all-reduce.35.cloned.1.call-start = ((), (), s32[]{:S(2)}) async-start(), calls=%async_computation | async-start | bytes 33554432 | tf_op jit(solution)/shard_map/psum | solution.py:85
  16.3 17.8 %copy-start.82 = (f32[2048]{0:T(1024)}, f32[2048]{0:T(1024)S(1)}, u32[]{:S(2)}) copy-start(f32[2048]{0:T(1024)S(1)} %convert_element_type.655) | copy-start | bytes 24580
  16.3 10.7 %copy-start.2 = (bf16[1,4096,2048]{2,1,0:T(8,128)(2,1)S(1)}, bf16[1,4096,2048]{2,1,0:T(8,128)(2,1)}, u32[]{:S(2)}) copy-start(bf16[1,4096,2048]{2,1,0:T(8,128)(2,1)} %param.9) | copy-start | bytes 50331652
  27.0 7.2 copy-start.74
  46.9 34.5 %copy-start.39 = (bf16[4096,192]{0,1:T(8,128)(2,1)}, bf16[4096,192]{0,1:T(8,128)(2,1)S(1)}, u32[]{:S(2)}) copy-start(bf16[4096,192]{0,1:T(8,128)(2,1)S(1)} %convolution_convert_fusion.1) | copy-start | bytes 4718596
  47.0 32.2 %copy-start.57 = (bf16[1,4096,1,64]{1,3,2,0:T(8,128)(2,1)}, bf16[1,4096,1,64]{1,3,2,0:T(8,128)(2,1)S(1)}, u32[]{:S(2)}) copy-start(bf16[1,4096,1,64]{1,3,2,0:T(8,128)(2,1)S(1)} %get-tuple-element.18) | copy-start | bytes 1572868
  93.0 395.3 %all-reduce.37.cloned.1.call-start = ((), (), s32[]{:S(2)}) async-start(), calls=%async_computation.1 | async-start | bytes 33554432 | tf_op jit(solution)/shard_map/psum | solution.py:98
  283.6 19.1 %slice-start.4 = ((s8[16777216]{0:T(1024)(128)(4,1)}), s8[4194304]{0:T(1024)(128)(4,1)S(1)}, s32[]{:S(2)}) async-start(s8[16777216]{0:T(1024)(128)(4,1)} %bitcast.850), calls=%async_computation.7 | async-start | bytes 8388608
  283.6 19.1 %slice-start.5 = ((s8[16777216]{0:T(1024)(128)(4,1)}), s8[4194304]{0:T(1024)(128)(4,1)S(1)}, s32[]{:S(2)}) async-start(s8[16777216]{0:T(1024)(128)(4,1)} %bitcast.850), calls=%async_computation.8 | async-start | bytes 8388608
  283.6 19.1 %slice-start.6 = ((s8[16777216]{0:T(1024)(128)(4,1)}), s8[4194304]{0:T(1024)(128)(4,1)S(1)}, s32[]{:S(2)}) async-start(s8[16777216]{0:T(1024)(128)(4,1)} %bitcast.850), calls=%async_computation.9 | async-start | bytes 8388608
  292.9 9.8 slice-start.7
  292.9 9.8 copy-start.103
  321.0 603.8 %all-reduce.39.cloned.1.call-start = ((), (), s32[]{:S(2)}) async-start(), calls=%async_computation.2 | async-start | bytes 67108864 | tf_op jit(solution)/shard_map/psum | solution.py:91
  321.1 245.1 %copy-start.89 = (f32[256]{0:T(256)}, f32[256]{0:T(256)S(1)}, u32[]{:S(2)}) copy-start(f32[256]{0:T(256)S(1)} %log_add_fusion.14) | copy-start | bytes 3076
  321.1 247.1 %copy-start.93 = (f32[256]{0:T(256)}, f32[256]{0:T(256)S(1)}, u32[]{:S(2)}) copy-start(f32[256]{0:T(256)S(1)} %log_add_fusion.13) | copy-start | bytes 3076
  321.1 251.8 %copy-start.91 = (f32[256]{0:T(256)}, f32[256]{0:T(256)S(1)}, u32[]{:S(2)}) copy-start(f32[256]{0:T(256)S(1)} %log_add_fusion.11) | copy-start | bytes 3076
  488.3 15.5 %copy-start.4 = (bf16[1,4096,2048]{2,1,0:T(8,128)(2,1)S(1)}, bf16[1,4096,2048]{2,1,0:T(8,128)(2,1)}, u32[]{:S(2)}) copy-start(bf16[1,4096,2048]{2,1,0:T(8,128)(2,1)} %all-reduce.37.cloned.1.call-done) | copy-start | bytes 50331652
  550.7 11.0 %copy-start.43 = (f32[256,256]{0,1:T(8,128)S(1)}, f32[256,256]{0,1:T(8,128)}, u32[]{:S(2)}) copy-start(f32[256,256]{0,1:T(8,128)} %copy-done.42) | copy-start | bytes 786436
  550.7 14.5 %copy-start.38 = (f32[256,512]{1,0:T(8,128)S(1)}, f32[256,512]{1,0:T(8,128)}, u32[]{:S(2)}) copy-start(f32[256,512]{1,0:T(8,128)} %copy-done.37) | copy-start | bytes 1572868
  666.5 8.2 copy-start.64
  676.3 9.7 copy-start.108
  676.3 19.4 %slice-start = ((s8[16777216]{0:T(1024)(128)(4,1)}), s8[4194304]{0:T(1024)(128)(4,1)S(1)}, s32[]{:S(2)}) async-start(s8[16777216]{0:T(1024)(128)(4,1)} %bitcast.848), calls=%async_computation.3 | async-start | bytes 8388608
  676.3 19.4 %slice-start.1 = ((s8[16777216]{0:T(1024)(128)(4,1)}), s8[4194304]{0:T(1024)(128)(4,1)S(1)}, s32[]{:S(2)}) async-start(s8[16777216]{0:T(1024)(128)(4,1)} %bitcast.848), calls=%async_computation.4 | async-start | bytes 8388608
  676.3 19.4 %slice-start.2 = ((s8[16777216]{0:T(1024)(128)(4,1)}), s8[4194304]{0:T(1024)(128)(4,1)S(1)}, s32[]{:S(2)}) async-start(s8[16777216]{0:T(1024)(128)(4,1)} %bitcast.848), calls=%async_computation.5 | async-start | bytes 8388608
  686.0 9.7 slice-start.3
  686.0 9.7 copy-start.45
  699.6 225.1 %copy-start.75 = (f32[4096]{0:T(1024)S(1)}, f32[4096]{0:T(1024)}, u32[]{:S(2)}) copy-start(f32[4096]{0:T(1024)} %copy-done.74) | copy-start | bytes 49156
  699.6 225.1 %copy-start.83 = (f32[2048]{0:T(1024)S(1)}, f32[2048]{0:T(1024)}, u32[]{:S(2)}) copy-start(f32[2048]{0:T(1024)} %copy-done.82) | copy-start | bytes 24580
  924.8 15.0 %copy-start.85 = (f32[4096]{0:T(1024)S(1)}, f32[4096]{0:T(1024)}, u32[]{:S(2)}) copy-start(f32[4096]{0:T(1024)} %copy-done.84) | copy-start | bytes 49156
  924.8 15.0 %copy-start.79 = (f32[4096]{0:T(1024)S(1)}, f32[4096]{0:T(1024)}, u32[]{:S(2)}) copy-start(f32[4096]{0:T(1024)} %copy-done.78) | copy-start | bytes 49156
  969.5 26.8 %copy-start.1 = (bf16[2048,256]{1,0:T(8,128)(2,1)S(1)}, bf16[2048,256]{1,0:T(8,128)(2,1)}, u32[]{:S(2)}) copy-start(bf16[2048,256]{1,0:T(8,128)(2,1)} %param.15) | copy-start | bytes 3145732
  (92 other events, 230.5 us)
Sparse Core Ops, SparseCore 0:
  93.1 170.3 all-reduce.34
  321.1 167.1 all-reduce.36
  674.9 249.7 all-reduce.38
where the time goes:
time: 1010 us; the launch traced here: 1000 us
  waiting for transfers between devices  538 us (53%)
  other arithmetic  217 us (21%)
  matrix products  206 us (20%)
  local copies, waits for them, and re-layouts  27.3 us (3%)
  between operations  15.4 us (2%)
    psum x1, waiting for transfers between devices, local_step(): sum_two = lax.psum(part_two, 'model')  217 us
    psum x1, waiting for transfers between devices, local_step(): sum_one = lax.psum(part_one, 'model')  170 us
    psum x1, waiting for transfers between devices, local_step(): d_norm_two = lax.psum(d_norm_part, 'model')  151 us
    reduce_sum x4, other arithmetic, layer_norm(): centered * lax.rsqrt(row_var + LN_EPS) * gain.astype(jnp.float32)  80.1 us
    add x1, other arithmetic, local_step(): d_resid = d_y + d_resid_ln  26.9 us
    add x1, other arithmetic, local_step(): d_x = d_resid + d_x_ln  26.8 us
    dot_general x16, matrix products, attention_backward(): jnp.einsum('bqnd,bknd->bnqk', d_out_blk, v_all[:, :stop], preferred_eleme...  22.4 us
    reduce_sum x2, other arithmetic, layer_norm(): row_mean = jnp.mean(x_wide, axis=-1, keepdims=True)  20.5 us
  transfers between devices with their start and end apart: 3, of which 3 were waited for; matrix products, arithmetic and copies ran while one was open for 5% of the time, Pallas kernels for 0%

commit v1 on v0

v1 whole, which is shorter than its diff:
```python
import functools

import jax
import jax.numpy as jnp
from jax import lax
from jax.experimental import pallas as pl
from jax.experimental.pallas import tpu as pltpu
from jax.sharding import PartitionSpec as P

LN_EPS = 1e-5
LOG2E = 1.4426950408889634
NEG = -1e30
MESH = pl.DeviceIdType.MESH
VMEM_LIMIT = 60 * 1024 * 1024
F32 = jnp.float32
BF16 = jnp.bfloat16


def mm(a, b, ca, cb):
    return lax.dot_general(a, b, (((ca,), (cb,)), ((), ())), preferred_element_type=F32)


def ln_qkv_kernel(x_ref, g_ref, w_ref, a_ref, q_ref, k_ref, v_ref, t_ref):
    x = x_ref[...].astype(F32)
    mean = jnp.mean(x, axis=-1, keepdims=True)
    cen = x - mean
    var = jnp.mean(cen * cen, axis=-1, keepdims=True)
    a = (cen * lax.rsqrt(var + LN_EPS) * g_ref[...].astype(F32)).astype(BF16)
    a_ref[...] = a
    qkv = mm(a, w_ref[...], 1, 1)
    t_ref[...] = qkv.T.astype(BF16)
    hd = q_ref.shape[1]
    qkv = qkv.astype(BF16)
    q_ref[...] = qkv[:, :hd]
    k_ref[...] = qkv[:, hd:2 * hd]
    v_ref[...] = qkv[:, 2 * hd:]


def ln_qkv(x, g, w):
    t, h = x.shape
    c = w.shape[0]
    hd = c // 3
    bt = min(512, t)
    row = lambda n: pl.BlockSpec((bt, n), lambda i: (i, 0))
    return pl.pallas_call(
        ln_qkv_kernel,
        grid=(t // bt,),
        in_specs=[row(h), pl.BlockSpec((1, h), lambda i: (0, 0)), pl.BlockSpec((c, h), lambda i: (0, 0))],
        out_specs=[row(h), row(hd), row(hd), row(hd), pl.BlockSpec((c, bt), lambda i: (0, i))],
        out_shape=[jax.ShapeDtypeStruct((t, h), BF16)] + [jax.ShapeDtypeStruct((t, hd), BF16)] * 3 + [jax.ShapeDtypeStruct((c, t), BF16)],
        compiler_params=pltpu.CompilerParams(vmem_limit_bytes=VMEM_LIMIT),
        cost_estimate=pl.CostEstimate(flops=2 * t * h * c + 20 * t * h, bytes_accessed=4 * t * h, transcendentals=0),
        name='ln_qkv',
    )(x, g.reshape(1, h), w)


def visible(kb, bk, q0, bq, start):
    k_pos = kb * bk + lax.broadcasted_iota(jnp.int32, (bk, bq), 0)
    q_pos = q0 + lax.broadcasted_iota(jnp.int32, (bk, bq), 1)
    return (k_pos <= q_pos) & (k_pos >= start)


def attn_fwd_kernel(bk, tab_ref, k_ref, qt_ref, vt_ref, start_ref, ot_ref, lse_ref):
    i = pl.program_id(0)
    bq = qt_ref.shape[1]
    hd = qt_ref.shape[0]
    scale = LOG2E * hd ** -0.5
    qt = qt_ref[...]
    start = start_ref[...]
    lo, mid, hi, top = tab_ref[0, i], tab_ref[1, i], tab_ref[2, i], tab_ref[3, i]

    def step(masked, kb, carry):
        m, l, acc = carry
        k0 = pl.multiple_of(kb * bk, bk)
        s = mm(k_ref[pl.ds(k0, bk), :], qt, 1, 0)
        if masked:
            s = jnp.where(visible(kb, bk, i * bq, bq, start), s, NEG)
        m_new = jnp.maximum(m, jnp.max(s, axis=0, keepdims=True))
        p = jnp.exp2((s - m_new) * scale)
        alpha = jnp.exp2((m - m_new) * scale)
        l = l * alpha + jnp.sum(p, axis=0, keepdims=True)
        acc = acc * alpha + mm(vt_ref[:, pl.ds(k0, bk)], p.astype(BF16), 1, 0)
        return m_new, l, acc

    carry = (jnp.full((1, bq), NEG, F32), jnp.zeros((1, bq), F32), jnp.zeros((hd, bq), F32))
    carry = lax.fori_loop(lo, mid, functools.partial(step, True), carry)
    carry = lax.fori_loop(mid, hi, functools.partial(step, False), carry)
    m, l, acc = lax.fori_loop(hi, top, functools.partial(step, True), carry)
    ot_ref[...] = (acc / l).astype(BF16)
    lse_ref[...] = m * scale + jnp.log2(l)


def document_starts(seg):
    t = seg.shape[0]
    wide = 128
    pos = jnp.arange(t, dtype=jnp.int32).reshape(t // wide, wide)
    before = jnp.concatenate([seg[:1], seg[:-1]])
    mark = jnp.where((seg != before).reshape(pos.shape), pos, 0)
    lane = jnp.arange(wide)
    inner = jnp.max(jnp.where(lane[None, :, None] >= lane[None, None, :], mark[:, None, :], 0), axis=-1)
    row = jnp.arange(t // wide)
    prior = jnp.max(jnp.where(row[:, None] > row[None, :], inner[:, -1][None, :], 0), axis=-1)
    return jnp.maximum(inner, prior[:, None]).reshape(t)


def block_table(seg, start, bq, bk):
    t = seg.shape[0]
    nq = t // bq
    q0 = jnp.arange(nq, dtype=jnp.int32) * bq
    first = start.reshape(nq, bq)[:, 0]
    last = start.reshape(nq, bq)[:, -1]
    lo = first // bk
    hi = q0 // bk
    top = (q0 + bq + bk - 1) // bk
    mid = jnp.clip((last + bk - 1) // bk, lo, hi)
    return jnp.stack([lo, mid, hi, top])


def attention_forward(k, qkvt, start, tab, bq, bk):
    t, hd = k.shape
    return pl.pallas_call(
        functools.partial(attn_fwd_kernel, bk),
        grid_spec=pltpu.PrefetchScalarGridSpec(
            num_scalar_prefetch=1,
            grid=(t // bq,),
            in_specs=[
                pl.BlockSpec((t, hd), lambda i, *_: (0, 0)),
                pl.BlockSpec((hd, bq), lambda i, *_: (0, i)),
                pl.BlockSpec((hd, t), lambda i, *_: (2, 0)),
                pl.BlockSpec((1, bq), lambda i, *_: (0, i)),
            ],
            out_specs=[pl.BlockSpec((hd, bq), lambda i, *_: (0, i)), pl.BlockSpec((1, bq), lambda i, *_: (0, i))],
        ),
        out_shape=[jax.ShapeDtypeStruct((hd, t), BF16), jax.ShapeDtypeStruct((1, t), F32)],
        compiler_params=pltpu.CompilerParams(vmem_limit_bytes=VMEM_LIMIT),
        cost_estimate=pl.CostEstimate(flops=16 * t * t * hd, bytes_accessed=8 * t * hd, transcendentals=t * t // 2),
        name='attn_fwd',
    )(tab, k, qkvt, qkvt, start)


def attn_bwd_kernel(bk, tab_ref, q_ref, k_ref, v_ref, t_ref, ot_ref, dot_ref, lse_ref, start_ref, d_ref, dk_acc, dv_acc):
    i = pl.program_id(0)
    bq, hd = q_ref.shape
    scale = LOG2E * hd ** -0.5
    t = k_ref.shape[0]

    @pl.when(i == 0)
    def _():
        dk_acc[...] = jnp.zeros_like(dk_acc)
        dv_acc[...] = jnp.zeros_like(dv_acc)

    c0 = pl.multiple_of(i * bq, bq)
    q = q_ref[...]
    qt = t_ref[:hd, pl.ds(c0, bq)]
    dot_blk = dot_ref[...]
    dot_wide = dot_blk.astype(F32)
    d_out = dot_wide.T.astype(BF16)
    delta = jnp.sum(dot_wide * ot_ref[...].astype(F32), axis=0, keepdims=True)
    lse = lse_ref[...]
    start = start_ref[...]
    lo, mid, hi, top = tab_ref[0, i], tab_ref[1, i], tab_ref[2, i], tab_ref[3, i]

    def step(masked, kb, dqt):
        k0 = pl.multiple_of(kb * bk, bk)
        rows = pl.ds(k0, bk)
        s = mm(k_ref[rows, :], qt, 1, 0)
        p = jnp.exp2(s * scale - lse)
        if masked:
            p = jnp.where(visible(kb, bk, i * bq, bq, start), p, 0.0)
        dp = mm(v_ref[rows, :], dot_blk, 1, 0)
        ds = (p * (dp - delta)).astype(BF16)
        dv_acc[rows, :] += mm(p.astype(BF16), d_out, 1, 0)
        dk_acc[rows, :] += mm(ds, q, 1, 0)
        return dqt + mm(t_ref[hd:2 * hd, rows], ds, 1, 0)

    dqt = jnp.zeros((hd, bq), F32)
    dqt = lax.fori_loop(lo, mid, functools.partial(step, True), dqt)
    dqt = lax.fori_loop(mid, hi, functools.partial(step, False), dqt)
    dqt = lax.fori_loop(hi, top, functools.partial(step, True), dqt)
    d_ref[pl.ds(c0, bq), :hd] = (dqt * hd ** -0.5).T.astype(BF16)

    @pl.when(i == pl.num_programs(0) - 1)
    def _():
        def put(r, _):
            rows = pl.ds(pl.multiple_of(r * bk, bk), bk)
            d_ref[rows, hd:2 * hd] = (dk_acc[rows, :] * hd ** -0.5).astype(BF16)
            d_ref[rows, 2 * hd:] = dv_acc[rows, :].astype(BF16)
            return 0

        lax.fori_loop(0, t // bk, put, 0)


def attention_backward(q, k, v, qkvt, ot, dot, lse, start, tab, bq, bk):
    t, hd = k.shape
    whole = lambda shape: pl.BlockSpec(shape, lambda i, *_: (0, 0))
    cols = lambda n: pl.BlockSpec((n, bq), lambda i, *_: (0, i))
    return pl.pallas_call(
        functools.partial(attn_bwd_kernel, bk),
        grid_spec=pltpu.PrefetchScalarGridSpec(
            num_scalar_prefetch=1,
            grid=(t // bq,),
            in_specs=[
                pl.BlockSpec((bq, hd), lambda i, *_: (i, 0)), whole((t, hd)), whole((t, hd)), whole((3 * hd, t)),
                cols(hd), cols(hd), cols(1), cols(1),
            ],
            out_specs=whole((t, 3 * hd)),
            scratch_shapes=[pltpu.VMEM((t, hd), F32), pltpu.VMEM((t, hd), F32)],
        ),
        out_shape=jax.ShapeDtypeStruct((t, 3 * hd), BF16),
        compiler_params=pltpu.CompilerParams(vmem_limit_bytes=VMEM_LIMIT),
        cost_estimate=pl.CostEstimate(flops=40 * t * t * hd, bytes_accessed=16 * t * hd, transcendentals=t * t // 2),
        name='attn_bwd',
    )(tab, q, k, v, qkvt, ot, dot, lse, start)


def exchange_kernel(n, src_of, dst_of, in_ref, out_ref, send_sem, recv_sem, own_sem):
    me = lax.axis_index('model')
    barrier = pltpu.get_barrier_semaphore()

    def hello(off, _):
        pl.semaphore_signal(barrier, inc=1, device_id={'model': lax.rem(me + off, n)}, device_id_type=MESH)
        return 0

    lax.fori_loop(1, n, hello, 0)
    own = pltpu.make_async_copy(src_of(in_ref, me), dst_of(out_ref, me), own_sem)
    own.start()
    pl.semaphore_wait(barrier, n - 1)

    def send(off, _):
        to = lax.rem(me + off, n)
        pltpu.make_async_remote_copy(
            src_ref=src_of(in_ref, to), dst_ref=dst_of(out_ref, me), send_sem=send_sem.at[off], recv_sem=recv_sem.at[off],
            device_id={'model': to}, device_id_type=MESH,
        ).start()
        return 0

    lax.fori_loop(1, n, send, 0)

    def finish(off, _):
        to = lax.rem(me + off, n)
        come = lax.rem(me - off + n, n)
        pltpu.make_async_remote_copy(
            src_ref=src_of(in_ref, to), dst_ref=dst_of(out_ref, come), send_sem=send_sem.at[off], recv_sem=recv_sem.at[off],
            device_id={'model': to}, device_id_type=MESH,
        ).wait()
        return 0

    lax.fori_loop(1, n, finish, 0)
    own.wait()


def exchange(n, value, out_shape, src_of, dst_of, collective_id, name):
    return pl.pallas_call(
        functools.partial(exchange_kernel, n, src_of, dst_of),
        out_shape=jax.ShapeDtypeStruct(out_shape, value.dtype),
        in_specs=[pl.BlockSpec(memory_space=pltpu.VMEM)],
        out_specs=pl.BlockSpec(memory_space=pltpu.VMEM),
        scratch_shapes=[pltpu.SemaphoreType.DMA((n,)), pltpu.SemaphoreType.DMA((n,)), pltpu.SemaphoreType.DMA],
        compiler_params=pltpu.CompilerParams(collective_id=collective_id, has_side_effects=True),
        cost_estimate=pl.CostEstimate(flops=2_000_000_000, bytes_accessed=2 * value.size * 2, transcendentals=0),
        name=name,
    )(value)


def column_block(width):
    return lambda ref, j: ref.at[:, pl.ds(pl.multiple_of(j * width, width), width)]


def leading(ref, j):
    return ref.at[j]


def whole_ref(ref, j):
    return ref


def ln_rows(z, gain):
    wide = z.astype(F32)
    mean = jnp.mean(wide, axis=-1, keepdims=True)
    cen = wide - mean
    rstd = lax.rsqrt(jnp.mean(cen * cen, axis=-1, keepdims=True) + LN_EPS)
    hat = cen * rstd
    return (hat * gain.astype(F32)).astype(BF16), hat, rstd


def ln_back(d_out, hat, rstd, gain):
    d_wide = d_out.astype(F32)
    d_hat = d_wide * gain.astype(F32)
    mean_a = jnp.mean(d_hat, axis=-1, keepdims=True)
    mean_b = jnp.mean(d_hat * hat, axis=-1, keepdims=True)
    return (rstd * (d_hat - mean_a - hat * mean_b)).astype(BF16), jnp.sum(d_wide * hat, axis=0)


def gelu_tanh(up_proj):
    return jax.nn.gelu(up_proj.astype(F32), approximate=True).astype(BF16)


def solution(mesh):
    n = mesh.shape['model']

    def local_step(x_in, seg_ids, gain_one, w_qkv, w_out, gain_two, w_up, w_down, d_y):
        x = x_in[0]
        dy = d_y[0]
        seg = seg_ids[0]
        t, h = x.shape
        n_local, hd = w_out.shape[:2]
        inner = n * n_local * hd
        ts = t // n
        bq = min(512, t)
        bk = min(512, t)
        me = lax.axis_index('model')

        wo_full = lax.all_gather(w_out, 'model', axis=0, tiled=True).reshape(inner, h)

        start = document_starts(seg)
        tab = block_table(seg, start, bq, bk)
        start_row = start.reshape(1, t)

        a_full, q, k, v, qkvt = ln_qkv(x, gain_one, w_qkv.T)
        ot, lse = attention_forward(k, qkvt, start_row, tab, bq, bk)
        o_mine = exchange(n, ot, (n, hd, ts), column_block(ts), leading, 0, 'heads_to_tokens')

        x_s = lax.dynamic_slice(x, (me * ts, 0), (ts, h))
        dy_s = lax.dynamic_slice(dy, (me * ts, 0), (ts, h))
        proj = mm(o_mine.reshape(inner, ts), wo_full, 0, 0)
        resid = (x_s.astype(F32) + proj).astype(BF16)
        b1_s, hat_two, rstd_two = ln_rows(resid, gain_two)
        b1 = lax.all_gather(b1_s, 'model', axis=0, tiled=True)

        d_gelu = mm(dy, w_down, 1, 1).astype(BF16)
        up = mm(b1, w_up, 1, 0).astype(BF16)
        gelu_out, gelu_pull = jax.vjp(gelu_tanh, up)
        (d_up,) = gelu_pull(d_gelu)
        d_b1 = mm(d_up, w_up, 1, 1).astype(BF16)
        late_gelu, d_b1 = lax.optimization_barrier((gelu_out, d_b1))
        d_b1 = lax.psum_scatter(d_b1, 'model', scatter_dimension=0, tiled=True)
        part_two = mm(late_gelu, w_down, 1, 0).astype(BF16)
        late_gelu, late_up, part_two = lax.optimization_barrier((late_gelu, d_up, part_two))
        part_two = lax.psum_scatter(part_two, 'model', scatter_dimension=0, tiled=True)
        d_w_down = mm(late_gelu, dy, 0, 0).astype(BF16)
        d_w_up = mm(b1, late_up, 0, 0).astype(BF16)

        d_ln, d_gain_two = ln_back(d_b1, hat_two, rstd_two, gain_two)
        d_resid_s = dy_s + d_ln
        d_heads = mm(wo_full, d_resid_s, 1, 1).astype(BF16).reshape(n, hd, ts)
        dot = exchange(n, d_heads, (hd, t), leading, column_block(ts), 1, 'tokens_to_heads')
        d_resid = lax.all_gather(d_resid_s, 'model', axis=0, tiled=True)

        d_qkv = attention_backward(q, k, v, qkvt, ot, dot, lse, start_row, tab, bq, bk)
        part_two, _ = lax.optimization_barrier((part_two, d_qkv))
        y_s = (resid.astype(F32) + part_two.astype(F32)).astype(BF16)
        y_out = lax.all_gather(y_s[None], 'model', axis=1, tiled=True)
        d_norm = lax.psum_scatter(mm(d_qkv, w_qkv, 1, 1).astype(BF16), 'model', scatter_dimension=0, tiled=True)
        d_w_qkv = mm(a_full, d_qkv, 0, 0).astype(BF16)
        d_w_out = mm(ot, d_resid, 1, 0).astype(BF16)

        _, hat_one, rstd_one = ln_rows(x_s, gain_one)
        d_ln, d_gain_one = ln_back(d_norm, hat_one, rstd_one, gain_one)
        d_x = lax.all_gather((d_resid_s + d_ln)[None], 'model', axis=1, tiled=True)
        gains = jnp.concatenate([d_gain_one, d_gain_two]).reshape(1, 2 * h)
        gains = exchange(n, gains, (n, 1, 2 * h), whole_ref, leading, 2, 'gain_sums')
        gains = jnp.sum(gains, axis=(0, 1)).astype(BF16)
        return (y_out, d_x, d_w_qkv, d_w_out.reshape(n_local, hd, h), d_w_up, d_w_down, gains[:h], gains[h:])

    in_specs = (P('data'), P('data'), P(), P(None, 'model'), P('model'), P(), P(None, 'model'), P('model'), P('data'))
    out_specs = (P('data'), P('data'), P('data', 'model'), P(('data', 'model')), P('data', 'model'), P(('data', 'model')), P('data'), P('data'))
    return jax.shard_map(local_step, mesh=mesh, in_specs=in_specs, out_specs=out_specs, check_vma=False)
```

time: 1010 us -> 759 us (0.75)
  other arithmetic: 217 us -> 19.7 us
  Pallas kernels: 0 us -> 116 us
  matrix products: 206 us -> 101 us
  waiting for transfers between devices: 538 us -> 472 us
    psum x3 -> x0, waiting for transfers between devices: 538 us -> none  [the longest x1 217 us: local_step(): sum_two = lax.psum(part_two, 'model')]
    reduce_scatter x0 -> x3, waiting for transfers between devices: none -> 251 us  [the longest x1 105 us: local_step(): lax.psum_scatter(mm(d_qkv, w_qkv, 1, 1).astype(BF16), 'model', scatter_di...]
    all_gather x0 -> x5, waiting for transfers between devices: none -> 219 us  [the longest x1 69 us: local_step(): d_resid = lax.all_gather(d_resid_s, 'model', axis=0, tiled=True)]
    pallas_call x0 -> x6, Pallas kernels: none -> 116 us  [the longest x3 58.4 us: exchange(): pl.pallas_call(functools.partial(exchange_kernel, n, src_of, dst_of), out...]
    reduce_sum x24 -> x6, other arithmetic: 121 us -> 7.36 us  [the longest x2 3.17 us: ln_back(): jnp.sum(d_wide * hat, axis=0)]
    dot_general x108 -> x11, matrix products: 206 us -> 101 us  [mm(): lax.dot_general(a, b, (((ca,), (cb,)), ((), ())), preferred_element_type=...]
    add x33 -> x2, other arithmetic: 58.6 us -> 4.26 us  [the longest x1 2.54 us: local_step(): d_x = lax.all_gather((d_resid_s + d_ln)[None], 'model', axis=1, tiled=True)]
    another operation x3 -> x1, other arithmetic: 17.7 us -> 0.59 us  [block_table(): return jnp.stack([lo, mid, hi, top])]
  transfers between devices with their start and end apart: 3 -> 8, of which waited for: 3 -> 7; matrix products, arithmetic and copies ran while one was open for 5% -> 11% of each run, Pallas kernels for 0% -> 15%
where the time goes in v1:
time: 759 us; the launch traced here: 753 us
  waiting for transfers between devices  472 us (62%)
  Pallas kernels  116 us (15%)
  matrix products  101 us (13%)
  local copies, waits for them, and re-layouts  27.5 us (4%)
  other arithmetic  19.7 us (3%)
  between operations  14.7 us (2%)
    reduce_scatter x1, waiting for transfers between devices, local_step(): lax.psum_scatter(mm(d_qkv, w_qkv, 1, 1).astype(BF16), 'model', scatter_di...  105 us
    dot_general x11, matrix products, mm(): lax.dot_general(a, b, (((ca,), (cb,)), ((), ())), preferred_element_type=...  101 us
    reduce_scatter x1, waiting for transfers between devices, local_step(): d_b1 = lax.psum_scatter(d_b1, 'model', scatter_dimension=0, tiled=True)  94.7 us
    all_gather x1, waiting for transfers between devices, local_step(): d_resid = lax.all_gather(d_resid_s, 'model', axis=0, tiled=True)  69 us
    all_gather x1, waiting for transfers between devices, local_step(): b1 = lax.all_gather(b1_s, 'model', axis=0, tiled=True)  67.4 us
    all_gather x1, waiting for transfers between devices, local_step(): d_x = lax.all_gather((d_resid_s + d_ln)[None], 'model', axis=1, tiled=True)  59.3 us
    pallas_call x3, Pallas kernels, exchange(): pl.pallas_call(functools.partial(exchange_kernel, n, src_of, dst_of), out...  58.4 us
    reduce_scatter x1, waiting for transfers between devices, local_step(): lax.psum_scatter(part_two, 'model', scatter_dimension=0, tiled=True)  51.2 us
  transfers between devices with their start and end apart: 8, of which 7 were waited for; matrix products, arithmetic and copies ran while one was open for 11% of the time, Pallas kernels for 15%

profile of v1, /device:TPU:97, one launch (start us, length us, event | category | flops | bytes accessed | tf_op | source)
XLA Modules:
  0.0 752.7 jit_solution(4646963937497347624)
XLA Ops:
  11.2 1.5 add_select_fusion
  15.4 20.6 %ln_qkv.1 = (bf16[4096,2048]{1,0:T(8,128)(2,1)}, bf16[4096,64]{1,0:T(8,128)(2,1)}, bf16[4096,64]{1,0:T(8,128)(2,1)}, bf16[4096,64]{1,0:T(8,128)(2,1)}, bf16[192,4096]{1,0:T(8,128)(2,1)}) custom-call(bf16[4096,2048]{1,0:T(8,128)(2,1)} %bitcast.116, bf16[1,2048]{1,0:T(2,128)(2,1)} %reshape.399.g_ref, bf16[192,2048]{1,0:T(8,128)(2,1)} %bitcast.119), custom_call_target="tpu_custom_call" | custom-call | flops 3388997632 | bytes 33554432 | tf_op jit(solution)/shard_map/ln_qkv/pallas_call | solution.py:45
  36.0 15.0 %attn_fwd.1 = (bf16[64,4096]{1,0:T(8,128)(2,1)}, f32[1,4096]{1,0:T(1,128)}) custom-call(s32[4,8]{1,0:T(4,128)} %pad_add_fusion.tab_ref, bf16[4096,64]{1,0:T(8,128)(2,1)} %get-tuple-element.21.k_ref, bf16[192,4096]{1,0:T(8,128)(2,1)} %get-tuple-element.22.qt_ref.vt_ref.t_ref, bf16[192,4096]{1,0:T(8,128)(2,1)} %get-tuple-element.22.qt_ref.vt_ref.t_ref, ...), custom_call_target="tpu_custom_call" | custom-call | flops 17179869184 | bytes 2097152 | tf_op jit(solution)/shard_map/attn_fwd/pallas_call | solution.py:121
  51.1 19.1 %heads_to_tokens.1 = bf16[32,64,128]{2,1,0:T(8,128)(2,1)} custom-call(bf16[64,4096]{1,0:T(8,128)(2,1)} %get-tuple-element.23.in_ref.ot_ref), custom_call_target="tpu_custom_call" | custom-call | flops 2000000000 | bytes 1048576 | tf_op jit(solution)/shard_map/heads_to_tokens/pallas_call | solution.py:253
  70.2 4.9 fusion.54
  77.1 67.4 %all-gather.10.cloned.1.call-done = bf16[4096,2048]{1,0:T(8,128)(2,1)} async-done(((bf16[128,2048]{1,0:T(8,128)(2,1)}), bf16[4096,2048]{1,0:T(8,128)(2,1)}) %all-gather.10.cloned.1.call-update) | async-done | bytes 16777232 | tf_op jit(solution)/shard_map/all_gather | solution.py:328
  144.5 12.7 %fusion.15 = (bf16[4096,256]{1,0:T(8,128)(2,1)}, bf16[4096,256]{1,0:T(8,128)(2,1)S(1)}) fusion(bf16[4096,2048]{1,0:T(8,128)(2,1)} %all-gather.10.cloned.1.call-done, bf16[2048,256]{1,0:T(8,128)(2,1)S(1)} %copy-done), kind=kOutput, calls=%fused_computation.23 | convolution fusion | flops 4306501632 | bytes 22020096 | tf_op jit(solution)/shard_map/dot_general | solution.py:20
  157.2 14.5 %fusion.10 = bf16[4096,256]{1,0:T(8,128)(2,1)} fusion(bf16[4096,256]{1,0:T(8,128)(2,1)S(1)} %get-tuple-element.49, bf16[256,2048]{1,0:T(8,128)(2,1)S(1)} %copy-done.10, bf16[1,4096,2048]{2,1,0:T(8,128)(2,1)} %param.17), kind=kOutput, calls=%fused_computation.18 | convolution fusion | flops 4319084544 | bytes 22020096 | tf_op jit(solution)/shard_map/dot_general | solution.py:20
  171.7 9.8 %convolution_convert_fusion.2 = bf16[4096,2048]{1,0:T(8,128)(2,1)} fusion(bf16[4096,256]{1,0:T(8,128)(2,1)} %fusion.10, bf16[2048,256]{1,0:T(8,128)(2,1)S(1)} %copy-done), kind=kOutput, calls=%fused_computation.6 | convolution fusion | flops 4303355904 | bytes 19922944 | tf_op jit(solution)/shard_map/dot_general | solution.py:20
  181.6 10.1 %convolution_convert_fusion.1 = bf16[4096,2048]{1,0:T(8,128)(2,1)} fusion(bf16[4096,256]{1,0:T(8,128)(2,1)} %get-tuple-element.33, bf16[256,2048]{1,0:T(8,128)(2,1)S(1)} %copy-done.10), kind=kOutput, calls=%fused_computation.5 | convolution fusion | flops 4303355904 | bytes 19922944 | tf_op jit(solution)/shard_map/dot_general | solution.py:20
  191.8 94.7 %reduce-scatter.6.cloned.1.call-done = bf16[128,2048]{1,0:T(8,128)(2,1)} async-done(((bf16[4096,2048]{1,0:T(8,128)(2,1)}), bf16[128,2048]{1,0:T(8,128)(2,1)}) %reduce-scatter.6.cloned.1.call-update) | async-done | bytes 524304 | tf_op jit(solution)/shard_map/reduce_scatter | solution.py:336
  288.1 1.7 fusion.49
  289.8 6.4 fusion.26
  297.3 17.0 %tokens_to_heads.1.dot_ref = bf16[64,4096]{1,0:T(8,128)(2,1)} custom-call(bf16[32,64,128]{2,1,0:T(8,128)(2,1)} %bitcast.120), custom_call_target="tpu_custom_call" | custom-call | flops 2000000000 | bytes 1048576 | tf_op jit(solution)/shard_map/tokens_to_heads/pallas_call | solution.py:253
  314.3 22.2 %attn_bwd.1 = bf16[4096,192]{1,0:T(8,128)(2,1)} custom-call(s32[4,8]{1,0:T(4,128)} %pad_add_fusion.tab_ref, bf16[4096,64]{1,0:T(8,128)(2,1)} %get-tuple-element.26.q_ref, bf16[4096,64]{1,0:T(8,128)(2,1)} %get-tuple-element.21.k_ref, bf16[4096,64]{1,0:T(8,128)(2,1)} %get-tuple-element.27.v_ref, bf16[192,4096]{1,0:T(8,128)(2,1)} %get-tuple-element.22.qt_ref.vt_ref.t_ref, ...), custom_call_target="tpu_custom_call" | custom-call | flops 42949672960 | bytes 4194304 | tf_op jit(solution)/shard_map/attn_bwd/pallas_call | solution.py:197
  336.5 9.7 %convolution_convert_fusion = bf16[4096,2048]{1,0:T(8,128)(2,1)} fusion(bf16[4096,192]{1,0:T(8,128)(2,1)} %attn_bwd.1, bf16[2048,192]{0,1:T(8,128)(2,1)S(1)} %copy-done.7), kind=kOutput, calls=%fused_computation.4 | convolution fusion | flops 3229614080 | bytes 19136512 | tf_op jit(solution)/shard_map/dot_general | solution.py:20
  346.4 51.2 %reduce-scatter.4.cloned.1.call-done = bf16[128,2048]{1,0:T(8,128)(2,1)} async-done(((bf16[4096,2048]{1,0:T(8,128)(2,1)}), bf16[128,2048]{1,0:T(8,128)(2,1)}) %reduce-scatter.4.cloned.1.call-update) | async-done | bytes 524304 | tf_op jit(solution)/shard_map/reduce_scatter | solution.py:339
  397.6 1.9 add_convert_fusion
  403.1 105.0 %reduce-scatter.8.cloned.1.call-done = bf16[128,2048]{1,0:T(8,128)(2,1)} async-done(((bf16[4096,2048]{1,0:T(8,128)(2,1)}), bf16[128,2048]{1,0:T(8,128)(2,1)}) %reduce-scatter.8.cloned.1.call-update) | async-done | bytes 524304 | tf_op jit(solution)/shard_map/reduce_scatter | solution.py:353
  508.1 1.7 fusion.48
  509.8 2.5 fusion.50
  512.5 9.9 %convolution_convert_fusion.4 = bf16[2048,256]{1,0:T(8,128)(2,1)} fusion(bf16[4096,2048]{1,0:T(8,128)(2,1)} %all-gather.10.cloned.1.call-done, bf16[4096,256]{1,0:T(8,128)(2,1)S(1)} %copy-done.8), kind=kOutput, calls=%fused_computation.27 | convolution fusion | flops 4295491584 | bytes 19922944 | tf_op jit(solution)/shard_map/dot_general | solution.py:20
  522.4 9.4 %fusion.20 = bf16[256,2048]{1,0:T(8,128)(2,1)} fusion(bf16[4096,256]{1,0:T(8,128)(2,1)S(1)} %copy-done.3, bf16[1,4096,2048]{2,1,0:T(8,128)(2,1)} %param.17), kind=kOutput, calls=%fused_computation.26 | convolution fusion | flops 4295491584 | bytes 19922944 | tf_op jit(solution)/shard_map/dot_general | solution.py:20
  531.8 4.3 convolution_convert_fusion.5
  536.8 22.2 %gain_sums.1 = f32[32,1,4096]{2,1,0:T(1,128)} custom-call(f32[1,4096]{1,0:T(1,128)} %bitcast.125), custom_call_target="tpu_custom_call" | custom-call | flops 2000000000 | bytes 16384 | tf_op jit(solution)/shard_map/gain_sums/pallas_call | solution.py:253
  561.0 23.7 %all-gather.14.cloned.1.call-done = bf16[4096,2048]{1,0:T(8,128)(2,1)} async-done(((bf16[128,2048]{1,0:T(8,128)(2,1)}), bf16[4096,2048]{1,0:T(8,128)(2,1)}) %all-gather.14.cloned.1.call-update) | async-done | bytes 16777232 | tf_op jit(solution)/shard_map/all_gather | solution.py:352
  584.8 69.0 %all-gather.12.cloned.1.call-done = bf16[4096,2048]{1,0:T(8,128)(2,1)} async-done(((bf16[128,2048]{1,0:T(8,128)(2,1)}), bf16[4096,2048]{1,0:T(8,128)(2,1)}) %all-gather.12.cloned.1.call-update) | async-done | bytes 16777232 | tf_op jit(solution)/shard_map/all_gather | solution.py:347
  653.7 9.5 %fusion.27 = bf16[1,64,2048]{2,1,0:T(8,128)(2,1)} fusion(bf16[64,4096]{1,0:T(8,128)(2,1)S(1)} %copy-done.9, bf16[4096,2048]{1,0:T(8,128)(2,1)} %all-gather.12.cloned.1.call-done), kind=kOutput, calls=%fused_computation.36 | convolution fusion | flops 1073872896 | bytes 17563648 | tf_op jit(solution)/shard_map/dot_general | solution.py:20
  663.2 59.3 %all-gather.16.cloned.1.call-done = bf16[4096,2048]{1,0:T(8,128)(2,1)} async-done(((bf16[128,2048]{1,0:T(8,128)(2,1)}), bf16[4096,2048]{1,0:T(8,128)(2,1)}) %all-gather.16.cloned.1.call-update) | async-done | bytes 16777232 | tf_op jit(solution)/shard_map/all_gather | solution.py:359
  722.5 15.1 %copy.38 = bf16[1,4096,2048]{2,1,0:T(8,128)(2,1)} copy(bf16[1,4096,2048]{2,1,0:T(8,128)(2,1)} %bitcast.117) | data formatting | bytes 33554432
  737.6 1.8 copy-done.2
  739.4 6.2 copy.39
  (83 shorter events, 17.6 us)
Async XLA Ops:
  7.2 137.3 %copy-start = (bf16[2048,256]{1,0:T(8,128)(2,1)S(1)}, bf16[2048,256]{1,0:T(8,128)(2,1)}, u32[]{:S(2)}) copy-start(bf16[2048,256]{1,0:T(8,128)(2,1)} %param.15) | copy-start | bytes 3145732
  7.2 63.0 %all-gather.8.cloned.1.call-start = ((), (), s32[]{:S(2)}) async-start(), calls=%async_computation.3 | async-start | bytes 8650752 | tf_op jit(solution)/shard_map/all_gather | solution.py:313
  8.0 136.5 %all-gather.10.cloned.1.call-start = ((), (), s32[]{:S(2)}) async-start(), calls=%async_computation.4 | async-start | bytes 17301504 | tf_op jit(solution)/shard_map/all_gather | solution.py:328
  76.5 80.7 %copy-start.10 = (bf16[256,2048]{1,0:T(8,128)(2,1)S(1)}, bf16[256,2048]{1,0:T(8,128)(2,1)}, u32[]{:S(2)}) copy-start(bf16[256,2048]{1,0:T(8,128)(2,1)} %param.16) | copy-start | bytes 3145732
  76.5 210.0 %reduce-scatter.6.cloned.1.call-start = ((), (), s32[]{:S(2)}) async-start(), calls=%async_computation.6 | async-start | bytes 17301504 | tf_op jit(solution)/shard_map/reduce_scatter | solution.py:336
  181.5 216.1 %reduce-scatter.4.cloned.1.call-start = ((), (), s32[]{:S(2)}) async-start(), calls=%async_computation.5 | async-start | bytes 17301504 | tf_op jit(solution)/shard_map/reduce_scatter | solution.py:339
  191.8 316.3 %reduce-scatter.8.cloned.1.call-start = ((), (), s32[]{:S(2)}) async-start(), calls=%async_computation.7 | async-start | bytes 17301504 | tf_op jit(solution)/shard_map/reduce_scatter | solution.py:353
  289.8 6.5 copy-start.4
  314.3 22.2 %copy-start.7 = (bf16[2048,192]{0,1:T(8,128)(2,1)S(1)}, bf16[2048,192]{0,1:T(8,128)(2,1)}, u32[]{:S(2)}) copy-start(bf16[2048,192]{0,1:T(8,128)(2,1)} %param.12) | copy-start | bytes 2359300
  346.3 54.2 %copy-start.11 = (bf16[2048]{0:T(1024)(128)(2,1)S(1)}, bf16[2048]{0:T(1024)(128)(2,1)}, u32[]{:S(2)}) copy-start(bf16[2048]{0:T(1024)(128)(2,1)} %param.11) | copy-start | bytes 12292
  346.3 163.5 %copy-start.5 = (bf16[128,2048]{1,0:T(8,128)(2,1)S(1)}, bf16[128,2048]{1,0:T(8,128)(2,1)}, u32[]{:S(2)}) copy-start(bf16[128,2048]{1,0:T(8,128)(2,1)} %copy-done.4) | copy-start | bytes 1572868
  346.3 238.4 %all-gather.14.cloned.1.call-start = ((), (), s32[]{:S(2)}) async-start(), calls=%async_computation.9 | async-start | bytes 17301504 | tf_op jit(solution)/shard_map/all_gather | solution.py:352
  399.5 112.9 %copy-start.8 = (bf16[4096,256]{1,0:T(8,128)(2,1)S(1)}, bf16[4096,256]{1,0:T(8,128)(2,1)}, u32[]{:S(2)}) copy-start(bf16[4096,256]{1,0:T(8,128)(2,1)} %fusion.10) | copy-start | bytes 6291460
  399.6 254.1 %all-gather.12.cloned.1.call-start = ((), (), s32[]{:S(2)}) async-start(), calls=%async_computation.8 | async-start | bytes 17301504 | tf_op jit(solution)/shard_map/all_gather | solution.py:347
  400.4 322.1 %all-gather.16.cloned.1.call-start = ((), (), s32[]{:S(2)}) async-start(), calls=%async_computation.10 | async-start | bytes 17301504 | tf_op jit(solution)/shard_map/all_gather | solution.py:359
  512.4 9.9 %copy-start.3 = (bf16[4096,256]{1,0:T(8,128)(2,1)S(1)}, bf16[4096,256]{1,0:T(8,128)(2,1)}, u32[]{:S(2)}) copy-start(bf16[4096,256]{1,0:T(8,128)(2,1)} %get-tuple-element.33) | copy-start | bytes 6291460
  512.4 19.4 %slice-start = ((s8[16777216]{0:T(1024)(128)(4,1)}), s8[4194304]{0:T(1024)(128)(4,1)S(1)}, s32[]{:S(2)}) async-start(s8[16777216]{0:T(1024)(128)(4,1)} %bitcast.126), calls=%async_computation.11 | async-start | bytes 8388608
  512.4 19.4 %slice-start.1 = ((s8[16777216]{0:T(1024)(128)(4,1)}), s8[4194304]{0:T(1024)(128)(4,1)S(1)}, s32[]{:S(2)}) async-start(s8[16777216]{0:T(1024)(128)(4,1)} %bitcast.126), calls=%async_computation.12 | async-start | bytes 8388608
  512.4 19.4 %slice-start.2 = ((s8[16777216]{0:T(1024)(128)(4,1)}), s8[4194304]{0:T(1024)(128)(4,1)S(1)}, s32[]{:S(2)}) async-start(s8[16777216]{0:T(1024)(128)(4,1)} %bitcast.126), calls=%async_computation.13 | async-start | bytes 8388608
  522.4 9.4 %copy-start.6 = (bf16[4096,192]{1,0:T(8,128)(2,1)S(1)}, bf16[4096,192]{1,0:T(8,128)(2,1)}, u32[]{:S(2)}) copy-start(bf16[4096,192]{1,0:T(8,128)(2,1)} %attn_bwd.1) | copy-start | bytes 4718596
  522.4 9.5 %slice-start.3 = ((s8[16777216]{0:T(1024)(128)(4,1)}), s8[4194304]{0:T(1024)(128)(4,1)S(1)}, s32[]{:S(2)}) async-start(s8[16777216]{0:T(1024)(128)(4,1)} %bitcast.126), calls=%async_computation.14 | async-start | bytes 8388608
  536.2 117.6 %copy-start.9 = (bf16[64,4096]{1,0:T(8,128)(2,1)S(1)}, bf16[64,4096]{1,0:T(8,128)(2,1)}, u32[]{:S(2)}) copy-start(bf16[64,4096]{1,0:T(8,128)(2,1)} %get-tuple-element.23.in_ref.ot_ref) | copy-start | bytes 1572868
  722.5 16.9 %copy-start.2 = (bf16[4096,2048]{1,0:T(8,128)(2,1)S(1)}, bf16[4096,2048]{1,0:T(8,128)(2,1)}, u32[]{:S(2)}) copy-start(bf16[4096,2048]{1,0:T(8,128)(2,1)} %all-gather.16.cloned.1.call-done) | copy-start | bytes 50331652
  739.4 6.2 copy-start.1
Sparse Core Ops, SparseCore 0:
  10.1 51.6 all-gather.7
  76.7 67.8 all-gather.9
  181.6 104.8 reduce-scatter.5
  290.8 106.8 reduce-scatter.3
  401.2 106.8 reduce-scatter.7
  510.6 74.1 all-gather.13
  586.8 66.8 all-gather.11
  655.8 66.6 all-gather.15

commit v2 on v1

--- a/solution.py
+++ b/solution.py
@@ -1,4 +1,5 @@
 import functools
+import math
 
 import jax
 import jax.numpy as jnp
@@ -274,6 +275,176 @@
     return ref
 
 
+def ring_place(n, q):
+    me = lax.axis_index('model')
+    side = math.isqrt(n // 2)
+    core = lax.rem(me, 2)
+    chip = me // 2
+    x = lax.rem(chip, side)
+    y = chip // side
+    turn = q // 2
+    sign = 1 - 2 * lax.rem(q, 2)
+    a = x * (1 - turn) + y * turn
+    b = y * (1 - turn) + x * turn
+
+    def chip_at(pa, pb):
+        pa = lax.rem(pa + 2 * side, side)
+        pb = lax.rem(pb + 2 * side, side)
+        return (pb * (1 - turn) + pa * turn) * side + pa * (1 - turn) + pb * turn
+
+    return side, core, sign, a, b, chip_at
+
+
+def greet_neighbours(n):
+    me = lax.axis_index('model')
+    barrier = pltpu.get_barrier_semaphore()
+    core = lax.rem(me, 2)
+    pl.semaphore_signal(barrier, inc=1, device_id={'model': me + 1 - 2 * core}, device_id_type=MESH)
+
+    def hello(q, _):
+        side, core, sign, a, b, chip_at = ring_place(n, q)
+        pl.semaphore_signal(barrier, inc=1, device_id={'model': chip_at(a + sign, b) * 2 + core}, device_id_type=MESH)
+        return 0
+
+    lax.fori_loop(0, 4, hello, 0)
+    pl.semaphore_wait(barrier, 5)
+
+
+def reduce_kernel(n, r_dim, l_ref, r_ref, out_ref, l_peer, r_peer, first, slot1, slot2, s_send, s_recv, p_send, p_recv, x_send, x_recv):
+    me = lax.axis_index('model')
+    my_core = lax.rem(me, 2)
+    chips, _, tb, _ = l_ref.shape
+    width = out_ref.shape[1] // 4
+    side = math.isqrt(chips)
+    greet_neighbours(n)
+    peer = {'model': me + 1 - 2 * my_core}
+    swap = [
+        pltpu.make_async_remote_copy(src, dst, x_send.at[i], x_recv.at[i], device_id=peer, device_id_type=MESH)
+        for i, (src, dst) in enumerate([(r_ref, r_peer), (l_ref.at[:, 1 - my_core], l_peer)])
+    ]
+    for copy in swap:
+        copy.start()
+
+    def partial(q, chip):
+        cols = pl.ds(pl.multiple_of(q * width, width), width)
+        mine, other = (r_ref[:, cols], r_peer[:, cols]) if r_dim == 0 else (r_ref[cols, :], r_peer[cols, :])
+        return mm(l_ref[chip, my_core], mine, 1, r_dim) + mm(l_peer[chip], other, 1, r_dim)
+
+    def hop(q, s, j, src):
+        _, core, sign, a, b, chip_at = ring_place(n, q)
+        at = (q * (side - 1) + s) * side + j
+        return pltpu.make_async_remote_copy(
+            src, slot1.at[at], s_send.at[at], s_recv.at[at], device_id={'model': chip_at(a + sign, b) * 2 + core}, device_id_type=MESH)
+
+    def turn_hop(q, s, src):
+        _, core, sign, a, b, chip_at = ring_place(n, q)
+        at = q * (side - 1) + s
+        return pltpu.make_async_remote_copy(
+            src, slot2.at[at], p_send.at[at], p_recv.at[at], device_id={'model': chip_at(a, b + sign) * 2 + core}, device_id_type=MESH)
+
+    def arrived(q, s, j):
+        return (q * (side - 1) + s) * side + j
+
+    for copy in swap:
+        copy.wait()
+
+    def start_round(t, _):
+        j, q = t // 4, lax.rem(t, 4)
+        _, _, sign, a, b, chip_at = ring_place(n, q)
+        at = q * side + j
+        first[at] = partial(q, chip_at(a - sign, b - sign * (1 + j))).astype(BF16)
+        hop(q, 0, j, first.at[at]).start()
+        return 0
+
+    lax.fori_loop(0, 4 * side, start_round, 0)
+
+    def middle_round(t, _):
+        s, rest = 1 + t // (4 * side), lax.rem(t, 4 * side)
+        j, q = rest // 4, lax.rem(rest, 4)
+        _, _, sign, a, b, chip_at = ring_place(n, q)
+        at = arrived(q, s - 1, j)
+        own = partial(q, chip_at(a - sign * (1 + s), b - sign * (1 + j)))
+        hop(q, s - 1, j, slot1.at[at]).wait_recv()
+        slot1[at] = (slot1[at].astype(F32) + own).astype(BF16)
+        hop(q, s, j, slot1.at[at]).start()
+        return 0
+
+    lax.fori_loop(0, 4 * side * (side - 2), middle_round, 0)
+
+    def last_sum(q, j):
+        _, _, sign, a, b, chip_at = ring_place(n, q)
+        at = arrived(q, side - 2, j)
+        own = partial(q, chip_at(a, b - sign * (1 + j)))
+        hop(q, side - 2, j, slot1.at[at]).wait_recv()
+        return at, slot1[at].astype(F32) + own
+
+    def turn_first(q, _):
+        at, total = last_sum(q, 0)
+        slot1[at] = total.astype(BF16)
+        turn_hop(q, 0, slot1.at[at]).start()
+        return 0
+
+    lax.fori_loop(0, 4, turn_first, 0)
+
+    def turn_round(t, _):
+        s, q = 1 + t // 4, lax.rem(t, 4)
+        _, total = last_sum(q, s)
+        at = q * (side - 1) + s - 1
+        turn_hop(q, s - 1, slot2.at[at]).wait_recv()
+        slot2[at] = (slot2[at].astype(F32) + total).astype(BF16)
+        turn_hop(q, s, slot2.at[at]).start()
+        return 0
+
+    lax.fori_loop(0, 4 * (side - 2), turn_round, 0)
+
+    def turn_last(q, _):
+        _, total = last_sum(q, side - 1)
+        at = q * (side - 1) + side - 2
+        turn_hop(q, side - 2, slot2.at[at]).wait_recv()
+        out_ref[:, pl.ds(pl.multiple_of(q * width, width), width)] = (slot2[at].astype(F32) + total).astype(BF16)
+        return 0
+
+    lax.fori_loop(0, 4, turn_last, 0)
+
+    def drain(t, _):
+        q, s = t // (side - 1), lax.rem(t, side - 1)
+        turn_hop(q, s, slot2.at[t]).wait_send()
+        for j in range(side):
+            hop(q, s, j, slot1.at[t * side + j]).wait_send()
+        return 0
+
+    lax.fori_loop(0, 4 * (side - 1), drain, 0)
+
+
+def matmul_reduce_scatter(n, left, right, r_dim, collective_id, name):
+    t, k = left.shape
+    f = right.shape[1 - r_dim]
+    chips = n // 2
+    side = math.isqrt(chips)
+    tb = t // n
+    hops = 4 * (side - 1)
+    vmem = pl.BlockSpec(memory_space=pltpu.VMEM)
+    return pl.pallas_call(
+        functools.partial(reduce_kernel, n, r_dim),
+        out_shape=jax.ShapeDtypeStruct((tb, f), BF16),
+        in_specs=[vmem, vmem],
+        out_specs=vmem,
+        scratch_shapes=[
+            pltpu.VMEM((chips, tb, k), BF16),
+            pltpu.VMEM(right.shape, BF16),
+            pltpu.VMEM((4 * side, tb, f // 4), BF16),
+            pltpu.VMEM((hops * side, tb, f // 4), BF16),
+            pltpu.VMEM((hops, tb, f // 4), BF16),
+            pltpu.SemaphoreType.DMA((hops * side,)), pltpu.SemaphoreType.DMA((hops * side,)),
+            pltpu.SemaphoreType.DMA((hops,)), pltpu.SemaphoreType.DMA((hops,)),
+            pltpu.SemaphoreType.DMA((2,)), pltpu.SemaphoreType.DMA((2,)),
+        ],
+        compiler_params=pltpu.CompilerParams(collective_id=collective_id, has_side_effects=True, vmem_limit_bytes=40 * 1024 * 1024),
+        cost_estimate=pl.CostEstimate(flops=40_000_000_000, bytes_accessed=4 * t * k, transcendentals=0),
+        name=name,
+    )(left.reshape(chips, 2, tb, k), right)
+
+
 def ln_rows(z, gain):
     wide = z.astype(F32)
     mean = jnp.mean(wide, axis=-1, keepdims=True)
@@ -331,12 +502,10 @@
         up = mm(b1, w_up, 1, 0).astype(BF16)
         gelu_out, gelu_pull = jax.vjp(gelu_tanh, up)
         (d_up,) = gelu_pull(d_gelu)
-        d_b1 = mm(d_up, w_up, 1, 1).astype(BF16)
+        d_b1 = matmul_reduce_scatter(n, d_up, w_up, 1, 3, 'reduce_d_b1')
         late_gelu, d_b1 = lax.optimization_barrier((gelu_out, d_b1))
-        d_b1 = lax.psum_scatter(d_b1, 'model', scatter_dimension=0, tiled=True)
-        part_two = mm(late_gelu, w_down, 1, 0).astype(BF16)
+        part_two = matmul_reduce_scatter(n, late_gelu, w_down, 0, 4, 'reduce_y')
         late_gelu, late_up, part_two = lax.optimization_barrier((late_gelu, d_up, part_two))
-        part_two = lax.psum_scatter(part_two, 'model', scatter_dimension=0, tiled=True)
         d_w_down = mm(late_gelu, dy, 0, 0).astype(BF16)
         d_w_up = mm(b1, late_up, 0, 0).astype(BF16)
 
@@ -347,10 +516,9 @@
         d_resid = lax.all_gather(d_resid_s, 'model', axis=0, tiled=True)
 
         d_qkv = attention_backward(q, k, v, qkvt, ot, dot, lse, start_row, tab, bq, bk)
-        part_two, _ = lax.optimization_barrier((part_two, d_qkv))
         y_s = (resid.astype(F32) + part_two.astype(F32)).astype(BF16)
         y_out = lax.all_gather(y_s[None], 'model', axis=1, tiled=True)
-        d_norm = lax.psum_scatter(mm(d_qkv, w_qkv, 1, 1).astype(BF16), 'model', scatter_dimension=0, tiled=True)
+        d_norm = matmul_reduce_scatter(n, d_qkv, w_qkv.T, 0, 5, 'reduce_d_x')
         d_w_qkv = mm(a_full, d_qkv, 0, 0).astype(BF16)
         d_w_out = mm(ot, d_resid, 1, 0).astype(BF16)
 

time: 759 us -> 647 us (0.85)
  waiting for transfers between devices: 472 us -> 224 us
  Pallas kernels: 116 us -> 280 us
  matrix products: 101 us -> 71.9 us
    reduce_scatter x3 -> x0, waiting for transfers between devices: 251 us -> none  [the longest x1 105 us: local_step(): lax.psum_scatter(mm(d_qkv, w_qkv, 1, 1).astype(BF16), 'model', scatter_di...]
    pallas_call x0 -> x3, Pallas kernels: none -> 169 us  [matmul_reduce_scatter(): pl.pallas_call(functools.partial(reduce_kernel, n, r_dim), out_shape=jax....]
    all_gather x1, waiting for transfers between devices: 23.7 us -> 68.6 us  [local_step(): y_out = lax.all_gather(y_s[None], 'model', axis=1, tiled=True)]
    all_gather x1, waiting for transfers between devices: 59.3 us -> 21.3 us  [local_step(): d_x = lax.all_gather((d_resid_s + d_ln)[None], 'model', axis=1, tiled=True)]
    dot_general x11 -> x8, matrix products: 101 us -> 71.9 us  [mm(): lax.dot_general(a, b, (((ca,), (cb,)), ((), ())), preferred_element_type=...]
    unnamed x34 -> x48, local copies, waits for them, and re-layouts: 23.1 us -> 23.9 us
  transfers between devices with their start and end apart: 8 -> 5, of which waited for: 7 -> 4; matrix products, arithmetic and copies ran while one was open for 11% -> 6% of each run, Pallas kernels for 15% -> 11%
where the time goes in v2:
time: 647 us; the launch traced here: 638 us
  Pallas kernels  280 us (43%)
  waiting for transfers between devices  224 us (35%)
  matrix products  71.9 us (11%)
  local copies, waits for them, and re-layouts  28.3 us (4%)
  other arithmetic  18.2 us (3%)
  between operations  14.4 us (2%)
    pallas_call x3, Pallas kernels, matmul_reduce_scatter(): pl.pallas_call(functools.partial(reduce_kernel, n, r_dim), out_shape=jax....  169 us
    dot_general x8, matrix products, mm(): lax.dot_general(a, b, (((ca,), (cb,)), ((), ())), preferred_element_type=...  71.9 us
    all_gather x1, waiting for transfers between devices, local_step(): y_out = lax.all_gather(y_s[None], 'model', axis=1, tiled=True)  68.6 us
    all_gather x1, waiting for transfers between devices, local_step(): d_resid = lax.all_gather(d_resid_s, 'model', axis=0, tiled=True)  68.6 us
    all_gather x1, waiting for transfers between devices, local_step(): b1 = lax.all_gather(b1_s, 'model', axis=0, tiled=True)  63.6 us
    pallas_call x3, Pallas kernels, exchange(): pl.pallas_call(functools.partial(exchange_kernel, n, src_of, dst_of), out...  56.3 us
    unnamed x48, local copies, waits for them, and re-layouts  23.9 us
    all_gather x1, waiting for transfers between devices, local_step(): d_x = lax.all_gather((d_resid_s + d_ln)[None], 'model', axis=1, tiled=True)  21.3 us
  transfers between devices with their start and end apart: 5, of which 4 were waited for; matrix products, arithmetic and copies ran while one was open for 6% of the time, Pallas kernels for 11%

profile of v2, /device:TPU:97, one launch (start us, length us, event | category | flops | bytes accessed | tf_op | source)
XLA Modules:
  0.0 637.7 jit_solution(15162492284263430847)
XLA Ops:
  9.2 1.5 add_select_fusion
  11.8 1.3 reshape.408.g_ref
  15.4 20.6 %ln_qkv.1 = (bf16[4096,2048]{1,0:T(8,128)(2,1)}, bf16[4096,64]{1,0:T(8,128)(2,1)}, bf16[4096,64]{1,0:T(8,128)(2,1)}, bf16[4096,64]{1,0:T(8,128)(2,1)}, bf16[192,4096]{1,0:T(8,128)(2,1)}) custom-call(bf16[4096,2048]{1,0:T(8,128)(2,1)} %bitcast.120, bf16[1,2048]{1,0:T(2,128)(2,1)} %reshape.408.g_ref, bf16[192,2048]{1,0:T(8,128)(2,1)} %bitcast.113), custom_call_target="tpu_custom_call" | custom-call | flops 3388997632 | bytes 33554432 | tf_op jit(solution)/shard_map/ln_qkv/pallas_call | solution.py:46
  36.0 13.6 %attn_fwd.1 = (bf16[64,4096]{1,0:T(8,128)(2,1)}, f32[1,4096]{1,0:T(1,128)}) custom-call(s32[4,8]{1,0:T(4,128)} %pad_add_fusion.tab_ref, bf16[4096,64]{1,0:T(8,128)(2,1)} %get-tuple-element.20.k_ref, bf16[192,4096]{1,0:T(8,128)(2,1)} %get-tuple-element.21.qt_ref.vt_ref.t_ref, bf16[192,4096]{1,0:T(8,128)(2,1)} %get-tuple-element.21.qt_ref.vt_ref.t_ref, ...), custom_call_target="tpu_custom_call" | custom-call | flops 17179869184 | bytes 2097152 | tf_op jit(solution)/shard_map/attn_fwd/pallas_call | solution.py:122
  49.7 19.2 %heads_to_tokens.1 = bf16[32,64,128]{2,1,0:T(8,128)(2,1)} custom-call(bf16[64,4096]{1,0:T(8,128)(2,1)} %get-tuple-element.22.in_ref.ot_ref), custom_call_target="tpu_custom_call" | custom-call | flops 2000000000 | bytes 1048576 | tf_op jit(solution)/shard_map/heads_to_tokens/pallas_call | solution.py:254
  68.9 4.9 fusion.54
  78.3 1.3 fusion.41
  80.1 63.6 %all-gather.10.cloned.1.call-done = bf16[4096,2048]{1,0:T(8,128)(2,1)} async-done(((bf16[128,2048]{1,0:T(8,128)(2,1)}), bf16[4096,2048]{1,0:T(8,128)(2,1)}) %all-gather.10.cloned.1.call-update) | async-done | bytes 16777232 | tf_op jit(solution)/shard_map/all_gather | solution.py:499
  143.7 11.5 %fusion.15 = (bf16[4096,256]{1,0:T(8,128)(2,1)S(1)}, bf16[4096,256]{1,0:T(8,128)(2,1)S(1)}) fusion(bf16[4096,2048]{1,0:T(8,128)(2,1)} %all-gather.10.cloned.1.call-done, bf16[2048,256]{1,0:T(8,128)(2,1)S(1)} %copy-done.1), kind=kOutput, calls=%fused_computation.20 | convolution fusion | flops 4306501632 | bytes 22020096 | tf_op jit(solution)/shard_map/dot_general | solution.py:21
  155.2 13.2 %fusion.10 = bf16[4096,256]{1,0:T(8,128)(2,1)S(1)} fusion(bf16[4096,256]{1,0:T(8,128)(2,1)S(1)} %get-tuple-element.48, bf16[256,2048]{1,0:T(8,128)(2,1)S(1)} %copy-done.2, bf16[1,4096,2048]{2,1,0:T(8,128)(2,1)} %param.17), kind=kOutput, calls=%fused_computation.15 | convolution fusion | flops 4319084544 | bytes 22020096 | tf_op jit(solution)/shard_map/dot_general | solution.py:21
  168.4 56.5 %reduce_d_b1.1 = bf16[128,2048]{1,0:T(8,128)(2,1)S(1)} custom-call(bf16[16,2,128,256]{3,2,1,0:T(8,128)(2,1)S(1)} %bitcast.115, bf16[2048,256]{1,0:T(8,128)(2,1)S(1)} %copy-done.1), custom_call_target="tpu_custom_call" | custom-call | flops 40000000000 | bytes 4194304 | tf_op jit(solution)/shard_map/reduce_d_b1/pallas_call | solution.py:427
  224.9 57.1 %reduce_y.1 = bf16[128,2048]{1,0:T(8,128)(2,1)S(1)} custom-call(bf16[16,2,128,256]{3,2,1,0:T(8,128)(2,1)S(1)} %bitcast.112, bf16[256,2048]{1,0:T(8,128)(2,1)S(1)} %copy-done.2), custom_call_target="tpu_custom_call" | custom-call | flops 40000000000 | bytes 4194304 | tf_op jit(solution)/shard_map/reduce_y/pallas_call | solution.py:427
  282.0 1.3 fusion.46
  283.3 1.6 fusion.49
  284.9 6.4 %fusion.26 = bf16[2048,128]{0,1:T(8,128)(2,1)S(1)} fusion(bf16[128,2048]{1,0:T(8,128)(2,1)S(1)} %fusion.49, bf16[2048,2048]{1,0:T(8,128)(2,1)} %bitcast.117), kind=kOutput, calls=%fused_computation.31 | convolution fusion | flops 1074003968 | bytes 9437184 | tf_op jit(solution)/shard_map/dot_general | solution.py:21
  292.3 17.7 %tokens_to_heads.1.dot_ref = bf16[64,4096]{1,0:T(8,128)(2,1)} custom-call(bf16[32,64,128]{2,1,0:T(8,128)(2,1)} %bitcast.125), custom_call_target="tpu_custom_call" | custom-call | flops 2000000000 | bytes 1048576 | tf_op jit(solution)/shard_map/tokens_to_heads/pallas_call | solution.py:254
  310.1 20.5 %attn_bwd.1 = bf16[4096,192]{1,0:T(8,128)(2,1)} custom-call(s32[4,8]{1,0:T(4,128)} %pad_add_fusion.tab_ref, bf16[4096,64]{1,0:T(8,128)(2,1)} %get-tuple-element.26.q_ref, bf16[4096,64]{1,0:T(8,128)(2,1)} %get-tuple-element.20.k_ref, bf16[4096,64]{1,0:T(8,128)(2,1)} %get-tuple-element.27.v_ref, bf16[192,4096]{1,0:T(8,128)(2,1)} %get-tuple-element.21.qt_ref.vt_ref.t_ref, ...), custom_call_target="tpu_custom_call" | custom-call | flops 42949672960 | bytes 4194304 | tf_op jit(solution)/shard_map/attn_bwd/pallas_call | solution.py:198
  330.6 1.6 copy-done.5
  332.2 55.3 %reduce_d_x.1 = bf16[128,2048]{1,0:T(8,128)(2,1)S(1)} custom-call(bf16[16,2,128,192]{3,2,1,0:T(8,128)(2,1)S(1)} %bitcast.116, bf16[192,2048]{1,0:T(8,128)(2,1)S(1)} %bitcast.114), custom_call_target="tpu_custom_call" | custom-call | flops 40000000000 | bytes 3145728 | tf_op jit(solution)/shard_map/reduce_d_x/pallas_call | solution.py:427
  387.5 1.5 fusion.48
  389.0 2.4 fusion.50
  393.4 19.4 %gain_sums.1 = f32[32,1,4096]{2,1,0:T(1,128)} custom-call(f32[1,4096]{1,0:T(1,128)} %bitcast.130), custom_call_target="tpu_custom_call" | custom-call | flops 2000000000 | bytes 16384 | tf_op jit(solution)/shard_map/gain_sums/pallas_call | solution.py:254
  412.8 1.4 reduce_sum.109
  414.8 10.8 %convolution_convert_fusion.2 = bf16[2048,192]{0,1:T(8,128)(2,1)} fusion(bf16[4096,2048]{1,0:T(8,128)(2,1)} %get-tuple-element.29, bf16[4096,192]{1,0:T(8,128)(2,1)} %attn_bwd.1), kind=kOutput, calls=%fused_computation.25 | convolution fusion | flops 3221618688 | bytes 19136512 | tf_op jit(solution)/shard_map/dot_general | solution.py:21
  425.7 9.9 %convolution_convert_fusion.1 = bf16[2048,256]{1,0:T(8,128)(2,1)} fusion(bf16[4096,2048]{1,0:T(8,128)(2,1)} %all-gather.10.cloned.1.call-done, bf16[4096,256]{1,0:T(8,128)(2,1)S(1)} %copy-done.4), kind=kOutput, calls=%fused_computation.24 | convolution fusion | flops 4295491584 | bytes 19922944 | tf_op jit(solution)/shard_map/dot_general | solution.py:21
  435.6 5.5 fusion.20
  441.1 21.3 %all-gather.16.cloned.1.call-done = bf16[4096,2048]{1,0:T(8,128)(2,1)} async-done(((bf16[128,2048]{1,0:T(8,128)(2,1)}), bf16[4096,2048]{1,0:T(8,128)(2,1)}) %all-gather.16.cloned.1.call-update) | async-done | bytes 16777232 | tf_op jit(solution)/shard_map/all_gather | solution.py:527
  462.4 68.6 %all-gather.14.cloned.1.call-done = bf16[4096,2048]{1,0:T(8,128)(2,1)} async-done(((bf16[128,2048]{1,0:T(8,128)(2,1)}), bf16[4096,2048]{1,0:T(8,128)(2,1)}) %all-gather.14.cloned.1.call-update) | async-done | bytes 16777232 | tf_op jit(solution)/shard_map/all_gather | solution.py:520
  531.0 68.6 %all-gather.12.cloned.1.call-done = bf16[4096,2048]{1,0:T(8,128)(2,1)} async-done(((bf16[128,2048]{1,0:T(8,128)(2,1)}), bf16[4096,2048]{1,0:T(8,128)(2,1)}) %all-gather.12.cloned.1.call-update) | async-done | bytes 16777232 | tf_op jit(solution)/shard_map/all_gather | solution.py:516
  599.7 9.6 %fusion.27 = bf16[1,64,2048]{2,1,0:T(8,128)(2,1)} fusion(bf16[64,4096]{1,0:T(8,128)(2,1)S(1)} %copy-done.9, bf16[4096,2048]{1,0:T(8,128)(2,1)} %all-gather.12.cloned.1.call-done), kind=kOutput, calls=%fused_computation.33 | convolution fusion | flops 1073872896 | bytes 17563648 | tf_op jit(solution)/shard_map/dot_general | solution.py:21
  609.3 15.3 %copy.38 = bf16[1,4096,2048]{2,1,0:T(8,128)(2,1)} copy(bf16[1,4096,2048]{2,1,0:T(8,128)(2,1)} %bitcast.124) | data formatting | bytes 33554432
  624.7 6.2 copy.39
  (88 shorter events, 13.8 us)
Async XLA Ops:
  7.2 61.8 %all-gather.8.cloned.1.call-start = ((), (), s32[]{:S(2)}) async-start(), calls=%async_computation | async-start | bytes 8650752 | tf_op jit(solution)/shard_map/all_gather | solution.py:484
  8.0 135.7 %all-gather.10.cloned.1.call-start = ((), (), s32[]{:S(2)}) async-start(), calls=%async_computation.1 | async-start | bytes 17301504 | tf_op jit(solution)/shard_map/all_gather | solution.py:499
  68.9 7.6 %copy-start.11 = (bf16[2048]{0:T(1024)(128)(2,1)S(1)}, bf16[2048]{0:T(1024)(128)(2,1)}, u32[]{:S(2)}) copy-start(bf16[2048]{0:T(1024)(128)(2,1)} %param.11) | copy-start | bytes 12292
  73.9 1.0 copy-start.6
  73.9 69.8 %copy-start.1 = (bf16[2048,256]{1,0:T(8,128)(2,1)S(1)}, bf16[2048,256]{1,0:T(8,128)(2,1)}, u32[]{:S(2)}) copy-start(bf16[2048,256]{1,0:T(8,128)(2,1)} %r_ref.2) | copy-start | bytes 3145732
  75.9 386.4 %all-gather.16.cloned.1.call-start = ((), (), s32[]{:S(2)}) async-start(), calls=%async_computation.4 | async-start | bytes 17301504 | tf_op jit(solution)/shard_map/all_gather | solution.py:527
  78.3 76.9 %copy-start.12 = (f32[128]{0:T(128)}, f32[128]{0:T(128)S(1)}, u32[]{:S(2)}) copy-start(f32[128]{0:T(128)S(1)} %broadcast_multiply_fusion.2) | copy-start | bytes 1540
  143.7 11.5 %copy-start.2 = (bf16[256,2048]{1,0:T(8,128)(2,1)S(1)}, bf16[256,2048]{1,0:T(8,128)(2,1)}, u32[]{:S(2)}) copy-start(bf16[256,2048]{1,0:T(8,128)(2,1)} %r_ref.3) | copy-start | bytes 3145732
  168.4 56.5 %copy-start.3 = (bf16[4096,256]{1,0:T(8,128)(2,1)}, bf16[4096,256]{1,0:T(8,128)(2,1)S(1)}, u32[]{:S(2)}) copy-start(bf16[4096,256]{1,0:T(8,128)(2,1)S(1)} %fusion.10) | copy-start | bytes 6291460
  224.9 57.1 %copy-start.7 = (f32[128,2048]{1,0:T(8,128)S(1)}, f32[128,2048]{1,0:T(8,128)}, u32[]{:S(2)}) copy-start(f32[128,2048]{1,0:T(8,128)} %copy-done.6) | copy-start | bytes 3145732
  284.9 104.2 %copy-start.8 = (bf16[128,2048]{1,0:T(8,128)(2,1)}, bf16[128,2048]{1,0:T(8,128)(2,1)S(1)}, u32[]{:S(2)}) copy-start(bf16[128,2048]{1,0:T(8,128)(2,1)S(1)} %fusion.49) | copy-start | bytes 1572868
  310.1 20.5 %copy-start = (bf16[2048,192]{0,1:T(8,128)(2,1)S(1)}, bf16[2048,192]{0,1:T(8,128)(2,1)}, u32[]{:S(2)}) copy-start(bf16[2048,192]{0,1:T(8,128)(2,1)} %param.12) | copy-start | bytes 2359300
  330.6 1.6 copy-start.5
  332.1 55.3 %copy-start.10 = (f32[2048]{0:T(1024)S(1)}, f32[2048]{0:T(1024)}, u32[]{:S(2)}) copy-start(f32[2048]{0:T(1024)} %convert_element_type.100) | copy-start | bytes 24580
  332.1 55.3 %copy-start.13 = (f32[128]{0:T(128)S(1)}, f32[128]{0:T(128)}, u32[]{:S(2)}) copy-start(f32[128]{0:T(128)} %copy-done.12) | copy-start | bytes 1540
  332.2 55.3 %copy-start.14 = (f32[128]{0:T(128)S(1)}, f32[128]{0:T(128)}, u32[]{:S(2)}) copy-start(f32[128]{0:T(128)} %add_rsqrt_fusion) | copy-start | bytes 1540
  391.5 139.5 %all-gather.14.cloned.1.call-start = ((), (), s32[]{:S(2)}) async-start(), calls=%async_computation.3 | async-start | bytes 17301504 | tf_op jit(solution)/shard_map/all_gather | solution.py:520
  392.1 207.5 %all-gather.12.cloned.1.call-start = ((), (), s32[]{:S(2)}) async-start(), calls=%async_computation.2 | async-start | bytes 17301504 | tf_op jit(solution)/shard_map/all_gather | solution.py:516
  414.8 10.9 %copy-start.4 = (bf16[4096,256]{1,0:T(8,128)(2,1)S(1)}, bf16[4096,256]{1,0:T(8,128)(2,1)}, u32[]{:S(2)}) copy-start(bf16[4096,256]{1,0:T(8,128)(2,1)} %copy-done.3) | copy-start | bytes 6291460
  414.8 20.8 %slice-start = ((s8[16777216]{0:T(1024)(128)(4,1)}), s8[4194304]{0:T(1024)(128)(4,1)S(1)}, s32[]{:S(2)}) async-start(s8[16777216]{0:T(1024)(128)(4,1)} %bitcast.118), calls=%async_computation.5 | async-start | bytes 8388608
  414.8 20.8 %slice-start.1 = ((s8[16777216]{0:T(1024)(128)(4,1)}), s8[4194304]{0:T(1024)(128)(4,1)S(1)}, s32[]{:S(2)}) async-start(s8[16777216]{0:T(1024)(128)(4,1)} %bitcast.118), calls=%async_computation.6 | async-start | bytes 8388608
  425.6 9.9 %slice-start.2 = ((s8[16777216]{0:T(1024)(128)(4,1)}), s8[4194304]{0:T(1024)(128)(4,1)S(1)}, s32[]{:S(2)}) async-start(s8[16777216]{0:T(1024)(128)(4,1)} %bitcast.118), calls=%async_computation.7 | async-start | bytes 8388608
  425.6 9.9 %slice-start.3 = ((s8[16777216]{0:T(1024)(128)(4,1)}), s8[4194304]{0:T(1024)(128)(4,1)S(1)}, s32[]{:S(2)}) async-start(s8[16777216]{0:T(1024)(128)(4,1)} %bitcast.118), calls=%async_computation.8 | async-start | bytes 8388608
  435.6 164.1 %copy-start.9 = (bf16[64,4096]{1,0:T(8,128)(2,1)S(1)}, bf16[64,4096]{1,0:T(8,128)(2,1)}, u32[]{:S(2)}) copy-start(bf16[64,4096]{1,0:T(8,128)(2,1)} %get-tuple-element.22.in_ref.ot_ref) | copy-start | bytes 1572868
  599.7 25.0 %slice-start.4 = ((s8[16777216]{0:T(1024)(128)(4,1)}), s8[4194304]{0:T(1024)(128)(4,1)S(1)}, s32[]{:S(2)}) async-start(s8[16777216]{0:T(1024)(128)(4,1)} %bitcast.121), calls=%async_computation.9 | async-start | bytes 8388608
  599.7 25.0 %slice-start.5 = ((s8[16777216]{0:T(1024)(128)(4,1)}), s8[4194304]{0:T(1024)(128)(4,1)S(1)}, s32[]{:S(2)}) async-start(s8[16777216]{0:T(1024)(128)(4,1)} %bitcast.121), calls=%async_computation.10 | async-start | bytes 8388608
  609.3 15.4 %slice-start.6 = ((s8[16777216]{0:T(1024)(128)(4,1)}), s8[4194304]{0:T(1024)(128)(4,1)S(1)}, s32[]{:S(2)}) async-start(s8[16777216]{0:T(1024)(128)(4,1)} %bitcast.121), calls=%async_computation.11 | async-start | bytes 8388608
  609.3 15.4 %slice-start.7 = ((s8[16777216]{0:T(1024)(128)(4,1)}), s8[4194304]{0:T(1024)(128)(4,1)S(1)}, s32[]{:S(2)}) async-start(s8[16777216]{0:T(1024)(128)(4,1)} %bitcast.121), calls=%async_computation.12 | async-start | bytes 8388608
Sparse Core Ops, SparseCore 0:
  10.1 51.6 all-gather.7
  76.1 67.6 all-gather.9
  391.6 70.6 all-gather.15
  464.3 66.6 all-gather.13
  532.9 66.6 all-gather.11

commit v3 on v2

--- a/solution.py
+++ b/solution.py
@@ -7,6 +7,7 @@
 from jax.experimental import pallas as pl
 from jax.experimental.pallas import tpu as pltpu
 from jax.sharding import PartitionSpec as P
+
 
 LN_EPS = 1e-5
 LOG2E = 1.4426950408889634
@@ -250,7 +251,7 @@
     own.wait()
 
 
-def exchange(n, value, out_shape, src_of, dst_of, collective_id, name):
+def exchange(n, value, out_shape, src_of, dst_of, collective_id):
     return pl.pallas_call(
         functools.partial(exchange_kernel, n, src_of, dst_of),
         out_shape=jax.ShapeDtypeStruct(out_shape, value.dtype),
@@ -259,7 +260,6 @@
         scratch_shapes=[pltpu.SemaphoreType.DMA((n,)), pltpu.SemaphoreType.DMA((n,)), pltpu.SemaphoreType.DMA],
         compiler_params=pltpu.CompilerParams(collective_id=collective_id, has_side_effects=True),
         cost_estimate=pl.CostEstimate(flops=2_000_000_000, bytes_accessed=2 * value.size * 2, transcendentals=0),
-        name=name,
     )(value)
 
 
@@ -302,7 +302,7 @@
     pl.semaphore_signal(barrier, inc=1, device_id={'model': me + 1 - 2 * core}, device_id_type=MESH)
 
     def hello(q, _):
-        side, core, sign, a, b, chip_at = ring_place(n, q)
+        _, core, sign, a, b, chip_at = ring_place(n, q)
         pl.semaphore_signal(barrier, inc=1, device_id={'model': chip_at(a + sign, b) * 2 + core}, device_id_type=MESH)
         return 0
 
@@ -313,7 +313,7 @@
 def reduce_kernel(n, r_dim, l_ref, r_ref, out_ref, l_peer, r_peer, first, slot1, slot2, s_send, s_recv, p_send, p_recv, x_send, x_recv):
     me = lax.axis_index('model')
     my_core = lax.rem(me, 2)
-    chips, _, tb, _ = l_ref.shape
+    chips, _, _, _ = l_ref.shape
     width = out_ref.shape[1] // 4
     side = math.isqrt(chips)
     greet_neighbours(n)
@@ -416,7 +416,7 @@
     lax.fori_loop(0, 4 * (side - 1), drain, 0)
 
 
-def matmul_reduce_scatter(n, left, right, r_dim, collective_id, name):
+def matmul_reduce_scatter(n, left, right, r_dim, collective_id):
     t, k = left.shape
     f = right.shape[1 - r_dim]
     chips = n // 2
@@ -441,8 +441,195 @@
         ],
         compiler_params=pltpu.CompilerParams(collective_id=collective_id, has_side_effects=True, vmem_limit_bytes=40 * 1024 * 1024),
         cost_estimate=pl.CostEstimate(flops=40_000_000_000, bytes_accessed=4 * t * k, transcendentals=0),
-        name=name,
     )(left.reshape(chips, 2, tb, k), right)
+
+
+def gelu_parts(up):
+    c = math.sqrt(2.0 / math.pi)
+    sq = up * up
+    th = jnp.tanh(c * (up + 0.044715 * (sq * up)))
+    cdf = 0.5 + 0.5 * th
+    slope = cdf + up * (0.5 * (1.0 - th * th)) * (c + (3 * 0.044715 * c) * sq)
+    return up * cdf, slope
+
+
+def gather_mlp_kernel(n, own_ref, up_ref, down_ref, dy_ref, b1_ref, gelu_ref, d_up_ref,
+                      b1, acc, dg, dy_buf, a_send, a_recv, b_send, b_recv, x_send, x_recv, dy_sem, out_sem):
+    me = lax.axis_index('model')
+    my_core = lax.rem(me, 2)
+    _, h = own_ref.shape
+    width = h // 4
+    side = math.isqrt(n // 2)
+    rounds = side * side
+    peer = {'model': me + 1 - 2 * my_core}
+
+    def dy_copy(t):
+        return pltpu.make_async_copy(dy_ref.at[t], dy_buf.at[lax.rem(t, 2)], dy_sem.at[lax.rem(t, 2)])
+
+    dy_copy(0).start()
+    dy_copy(1).start()
+    greet_neighbours(n)
+
+    def cols_of(q):
+        return pl.ds(pl.multiple_of(q * width, width), width)
+
+    def place(q, r):
+        _, _, sign, a, b, chip_at = ring_place(n, q)
+        return chip_at(a - sign * lax.rem(r, side), b - sign * (r // side))
+
+    def along_a(q, j, src, blk):
+        _, core, sign, a, b, chip_at = ring_place(n, q)
+        at = q * (side - 1) + j
+        return pltpu.make_async_remote_copy(
+            src, b1.at[blk, :, cols_of(q)], a_send.at[at], a_recv.at[at], device_id={'model': chip_at(a + sign, b) * 2 + core}, device_id_type=MESH)
+
+    def along_b(q, r, src, blk):
+        _, core, sign, a, b, chip_at = ring_place(n, q)
+        at = q * (rounds - side) + r
+        return pltpu.make_async_remote_copy(
+            src, b1.at[blk, :, cols_of(q)], b_send.at[at], b_recv.at[at], device_id={'model': chip_at(a, b + sign) * 2 + core}, device_id_type=MESH)
+
+    def across(q, r, src, blk):
+        at = q * rounds + r
+        return pltpu.make_async_remote_copy(
+            src, b1.at[blk, :, cols_of(q)], x_send.at[at], x_recv.at[at], device_id=peer, device_id_type=MESH)
+
+    def keep(q, blk):
+        cols = cols_of(q)
+        pltpu.make_async_copy(b1.at[blk, :, cols], b1_ref.at[blk, :, cols], out_sem).start()
+
+    def add_up(q, blk, value):
+        acc[blk] += mm(value, up_ref[cols_of(q), :], 1, 0)
+
+    def back_proj(t):
+        dy_copy(t).wait()
+        dg[t] = mm(dy_buf[lax.rem(t, 2)], down_ref[...], 1, 1).astype(BF16)
+
+        @pl.when(t + 2 < n)
+        def _():
+            dy_copy(t + 2).start()
+
+    def own_round(q, _):
+        cols = cols_of(q)
+        src = own_ref.at[:, cols]
+        along_a(q, 0, src, me).start()
+        along_b(q, 0, src, me).start()
+        across(q, 0, src, me).start()
+        return 0
+
+    lax.fori_loop(0, 4, own_round, 0)
+    acc[...] = jnp.zeros_like(acc)
+    b1[me] = own_ref[...]
+    acc[me] = mm(own_ref[...], up_ref[...], 1, 0)
+
+    def pass_on(t):
+        r, q = t // 4, lax.rem(t, 4)
+        s, j = r // side, lax.rem(r, side)
+        blk = place(q, r) * 2 + my_core
+        src = b1.at[blk, :, cols_of(q)]
+
+        @pl.when(s == 0)
+        def _():
+            along_a(q, j - 1, src, blk).wait_recv()
+
+            @pl.when(j < side - 1)
+            def _():
+                along_a(q, j, src, blk).start()
+
+        @pl.when(s > 0)
+        def _():
+            along_b(q, r - side, src, blk).wait_recv()
+
+        @pl.when(s < side - 1)
+        def _():
+            along_b(q, r, src, blk).start()
+
+        across(q, r, src, blk).start()
+        keep(q, blk)
+        add_up(q, blk, b1[blk, :, cols_of(q)])
+        return 0
+
+    def take_across(q, r):
+        blk = place(q, r) * 2 + 1 - my_core
+        across(q, r, b1.at[blk, :, cols_of(q)], blk).wait_recv()
+        keep(q, blk)
+        add_up(q, blk, b1[blk, :, cols_of(q)])
+
+    def main_round(t, _):
+        pass_on(t)
+        r, q = t // 4, lax.rem(t, 4)
+        take_across(q, r - 1)
+
+        @pl.when(lax.rem(t, 2) == 0)
+        def _():
+            back_proj(t // 2 - 2)
+
+        return 0
+
+    lax.fori_loop(4, 4 * rounds, main_round, 0)
+    back_proj(n - 2)
+    back_proj(n - 1)
+
+    def final_across(q, _):
+        take_across(q, rounds - 1)
+        keep(q, me)
+        return 0
+
+    lax.fori_loop(0, 4, final_across, 0)
+
+    def activate(t, _):
+        up = acc[t].astype(BF16).astype(F32)
+        value, slope = gelu_parts(up)
+        gelu_ref[t] = value.astype(BF16)
+        d_up_ref[t] = (dg[t].astype(F32) * slope).astype(BF16)
+        return 0
+
+    lax.fori_loop(0, n, activate, 0)
+
+    def drain(t, _):
+        q, r = t // rounds, lax.rem(t, rounds)
+        blk = place(q, r) * 2 + my_core
+        src = b1.at[blk, :, cols_of(q)]
+        across(q, r, src, blk).wait_send()
+
+        @pl.when(r < rounds - side)
+        def _():
+            along_b(q, r, src, blk).wait_send()
+
+        @pl.when(r < side - 1)
+        def _():
+            along_a(q, r, src, blk).wait_send()
+
+        return 0
+
+    lax.fori_loop(0, 4 * rounds, drain, 0)
+    pltpu.make_async_copy(b1, b1_ref, out_sem).wait()
+
+
+def gather_mlp(n, own, w_up, w_down, dy, collective_id):
+    tb, h = own.shape
+    f = w_up.shape[1]
+    side = math.isqrt(n // 2)
+    rounds = side * side
+    vmem = pl.BlockSpec(memory_space=pltpu.VMEM)
+    anyspace = pl.BlockSpec(memory_space=pl.ANY)
+    a_hops, b_hops, x_hops = 4 * (side - 1), 4 * (rounds - side), 4 * rounds
+    sems = [pltpu.SemaphoreType.DMA((k,)) for k in (a_hops, a_hops, b_hops, b_hops, x_hops, x_hops, 2)]
+    return pl.pallas_call(
+        functools.partial(gather_mlp_kernel, n),
+        out_shape=[
+            jax.ShapeDtypeStruct((n, tb, h), BF16), jax.ShapeDtypeStruct((n, tb, f), BF16), jax.ShapeDtypeStruct((n, tb, f), BF16),
+        ],
+        in_specs=[vmem, vmem, vmem, anyspace],
+        out_specs=[anyspace, vmem, vmem],
+        scratch_shapes=[
+            pltpu.VMEM((n, tb, h), BF16), pltpu.VMEM((n, tb, f), F32), pltpu.VMEM((n, tb, f), BF16), pltpu.VMEM((2, tb, h), BF16),
+            *sems, pltpu.SemaphoreType.DMA,
+        ],
+        compiler_params=pltpu.CompilerParams(collective_id=collective_id, has_side_effects=True, vmem_limit_bytes=50 * 1024 * 1024),
+        cost_estimate=pl.CostEstimate(flops=40_000_000_000, bytes_accessed=4 * n * tb * h, transcendentals=0),
+        name='gather_mlp',
+    )(own, w_up, w_down, dy.reshape(n, tb, h))
 
 
 def ln_rows(z, gain):
@@ -462,14 +649,10 @@
     return (rstd * (d_hat - mean_a - hat * mean_b)).astype(BF16), jnp.sum(d_wide * hat, axis=0)
 
 
-def gelu_tanh(up_proj):
-    return jax.nn.gelu(up_proj.astype(F32), approximate=True).astype(BF16)
-
-
 def solution(mesh):
     n = mesh.shape['model']
 
-    def local_step(x_in, seg_ids, gain_one, w_qkv, w_out, gain_two, w_up, w_down, d_y):
+    def layer(x_in, seg_ids, gain_one, w_qkv, w_out, gain_two, w_up, w_down, d_y):
         x = x_in[0]
         dy = d_y[0]
         seg = seg_ids[0]
@@ -489,22 +672,17 @@
 
         a_full, q, k, v, qkvt = ln_qkv(x, gain_one, w_qkv.T)
         ot, lse = attention_forward(k, qkvt, start_row, tab, bq, bk)
-        o_mine = exchange(n, ot, (n, hd, ts), column_block(ts), leading, 0, 'heads_to_tokens')
+        o_mine = exchange(n, ot, (n, hd, ts), column_block(ts), leading, 0)
 
         x_s = lax.dynamic_slice(x, (me * ts, 0), (ts, h))
         dy_s = lax.dynamic_slice(dy, (me * ts, 0), (ts, h))
         proj = mm(o_mine.reshape(inner, ts), wo_full, 0, 0)
         resid = (x_s.astype(F32) + proj).astype(BF16)
         b1_s, hat_two, rstd_two = ln_rows(resid, gain_two)
-        b1 = lax.all_gather(b1_s, 'model', axis=0, tiled=True)
-
-        d_gelu = mm(dy, w_down, 1, 1).astype(BF16)
-        up = mm(b1, w_up, 1, 0).astype(BF16)
-        gelu_out, gelu_pull = jax.vjp(gelu_tanh, up)
-        (d_up,) = gelu_pull(d_gelu)
-        d_b1 = matmul_reduce_scatter(n, d_up, w_up, 1, 3, 'reduce_d_b1')
+        b1, gelu_out, d_up = (z.reshape(t, z.shape[-1]) for z in gather_mlp(n, b1_s, w_up, w_down, dy, 6))
+        d_b1 = matmul_reduce_scatter(n, d_up, w_up, 1, 3)
         late_gelu, d_b1 = lax.optimization_barrier((gelu_out, d_b1))
-        part_two = matmul_reduce_scatter(n, late_gelu, w_down, 0, 4, 'reduce_y')
+        part_two = matmul_reduce_scatter(n, late_gelu, w_down, 0, 4)
         late_gelu, late_up, part_two = lax.optimization_barrier((late_gelu, d_up, part_two))
         d_w_down = mm(late_gelu, dy, 0, 0).astype(BF16)
         d_w_up = mm(b1, late_up, 0, 0).astype(BF16)
@@ -512,13 +690,13 @@
         d_ln, d_gain_two = ln_back(d_b1, hat_two, rstd_two, gain_two)
         d_resid_s = dy_s + d_ln
         d_heads = mm(wo_full, d_resid_s, 1, 1).astype(BF16).reshape(n, hd, ts)
-        dot = exchange(n, d_heads, (hd, t), leading, column_block(ts), 1, 'tokens_to_heads')
+        dot = exchange(n, d_heads, (hd, t), leading, column_block(ts), 1)
         d_resid = lax.all_gather(d_resid_s, 'model', axis=0, tiled=True)
 
         d_qkv = attention_backward(q, k, v, qkvt, ot, dot, lse, start_row, tab, bq, bk)
         y_s = (resid.astype(F32) + part_two.astype(F32)).astype(BF16)
         y_out = lax.all_gather(y_s[None], 'model', axis=1, tiled=True)
-        d_norm = matmul_reduce_scatter(n, d_qkv, w_qkv.T, 0, 5, 'reduce_d_x')
+        d_norm = matmul_reduce_scatter(n, d_qkv, w_qkv.T, 0, 5)
         d_w_qkv = mm(a_full, d_qkv, 0, 0).astype(BF16)
         d_w_out = mm(ot, d_resid, 1, 0).astype(BF16)
 
@@ -526,10 +704,10 @@
         d_ln, d_gain_one = ln_back(d_norm, hat_one, rstd_one, gain_one)
         d_x = lax.all_gather((d_resid_s + d_ln)[None], 'model', axis=1, tiled=True)
         gains = jnp.concatenate([d_gain_one, d_gain_two]).reshape(1, 2 * h)
-        gains = exchange(n, gains, (n, 1, 2 * h), whole_ref, leading, 2, 'gain_sums')
+        gains = exchange(n, gains, (n, 1, 2 * h), whole_ref, leading, 2)
         gains = jnp.sum(gains, axis=(0, 1)).astype(BF16)
         return (y_out, d_x, d_w_qkv, d_w_out.reshape(n_local, hd, h), d_w_up, d_w_down, gains[:h], gains[h:])
 
     in_specs = (P('data'), P('data'), P(), P(None, 'model'), P('model'), P(), P(None, 'model'), P('model'), P('data'))
     out_specs = (P('data'), P('data'), P('data', 'model'), P(('data', 'model')), P('data', 'model'), P(('data', 'model')), P('data'), P('data'))
-    return jax.shard_map(local_step, mesh=mesh, in_specs=in_specs, out_specs=out_specs, check_vma=False)
+    return jax.shard_map(layer, mesh=mesh, in_specs=in_specs, out_specs=out_specs, check_vma=False)

time: 647 us -> 624 us (0.964); the launches traced: 638 us -> 623 us
  Pallas kernels: 280 us -> 353 us
  waiting for transfers between devices: 224 us -> 161 us
  matrix products: 71.9 us -> 47.2 us
    pallas_call x0 -> x1, Pallas kernels: none -> 71.3 us  [gather_mlp(): pl.pallas_call(functools.partial(gather_mlp_kernel, n), out_shape=[jax.Sh...]
    all_gather x5 -> x4, waiting for transfers between devices: 222 us -> 159 us  [the longest x1 69 us: layer(): y_out = lax.all_gather(y_s[None], 'model', axis=1, tiled=True)]
    dot_general x8 -> x6, matrix products: 71.9 us -> 47.2 us  [mm(): lax.dot_general(a, b, (((ca,), (cb,)), ((), ())), preferred_element_type=...]
    unnamed x48 -> x46, local copies, waits for them, and re-layouts: 23.9 us -> 24.8 us
  transfers between devices with their start and end apart: 5 -> 4, of which waited for: 4 -> 3; matrix products, arithmetic and copies ran while one was open for 6% -> 6% of each run, Pallas kernels for 11% -> 12%
where the time goes in v3:
time: 624 us; the launch traced here: 623 us
  Pallas kernels  353 us (57%)
  waiting for transfers between devices  161 us (26%)
  matrix products  47.2 us (8%)
  local copies, waits for them, and re-layouts  29.2 us (5%)
  other arithmetic  18.1 us (3%)
  between operations  14.1 us (2%)
    pallas_call x3, Pallas kernels, matmul_reduce_scatter(): pl.pallas_call(functools.partial(reduce_kernel, n, r_dim), out_shape=jax....  170 us
    pallas_call x1, Pallas kernels, gather_mlp(): pl.pallas_call(functools.partial(gather_mlp_kernel, n), out_shape=[jax.Sh...  71.3 us
    all_gather x1, waiting for transfers between devices, layer(): y_out = lax.all_gather(y_s[None], 'model', axis=1, tiled=True)  69 us
    all_gather x1, waiting for transfers between devices, layer(): d_resid = lax.all_gather(d_resid_s, 'model', axis=0, tiled=True)  68.8 us
    pallas_call x3, Pallas kernels, exchange(): pl.pallas_call(functools.partial(exchange_kernel, n, src_of, dst_of), out...  55.1 us
    dot_general x6, matrix products, mm(): lax.dot_general(a, b, (((ca,), (cb,)), ((), ())), preferred_element_type=...  47.2 us
    unnamed x46, local copies, waits for them, and re-layouts  24.8 us
    all_gather x1, waiting for transfers between devices, layer(): d_x = lax.all_gather((d_resid_s + d_ln)[None], 'model', axis=1, tiled=True)  21.3 us
  transfers between devices with their start and end apart: 4, of which 3 were waited for; matrix products, arithmetic and copies ran while one was open for 6% of the time, Pallas kernels for 12%

profile of v3, /device:TPU:97, one launch (start us, length us, event | category | flops | bytes accessed | tf_op | source)
XLA Modules:
  0.0 622.9 jit_solution(12952467295815425160)
XLA Ops:
  8.0 1.3 reshape.414.g_ref
  9.3 1.3 convert_element_type.76
  11.8 1.5 add_select_fusion
  17.2 1.3 fusion.23
  19.2 20.7 %ln_qkv.1 = (bf16[4096,2048]{1,0:T(8,128)(2,1)}, bf16[4096,64]{1,0:T(8,128)(2,1)}, bf16[4096,64]{1,0:T(8,128)(2,1)}, bf16[4096,64]{1,0:T(8,128)(2,1)}, bf16[192,4096]{1,0:T(8,128)(2,1)}) custom-call(bf16[4096,2048]{1,0:T(8,128)(2,1)} %bitcast.118, bf16[1,2048]{1,0:T(2,128)(2,1)} %reshape.414.g_ref, bf16[192,2048]{1,0:T(8,128)(2,1)} %bitcast.109), custom_call_target="tpu_custom_call" | custom-call | flops 3388997632 | bytes 33554432 | tf_op jit(solution)/shard_map/ln_qkv/pallas_call | solution.py:47
  39.9 14.4 %attn_fwd.1 = (bf16[64,4096]{1,0:T(8,128)(2,1)}, f32[1,4096]{1,0:T(1,128)}) custom-call(s32[4,8]{1,0:T(4,128)} %pad_add_fusion.tab_ref, bf16[4096,64]{1,0:T(8,128)(2,1)} %get-tuple-element.23.k_ref, bf16[192,4096]{1,0:T(8,128)(2,1)} %get-tuple-element.24.qt_ref.vt_ref.t_ref, bf16[192,4096]{1,0:T(8,128)(2,1)} %get-tuple-element.24.qt_ref.vt_ref.t_ref, ...), custom_call_target="tpu_custom_call" | custom-call | flops 17179869184 | bytes 2097152 | tf_op jit(solution)/shard_map/attn_fwd/pallas_call | solution.py:123
  54.2 19.1 %shard_map.152 = bf16[32,64,128]{2,1,0:T(8,128)(2,1)} custom-call(bf16[64,4096]{1,0:T(8,128)(2,1)} %get-tuple-element.25.in_ref.ot_ref), custom_call_target="tpu_custom_call" | custom-call | flops 2000000000 | bytes 1048576 | tf_op jit(solution)/shard_map/pallas_call | solution.py:255
  73.9 4.9 fusion.36
  79.4 71.3 %gather_mlp.1 = (bf16[32,128,2048]{2,1,0:T(8,128)(2,1)}, bf16[32,128,256]{2,1,0:T(8,128)(2,1)}, bf16[32,128,256]{2,1,0:T(8,128)(2,1)}) custom-call(bf16[128,2048]{1,0:T(8,128)(2,1)S(1)} %multiply_convert_fusion.own_ref, bf16[2048,256]{1,0:T(8,128)(2,1)S(1)} %copy-done.2, bf16[256,2048]{1,0:T(8,128)(2,1)S(1)} %copy-done.3, bf16[32,128,2048]{2,1,0:T(8,128)(2,1)} %bitcast.115), custom_call_target="tpu_custom_call" | custom-call | flops 40000000000 | bytes 33554432 | tf_op jit(solution)/shard_map/gather_mlp/pallas_call | solution.py:618
  150.6 1.6 copy-done.5
  152.2 56.6 %shard_map.153 = bf16[128,2048]{1,0:T(8,128)(2,1)S(1)} custom-call(bf16[16,2,128,256]{3,2,1,0:T(8,128)(2,1)S(1)} %bitcast.111, bf16[2048,256]{1,0:T(8,128)(2,1)S(1)} %copy-done.2), custom_call_target="tpu_custom_call" | custom-call | flops 40000000000 | bytes 4194304 | tf_op jit(solution)/shard_map/pallas_call | solution.py:427
  208.8 57.8 %shard_map.154 = bf16[128,2048]{1,0:T(8,128)(2,1)S(1)} custom-call(bf16[16,2,128,256]{3,2,1,0:T(8,128)(2,1)S(1)} %bitcast.107, bf16[256,2048]{1,0:T(8,128)(2,1)S(1)} %copy-done.4), custom_call_target="tpu_custom_call" | custom-call | flops 40000000000 | bytes 4194304 | tf_op jit(solution)/shard_map/pallas_call | solution.py:427
  266.7 1.3 fusion.28
  267.9 1.5 fusion.31
  269.5 6.5 %fusion.8 = bf16[2048,128]{0,1:T(8,128)(2,1)S(1)} fusion(bf16[128,2048]{1,0:T(8,128)(2,1)S(1)} %fusion.31, bf16[2048,2048]{1,0:T(8,128)(2,1)} %bitcast.114), kind=kOutput, calls=%fused_computation.10 | convolution fusion | flops 1074003968 | bytes 9437184 | tf_op jit(solution)/shard_map/dot_general | solution.py:22
  277.0 16.4 %shard_map.155.dot_ref = bf16[64,4096]{1,0:T(8,128)(2,1)} custom-call(bf16[32,64,128]{2,1,0:T(8,128)(2,1)} %bitcast.123), custom_call_target="tpu_custom_call" | custom-call | flops 2000000000 | bytes 1048576 | tf_op jit(solution)/shard_map/pallas_call | solution.py:255
  293.3 21.3 %attn_bwd.1 = bf16[4096,192]{1,0:T(8,128)(2,1)} custom-call(s32[4,8]{1,0:T(4,128)} %pad_add_fusion.tab_ref, bf16[4096,64]{1,0:T(8,128)(2,1)} %get-tuple-element.31.q_ref, bf16[4096,64]{1,0:T(8,128)(2,1)} %get-tuple-element.23.k_ref, bf16[4096,64]{1,0:T(8,128)(2,1)} %get-tuple-element.32.v_ref, bf16[192,4096]{1,0:T(8,128)(2,1)} %get-tuple-element.24.qt_ref.vt_ref.t_ref, ...), custom_call_target="tpu_custom_call" | custom-call | flops 42949672960 | bytes 4194304 | tf_op jit(solution)/shard_map/attn_bwd/pallas_call | solution.py:199
  314.7 1.6 copy-done.7
  316.3 55.9 %shard_map.156 = bf16[128,2048]{1,0:T(8,128)(2,1)S(1)} custom-call(bf16[16,2,128,192]{3,2,1,0:T(8,128)(2,1)S(1)} %bitcast.113, bf16[192,2048]{1,0:T(8,128)(2,1)S(1)} %bitcast.110), custom_call_target="tpu_custom_call" | custom-call | flops 40000000000 | bytes 3145728 | tf_op jit(solution)/shard_map/pallas_call | solution.py:427
  372.2 1.5 fusion.30
  373.7 2.4 fusion.32
  378.2 19.6 %shard_map.157 = f32[32,1,4096]{2,1,0:T(1,128)} custom-call(f32[1,4096]{1,0:T(1,128)} %bitcast.128), custom_call_target="tpu_custom_call" | custom-call | flops 2000000000 | bytes 16384 | tf_op jit(solution)/shard_map/pallas_call | solution.py:255
  397.8 1.4 reduce_sum.109
  399.8 10.8 %convolution_convert_fusion.1 = bf16[2048,192]{0,1:T(8,128)(2,1)} fusion(bf16[4096,2048]{1,0:T(8,128)(2,1)} %get-tuple-element.34, bf16[4096,192]{1,0:T(8,128)(2,1)} %attn_bwd.1), kind=kOutput, calls=%fused_computation.4 | convolution fusion | flops 3221618688 | bytes 19136512 | tf_op jit(solution)/shard_map/dot_general | solution.py:22
  410.7 9.8 %convolution_convert_fusion = bf16[2048,256]{1,0:T(8,128)(2,1)} fusion(bf16[4096,2048]{1,0:T(8,128)(2,1)} %bitcast.129, bf16[4096,256]{1,0:T(8,128)(2,1)S(1)} %bitcast.112), kind=kOutput, calls=%fused_computation.3 | convolution fusion | flops 4295491584 | bytes 19922944 | tf_op jit(solution)/shard_map/dot_general | solution.py:22
  420.6 5.5 fusion.2
  426.0 21.3 %all-gather.13.cloned.1.call-done = bf16[4096,2048]{1,0:T(8,128)(2,1)} async-done(((bf16[128,2048]{1,0:T(8,128)(2,1)}), bf16[4096,2048]{1,0:T(8,128)(2,1)}) %all-gather.13.cloned.1.call-update) | async-done | bytes 16777232 | tf_op jit(solution)/shard_map/all_gather | solution.py:705
  447.4 69.0 %all-gather.11.cloned.1.call-done = bf16[4096,2048]{1,0:T(8,128)(2,1)} async-done(((bf16[128,2048]{1,0:T(8,128)(2,1)}), bf16[4096,2048]{1,0:T(8,128)(2,1)}) %all-gather.11.cloned.1.call-update) | async-done | bytes 16777232 | tf_op jit(solution)/shard_map/all_gather | solution.py:698
  516.4 68.8 %all-gather.9.cloned.1.call-done = bf16[4096,2048]{1,0:T(8,128)(2,1)} async-done(((bf16[128,2048]{1,0:T(8,128)(2,1)}), bf16[4096,2048]{1,0:T(8,128)(2,1)}) %all-gather.9.cloned.1.call-update) | async-done | bytes 16777232 | tf_op jit(solution)/shard_map/all_gather | solution.py:694
  585.2 9.6 %fusion.9 = bf16[1,64,2048]{2,1,0:T(8,128)(2,1)} fusion(bf16[64,4096]{1,0:T(8,128)(2,1)S(1)} %copy-done.9, bf16[4096,2048]{1,0:T(8,128)(2,1)} %all-gather.9.cloned.1.call-done), kind=kOutput, calls=%fused_computation.12 | convolution fusion | flops 1073872896 | bytes 17563648 | tf_op jit(solution)/shard_map/dot_general | solution.py:22
  594.9 15.3 %copy.38 = bf16[1,4096,2048]{2,1,0:T(8,128)(2,1)} copy(bf16[1,4096,2048]{2,1,0:T(8,128)(2,1)} %bitcast.122) | data formatting | bytes 33554432
  610.2 6.2 copy.39
  (82 shorter events, 11.3 us)
Async XLA Ops:
  7.2 66.7 %all-gather.7.cloned.1.call-start = ((), (), s32[]{:S(2)}) async-start(), calls=%async_computation | async-start | bytes 8650752 | tf_op jit(solution)/shard_map/all_gather | solution.py:667
  8.0 439.4 %all-gather.13.cloned.1.call-start = ((), (), s32[]{:S(2)}) async-start(), calls=%async_computation.3 | async-start | bytes 17301504 | tf_op jit(solution)/shard_map/all_gather | solution.py:705
  17.2 22.7 %copy-start.11 = (f32[128]{0:T(128)}, f32[128]{0:T(128)S(1)}, u32[]{:S(2)}) copy-start(f32[128]{0:T(128)S(1)} %broadcast_multiply_fusion.2) | copy-start | bytes 1540
  54.2 25.1 %copy-start.2 = (bf16[2048,256]{1,0:T(8,128)(2,1)S(1)}, bf16[2048,256]{1,0:T(8,128)(2,1)}, u32[]{:S(2)}) copy-start(bf16[2048,256]{1,0:T(8,128)(2,1)} %r_ref.2) | copy-start | bytes 3145732
  54.2 25.1 %copy-start.3 = (bf16[256,2048]{1,0:T(8,128)(2,1)S(1)}, bf16[256,2048]{1,0:T(8,128)(2,1)}, u32[]{:S(2)}) copy-start(bf16[256,2048]{1,0:T(8,128)(2,1)} %r_ref.3) | copy-start | bytes 3145732
  150.6 1.6 copy-start.5
  152.2 56.6 %copy-start = (bf16[32,128,256]{2,1,0:T(8,128)(2,1)S(1)}, bf16[32,128,256]{2,1,0:T(8,128)(2,1)}, u32[]{:S(2)}) copy-start(bf16[32,128,256]{2,1,0:T(8,128)(2,1)} %get-tuple-element.26) | copy-start | bytes 6291460
  152.2 56.6 %copy-start.4 = (bf16[256,2048]{1,0:T(8,128)(2,1)S(1)}, bf16[256,2048]{1,0:T(8,128)(2,1)}, u32[]{:S(2)}) copy-start(bf16[256,2048]{1,0:T(8,128)(2,1)} %r_ref.3) | copy-start | bytes 3145732
  269.5 104.2 %copy-start.8 = (bf16[128,2048]{1,0:T(8,128)(2,1)}, bf16[128,2048]{1,0:T(8,128)(2,1)S(1)}, u32[]{:S(2)}) copy-start(bf16[128,2048]{1,0:T(8,128)(2,1)S(1)} %fusion.31) | copy-start | bytes 1572868
  293.3 21.3 %copy-start.1 = (bf16[2048,192]{0,1:T(8,128)(2,1)S(1)}, bf16[2048,192]{0,1:T(8,128)(2,1)}, u32[]{:S(2)}) copy-start(bf16[2048,192]{0,1:T(8,128)(2,1)} %param.12) | copy-start | bytes 2359300
  314.7 1.6 copy-start.7
  316.3 55.9 %copy-start.10 = (f32[2048]{0:T(1024)S(1)}, f32[2048]{0:T(1024)}, u32[]{:S(2)}) copy-start(f32[2048]{0:T(1024)} %convert_element_type.76) | copy-start | bytes 24580
  316.3 55.9 %copy-start.12 = (f32[128]{0:T(128)S(1)}, f32[128]{0:T(128)}, u32[]{:S(2)}) copy-start(f32[128]{0:T(128)} %copy-done.11) | copy-start | bytes 1540
  316.3 55.9 %copy-start.13 = (f32[128]{0:T(128)S(1)}, f32[128]{0:T(128)}, u32[]{:S(2)}) copy-start(f32[128]{0:T(128)} %add_rsqrt_fusion) | copy-start | bytes 1540
  376.2 140.2 %all-gather.11.cloned.1.call-start = ((), (), s32[]{:S(2)}) async-start(), calls=%async_computation.2 | async-start | bytes 17301504 | tf_op jit(solution)/shard_map/all_gather | solution.py:698
  377.0 208.2 %all-gather.9.cloned.1.call-start = ((), (), s32[]{:S(2)}) async-start(), calls=%async_computation.1 | async-start | bytes 17301504 | tf_op jit(solution)/shard_map/all_gather | solution.py:694
  399.2 11.5 %copy-start.6 = (bf16[32,128,256]{2,1,0:T(8,128)(2,1)S(1)}, bf16[32,128,256]{2,1,0:T(8,128)(2,1)}, u32[]{:S(2)}) copy-start(bf16[32,128,256]{2,1,0:T(8,128)(2,1)} %get-tuple-element.27) | copy-start | bytes 6291460
  399.8 20.7 %slice-start = ((s8[16777216]{0:T(1024)(128)(4,1)}), s8[4194304]{0:T(1024)(128)(4,1)S(1)}, s32[]{:S(2)}) async-start(s8[16777216]{0:T(1024)(128)(4,1)} %bitcast.116), calls=%async_computation.4 | async-start | bytes 8388608
  399.8 20.7 %slice-start.1 = ((s8[16777216]{0:T(1024)(128)(4,1)}), s8[4194304]{0:T(1024)(128)(4,1)S(1)}, s32[]{:S(2)}) async-start(s8[16777216]{0:T(1024)(128)(4,1)} %bitcast.116), calls=%async_computation.5 | async-start | bytes 8388608
  410.7 9.8 %slice-start.2 = ((s8[16777216]{0:T(1024)(128)(4,1)}), s8[4194304]{0:T(1024)(128)(4,1)S(1)}, s32[]{:S(2)}) async-start(s8[16777216]{0:T(1024)(128)(4,1)} %bitcast.116), calls=%async_computation.6 | async-start | bytes 8388608
  410.7 9.8 %slice-start.3 = ((s8[16777216]{0:T(1024)(128)(4,1)}), s8[4194304]{0:T(1024)(128)(4,1)S(1)}, s32[]{:S(2)}) async-start(s8[16777216]{0:T(1024)(128)(4,1)} %bitcast.116), calls=%async_computation.7 | async-start | bytes 8388608
  420.5 164.7 %copy-start.9 = (bf16[64,4096]{1,0:T(8,128)(2,1)S(1)}, bf16[64,4096]{1,0:T(8,128)(2,1)}, u32[]{:S(2)}) copy-start(bf16[64,4096]{1,0:T(8,128)(2,1)} %get-tuple-element.25.in_ref.ot_ref) | copy-start | bytes 1572868
  585.2 25.0 %slice-start.4 = ((s8[16777216]{0:T(1024)(128)(4,1)}), s8[4194304]{0:T(1024)(128)(4,1)S(1)}, s32[]{:S(2)}) async-start(s8[16777216]{0:T(1024)(128)(4,1)} %bitcast.119), calls=%async_computation.8 | async-start | bytes 8388608
  585.2 25.0 %slice-start.5 = ((s8[16777216]{0:T(1024)(128)(4,1)}), s8[4194304]{0:T(1024)(128)(4,1)S(1)}, s32[]{:S(2)}) async-start(s8[16777216]{0:T(1024)(128)(4,1)} %bitcast.119), calls=%async_computation.9 | async-start | bytes 8388608
  594.8 15.4 %slice-start.6 = ((s8[16777216]{0:T(1024)(128)(4,1)}), s8[4194304]{0:T(1024)(128)(4,1)S(1)}, s32[]{:S(2)}) async-start(s8[16777216]{0:T(1024)(128)(4,1)} %bitcast.119), calls=%async_computation.10 | async-start | bytes 8388608
  594.9 15.4 %slice-start.7 = ((s8[16777216]{0:T(1024)(128)(4,1)}), s8[4194304]{0:T(1024)(128)(4,1)S(1)}, s32[]{:S(2)}) async-start(s8[16777216]{0:T(1024)(128)(4,1)} %bitcast.119), calls=%async_computation.11 | async-start | bytes 8388608
Sparse Core Ops, SparseCore 0:
  10.1 51.9 all-gather.6
  376.3 70.9 all-gather.12
  449.4 66.8 all-gather.10
  518.3 66.8 all-gather.8

commit v4 on v3

--- a/solution.py
+++ b/solution.py
@@ -62,6 +62,10 @@
     return (k_pos <= q_pos) & (k_pos >= start)
 
 
+def masked_block(t, lo, mid, hi):
+    return jnp.where(t < mid - lo, lo + t, hi + t - (mid - lo))
+
+
 def attn_fwd_kernel(bk, tab_ref, k_ref, qt_ref, vt_ref, start_ref, ot_ref, lse_ref):
     i = pl.program_id(0)
     bq = qt_ref.shape[1]
@@ -85,9 +89,8 @@
         return m_new, l, acc
 
     carry = (jnp.full((1, bq), NEG, F32), jnp.zeros((1, bq), F32), jnp.zeros((hd, bq), F32))
-    carry = lax.fori_loop(lo, mid, functools.partial(step, True), carry)
     carry = lax.fori_loop(mid, hi, functools.partial(step, False), carry)
-    m, l, acc = lax.fori_loop(hi, top, functools.partial(step, True), carry)
+    m, l, acc = lax.fori_loop(0, mid - lo + top - hi, lambda t, c: step(True, masked_block(t, lo, mid, hi), c), carry)
     ot_ref[...] = (acc / l).astype(BF16)
     lse_ref[...] = m * scale + jnp.log2(l)
 
@@ -176,9 +179,8 @@
         return dqt + mm(t_ref[hd:2 * hd, rows], ds, 1, 0)
 
     dqt = jnp.zeros((hd, bq), F32)
-    dqt = lax.fori_loop(lo, mid, functools.partial(step, True), dqt)
     dqt = lax.fori_loop(mid, hi, functools.partial(step, False), dqt)
-    dqt = lax.fori_loop(hi, top, functools.partial(step, True), dqt)
+    dqt = lax.fori_loop(0, mid - lo + top - hi, lambda t, c: step(True, masked_block(t, lo, mid, hi), c), dqt)
     d_ref[pl.ds(c0, bq), :hd] = (dqt * hd ** -0.5).T.astype(BF16)
 
     @pl.when(i == pl.num_programs(0) - 1)
@@ -310,25 +312,32 @@
     pl.semaphore_wait(barrier, 5)
 
 
-def reduce_kernel(n, r_dim, l_ref, r_ref, out_ref, l_peer, r_peer, first, slot1, slot2, s_send, s_recv, p_send, p_recv, x_send, x_recv):
+def reduce_kernel(n, r_dim, l_ref, r_ref, out_ref, l_peer, r_peer, part, first, slot1, slot2, s_send, s_recv, p_send, p_recv, x_send, x_recv):
     me = lax.axis_index('model')
     my_core = lax.rem(me, 2)
-    chips, _, _, _ = l_ref.shape
+    side, _, _, tb, k = l_ref.shape
     width = out_ref.shape[1] // 4
-    side = math.isqrt(chips)
     greet_neighbours(n)
     peer = {'model': me + 1 - 2 * my_core}
     swap = [
         pltpu.make_async_remote_copy(src, dst, x_send.at[i], x_recv.at[i], device_id=peer, device_id_type=MESH)
-        for i, (src, dst) in enumerate([(r_ref, r_peer), (l_ref.at[:, 1 - my_core], l_peer)])
+        for i, (src, dst) in enumerate([(r_ref, r_peer), (l_ref.at[:, :, 1 - my_core], l_peer)])
     ]
     for copy in swap:
         copy.start()
 
-    def partial(q, chip):
-        cols = pl.ds(pl.multiple_of(q * width, width), width)
-        mine, other = (r_ref[:, cols], r_peer[:, cols]) if r_dim == 0 else (r_ref[cols, :], r_peer[cols, :])
-        return mm(l_ref[chip, my_core], mine, 1, r_dim) + mm(l_peer[chip], other, 1, r_dim)
+    def group(s, q):
+        _, _, sign, a, _, _ = ring_place(n, q)
+        at = lax.rem(a - sign * (1 + s) + 2 * side, side)
+        mine, other = (l_ref[:, at, my_core], l_peer[:, at]) if q < 2 else (l_ref[at, :, my_core], l_peer[at])
+        cols = pl.ds(q * width, width)
+        r_mine, r_other = (r_ref[:, cols], r_peer[:, cols]) if r_dim == 0 else (r_ref[cols, :], r_peer[cols, :])
+        total = mm(mine.reshape(side * tb, k), r_mine, 1, r_dim) + mm(other.reshape(side * tb, k), r_other, 1, r_dim)
+        part[lax.rem(s, 2), q] = total.reshape(side, tb, width)
+
+    def own_part(q, s, j):
+        _, _, sign, _, b, _ = ring_place(n, q)
+        return part[lax.rem(s, 2), q, lax.rem(b - sign * (1 + j) + 2 * side, side)]
 
     def hop(q, s, j, src):
         _, core, sign, a, b, chip_at = ring_place(n, q)
@@ -348,35 +357,44 @@
     for copy in swap:
         copy.wait()
 
-    def start_round(t, _):
-        j, q = t // 4, lax.rem(t, 4)
-        _, _, sign, a, b, chip_at = ring_place(n, q)
-        at = q * side + j
-        first[at] = partial(q, chip_at(a - sign, b - sign * (1 + j))).astype(BF16)
-        hop(q, 0, j, first.at[at]).start()
-        return 0
-
-    lax.fori_loop(0, 4 * side, start_round, 0)
+    def start_step(s, _):
+        for q in range(4):
+            group(s, q)
+
+            @pl.when(s == 0)
+            def _():
+                def start_round(j, _):
+                    at = q * side + j
+                    first[at] = own_part(q, 0, j).astype(BF16)
+                    hop(q, 0, j, first.at[at]).start()
+                    return 0
+
+                lax.fori_loop(0, side, start_round, 0)
+
+        return 0
+
+    lax.fori_loop(0, 2, start_step, 0)
 
     def middle_round(t, _):
         s, rest = 1 + t // (4 * side), lax.rem(t, 4 * side)
         j, q = rest // 4, lax.rem(rest, 4)
-        _, _, sign, a, b, chip_at = ring_place(n, q)
         at = arrived(q, s - 1, j)
-        own = partial(q, chip_at(a - sign * (1 + s), b - sign * (1 + j)))
         hop(q, s - 1, j, slot1.at[at]).wait_recv()
-        slot1[at] = (slot1[at].astype(F32) + own).astype(BF16)
+        slot1[at] = (slot1[at].astype(F32) + own_part(q, s, j)).astype(BF16)
         hop(q, s, j, slot1.at[at]).start()
+        for ahead in range(4):
+            @pl.when((q == 3) & (j == ahead))
+            def _():
+                group(s + 1, ahead)
+
         return 0
 
     lax.fori_loop(0, 4 * side * (side - 2), middle_round, 0)
 
     def last_sum(q, j):
-        _, _, sign, a, b, chip_at = ring_place(n, q)
         at = arrived(q, side - 2, j)
-        own = partial(q, chip_at(a, b - sign * (1 + j)))
         hop(q, side - 2, j, slot1.at[at]).wait_recv()
-        return at, slot1[at].astype(F32) + own
+        return at, slot1[at].astype(F32) + own_part(q, side - 1, j)
 
     def turn_first(q, _):
         at, total = last_sum(q, 0)
@@ -430,8 +448,9 @@
         in_specs=[vmem, vmem],
         out_specs=vmem,
         scratch_shapes=[
-            pltpu.VMEM((chips, tb, k), BF16),
+            pltpu.VMEM((side, side, tb, k), BF16),
             pltpu.VMEM(right.shape, BF16),
+            pltpu.VMEM((2, 4, side, tb, f // 4), F32),
             pltpu.VMEM((4 * side, tb, f // 4), BF16),
             pltpu.VMEM((hops * side, tb, f // 4), BF16),
             pltpu.VMEM((hops, tb, f // 4), BF16),
@@ -439,9 +458,9 @@
             pltpu.SemaphoreType.DMA((hops,)), pltpu.SemaphoreType.DMA((hops,)),
             pltpu.SemaphoreType.DMA((2,)), pltpu.SemaphoreType.DMA((2,)),
         ],
-        compiler_params=pltpu.CompilerParams(collective_id=collective_id, has_side_effects=True, vmem_limit_bytes=40 * 1024 * 1024),
+        compiler_params=pltpu.CompilerParams(collective_id=collective_id, has_side_effects=True, vmem_limit_bytes=48 * 1024 * 1024),
         cost_estimate=pl.CostEstimate(flops=40_000_000_000, bytes_accessed=4 * t * k, transcendentals=0),
-    )(left.reshape(chips, 2, tb, k), right)
+    )(left.reshape(side, side, 2, tb, k), right)
 
 
 def gelu_parts(up):
@@ -457,148 +476,148 @@
                       b1, acc, dg, dy_buf, a_send, a_recv, b_send, b_recv, x_send, x_recv, dy_sem, out_sem):
     me = lax.axis_index('model')
     my_core = lax.rem(me, 2)
-    _, h = own_ref.shape
+    tb, h = own_ref.shape
+    f = up_ref.shape[1]
     width = h // 4
     side = math.isqrt(n // 2)
     rounds = side * side
+    n_dy, _, _ = dy_ref.shape
     peer = {'model': me + 1 - 2 * my_core}
 
     def dy_copy(t):
         return pltpu.make_async_copy(dy_ref.at[t], dy_buf.at[lax.rem(t, 2)], dy_sem.at[lax.rem(t, 2)])
 
-    dy_copy(0).start()
-    dy_copy(1).start()
+    dy_copy(jnp.int32(0)).start()
+    dy_copy(jnp.int32(1)).start()
     greet_neighbours(n)
 
     def cols_of(q):
         return pl.ds(pl.multiple_of(q * width, width), width)
 
-    def place(q, r):
+    def quarter(q, r, core):
         _, _, sign, a, b, chip_at = ring_place(n, q)
-        return chip_at(a - sign * lax.rem(r, side), b - sign * (r // side))
-
-    def along_a(q, j, src, blk):
+        chip = chip_at(a - sign * lax.rem(r, side), b - sign * (r // side))
+        return b1.at[chip // side, lax.rem(chip, side), core, :, cols_of(q)]
+
+    def along_a(q, j, src):
         _, core, sign, a, b, chip_at = ring_place(n, q)
         at = q * (side - 1) + j
         return pltpu.make_async_remote_copy(
-            src, b1.at[blk, :, cols_of(q)], a_send.at[at], a_recv.at[at], device_id={'model': chip_at(a + sign, b) * 2 + core}, device_id_type=MESH)
-
-    def along_b(q, r, src, blk):
+            src, quarter(q, j, core), a_send.at[at], a_recv.at[at], device_id={'model': chip_at(a + sign, b) * 2 + core}, device_id_type=MESH)
+
+    def along_b(q, r, src):
         _, core, sign, a, b, chip_at = ring_place(n, q)
         at = q * (rounds - side) + r
         return pltpu.make_async_remote_copy(
-            src, b1.at[blk, :, cols_of(q)], b_send.at[at], b_recv.at[at], device_id={'model': chip_at(a, b + sign) * 2 + core}, device_id_type=MESH)
-
-    def across(q, r, src, blk):
+            src, quarter(q, r, core), b_send.at[at], b_recv.at[at], device_id={'model': chip_at(a, b + sign) * 2 + core}, device_id_type=MESH)
+
+    def across(q, r, src, core):
         at = q * rounds + r
         return pltpu.make_async_remote_copy(
-            src, b1.at[blk, :, cols_of(q)], x_send.at[at], x_recv.at[at], device_id=peer, device_id_type=MESH)
-
-    def keep(q, blk):
-        cols = cols_of(q)
-        pltpu.make_async_copy(b1.at[blk, :, cols], b1_ref.at[blk, :, cols], out_sem).start()
-
-    def add_up(q, blk, value):
-        acc[blk] += mm(value, up_ref[cols_of(q), :], 1, 0)
+            src, quarter(q, r, core), x_send.at[at], x_recv.at[at], device_id=peer, device_id_type=MESH)
 
     def back_proj(t):
         dy_copy(t).wait()
         dg[t] = mm(dy_buf[lax.rem(t, 2)], down_ref[...], 1, 1).astype(BF16)
 
-        @pl.when(t + 2 < n)
+        @pl.when(t + 2 < n_dy)
         def _():
             dy_copy(t + 2).start()
 
     def own_round(q, _):
-        cols = cols_of(q)
-        src = own_ref.at[:, cols]
-        along_a(q, 0, src, me).start()
-        along_b(q, 0, src, me).start()
-        across(q, 0, src, me).start()
+        src = own_ref.at[:, cols_of(q)]
+        along_a(q, 0, src).start()
+        along_b(q, 0, src).start()
+        across(q, 0, src, my_core).start()
         return 0
 
     lax.fori_loop(0, 4, own_round, 0)
+    b1[me // (2 * side), lax.rem(me // 2, side), my_core] = own_ref[...]
     acc[...] = jnp.zeros_like(acc)
-    b1[me] = own_ref[...]
-    acc[me] = mm(own_ref[...], up_ref[...], 1, 0)
-
-    def pass_on(t):
+
+    def add_up(s, q, core):
+        _, _, sign, _, b, _ = ring_place(n, q)
+        at = lax.rem(b - sign * s + 2 * side, side)
+        cols = pl.ds(q * width, width)
+        if q < 2:
+            pltpu.make_async_copy(b1.at[at, :, core, :, cols], b1_ref.at[at, :, core, :, cols], out_sem).start()
+            value = b1[at, :, core, :, cols].reshape(side * tb, width)
+        else:
+            pltpu.make_async_copy(b1.at[:, at, core, :, cols], b1_ref.at[:, at, core, :, cols], out_sem).start()
+            value = b1[:, at, core, :, cols].reshape(side * tb, width)
+        more = mm(value, up_ref[cols, :], 1, 0).reshape(side, tb, f)
+        if q < 2:
+            acc[at, :, core] += more
+        else:
+            acc[:, at, core] += more
+
+    def take_step(s, q):
+        add_up(s, q, my_core)
+        for j in range(side):
+            r = s * side + j
+            across(q, r, quarter(q, r, 1 - my_core), 1 - my_core).wait_recv()
+        add_up(s, q, 1 - my_core)
+
+    def main_round(t, _):
         r, q = t // 4, lax.rem(t, 4)
         s, j = r // side, lax.rem(r, side)
-        blk = place(q, r) * 2 + my_core
-        src = b1.at[blk, :, cols_of(q)]
+        src = quarter(q, r, my_core)
 
         @pl.when(s == 0)
         def _():
-            along_a(q, j - 1, src, blk).wait_recv()
+            along_a(q, j - 1, src).wait_recv()
 
             @pl.when(j < side - 1)
             def _():
-                along_a(q, j, src, blk).start()
+                along_a(q, j, src).start()
 
         @pl.when(s > 0)
         def _():
-            along_b(q, r - side, src, blk).wait_recv()
+            along_b(q, r - side, src).wait_recv()
 
         @pl.when(s < side - 1)
         def _():
-            along_b(q, r, src, blk).start()
-
-        across(q, r, src, blk).start()
-        keep(q, blk)
-        add_up(q, blk, b1[blk, :, cols_of(q)])
-        return 0
-
-    def take_across(q, r):
-        blk = place(q, r) * 2 + 1 - my_core
-        across(q, r, b1.at[blk, :, cols_of(q)], blk).wait_recv()
-        keep(q, blk)
-        add_up(q, blk, b1[blk, :, cols_of(q)])
-
-    def main_round(t, _):
-        pass_on(t)
-        r, q = t // 4, lax.rem(t, 4)
-        take_across(q, r - 1)
-
-        @pl.when(lax.rem(t, 2) == 0)
+            along_b(q, r, src).start()
+
+        across(q, r, src, my_core).start()
+        for late in range(4):
+            @pl.when((q == 3) & (j == late) & (s > 0))
+            def _():
+                take_step(s - 1, late)
+
+        @pl.when((q == 1) & (lax.rem(r, 2) == 1))
         def _():
-            back_proj(t // 2 - 2)
+            back_proj(r // 2)
 
         return 0
 
     lax.fori_loop(4, 4 * rounds, main_round, 0)
-    back_proj(n - 2)
-    back_proj(n - 1)
-
-    def final_across(q, _):
-        take_across(q, rounds - 1)
-        keep(q, me)
-        return 0
-
-    lax.fori_loop(0, 4, final_across, 0)
+    for q in range(4):
+        take_step(jnp.int32(side - 1), q)
 
     def activate(t, _):
-        up = acc[t].astype(BF16).astype(F32)
+        chip, core = t // 2, lax.rem(t, 2)
+        piece, rows = t // 4, pl.ds(pl.multiple_of(lax.rem(t, 4) * tb, tb), tb)
+        up = acc[chip // side, lax.rem(chip, side), core].astype(BF16).astype(F32)
         value, slope = gelu_parts(up)
-        gelu_ref[t] = value.astype(BF16)
-        d_up_ref[t] = (dg[t].astype(F32) * slope).astype(BF16)
+        gelu_ref[piece, rows, :] = value.astype(BF16)
+        d_up_ref[piece, rows, :] = (dg[piece, rows, :].astype(F32) * slope).astype(BF16)
         return 0
 
     lax.fori_loop(0, n, activate, 0)
 
     def drain(t, _):
         q, r = t // rounds, lax.rem(t, rounds)
-        blk = place(q, r) * 2 + my_core
-        src = b1.at[blk, :, cols_of(q)]
-        across(q, r, src, blk).wait_send()
+        src = quarter(q, r, my_core)
+        across(q, r, src, my_core).wait_send()
 
         @pl.when(r < rounds - side)
         def _():
-            along_b(q, r, src, blk).wait_send()
+            along_b(q, r, src).wait_send()
 
         @pl.when(r < side - 1)
         def _():
-            along_a(q, r, src, blk).wait_send()
+            along_a(q, r, src).wait_send()
 
         return 0
 
@@ -618,18 +637,33 @@
     return pl.pallas_call(
         functools.partial(gather_mlp_kernel, n),
         out_shape=[
-            jax.ShapeDtypeStruct((n, tb, h), BF16), jax.ShapeDtypeStruct((n, tb, f), BF16), jax.ShapeDtypeStruct((n, tb, f), BF16),
+            jax.ShapeDtypeStruct((side, side, 2, tb, h), BF16), jax.ShapeDtypeStruct((n // 4, 4 * tb, f), BF16), jax.ShapeDtypeStruct((n // 4, 4 * tb, f), BF16),
         ],
         in_specs=[vmem, vmem, vmem, anyspace],
         out_specs=[anyspace, vmem, vmem],
         scratch_shapes=[
-            pltpu.VMEM((n, tb, h), BF16), pltpu.VMEM((n, tb, f), F32), pltpu.VMEM((n, tb, f), BF16), pltpu.VMEM((2, tb, h), BF16),
+            pltpu.VMEM((side, side, 2, tb, h), BF16), pltpu.VMEM((side, side, 2, tb, f), F32),
+            pltpu.VMEM((n // 4, 4 * tb, f), BF16), pltpu.VMEM((2, 4 * tb, h), BF16),
             *sems, pltpu.SemaphoreType.DMA,
         ],
         compiler_params=pltpu.CompilerParams(collective_id=collective_id, has_side_effects=True, vmem_limit_bytes=50 * 1024 * 1024),
         cost_estimate=pl.CostEstimate(flops=40_000_000_000, bytes_accessed=4 * n * tb * h, transcendentals=0),
         name='gather_mlp',
-    )(own, w_up, w_down, dy.reshape(n, tb, h))
+    )(own, w_up, w_down, dy.reshape(n // 4, 4 * tb, h))
+
+
+def copy_kernel(src_ref, dst_ref):
+    dst_ref[...] = src_ref[...]
+
+
+def copy_rows(value):
+    t, h = value.shape
+    bt = min(512, t)
+    row = pl.BlockSpec((bt, h), lambda i: (i, 0))
+    return pl.pallas_call(
+        copy_kernel, grid=(t // bt,), in_specs=[row], out_specs=row, out_shape=jax.ShapeDtypeStruct((t, h), value.dtype),
+        cost_estimate=pl.CostEstimate(flops=10_000_000, bytes_accessed=4 * t * h, transcendentals=0),
+    )(value)
 
 
 def ln_rows(z, gain):
@@ -681,21 +715,22 @@
         b1_s, hat_two, rstd_two = ln_rows(resid, gain_two)
         b1, gelu_out, d_up = (z.reshape(t, z.shape[-1]) for z in gather_mlp(n, b1_s, w_up, w_down, dy, 6))
         d_b1 = matmul_reduce_scatter(n, d_up, w_up, 1, 3)
-        late_gelu, d_b1 = lax.optimization_barrier((gelu_out, d_b1))
+        d_ln, d_gain_two = ln_back(d_b1, hat_two, rstd_two, gain_two)
+        d_resid_s = dy_s + d_ln
+        d_resid = lax.all_gather(d_resid_s, 'model', axis=0, tiled=True)
+        late_gelu, _ = lax.optimization_barrier((gelu_out, d_resid_s))
         part_two = matmul_reduce_scatter(n, late_gelu, w_down, 0, 4)
         late_gelu, late_up, part_two = lax.optimization_barrier((late_gelu, d_up, part_two))
         d_w_down = mm(late_gelu, dy, 0, 0).astype(BF16)
         d_w_up = mm(b1, late_up, 0, 0).astype(BF16)
 
-        d_ln, d_gain_two = ln_back(d_b1, hat_two, rstd_two, gain_two)
-        d_resid_s = dy_s + d_ln
         d_heads = mm(wo_full, d_resid_s, 1, 1).astype(BF16).reshape(n, hd, ts)
         dot = exchange(n, d_heads, (hd, t), leading, column_block(ts), 1)
-        d_resid = lax.all_gather(d_resid_s, 'model', axis=0, tiled=True)
 
         d_qkv = attention_backward(q, k, v, qkvt, ot, dot, lse, start_row, tab, bq, bk)
         y_s = (resid.astype(F32) + part_two.astype(F32)).astype(BF16)
-        y_out = lax.all_gather(y_s[None], 'model', axis=1, tiled=True)
+        y_out = lax.all_gather(y_s, 'model', axis=0, tiled=True)
+        y_out = copy_rows(y_out)[None]
         d_norm = matmul_reduce_scatter(n, d_qkv, w_qkv.T, 0, 5)
         d_w_qkv = mm(a_full, d_qkv, 0, 0).astype(BF16)
         d_w_out = mm(ot, d_resid, 1, 0).astype(BF16)

time: 624 us -> 592 us (0.949); the launches traced: 623 us -> 582 us
  waiting for transfers between devices: 161 us -> 88.8 us
  Pallas kernels: 353 us -> 389 us
    all_gather x1, waiting for transfers between devices: 68.8 us -> 27.9 us  [layer(): d_resid = lax.all_gather(d_resid_s, 'model', axis=0, tiled=True)]
    pallas_call x3, Pallas kernels: 170 us -> 208 us  [matmul_reduce_scatter(): pl.pallas_call(functools.partial(reduce_kernel, n, r_dim), out_shape=jax....]
    all_gather x1, waiting for transfers between devices: 21.3 us -> 0.01 us  [layer(): d_x = lax.all_gather((d_resid_s + d_ln)[None], 'model', axis=1, tiled=True)]
    pallas_call x0 -> x1, Pallas kernels: none -> 13.8 us  [copy_rows(): pl.pallas_call(copy_kernel, grid=(t // bt,), in_specs=[row], out_specs=ro...]
    pallas_call x1, Pallas kernels: 71.3 us -> 61.1 us  [gather_mlp(): pl.pallas_call(functools.partial(gather_mlp_kernel, n), out_shape=[jax.Sh...]
    all_gather x1, waiting for transfers between devices: 69 us -> 59.3 us  [layer(): y_out = lax.all_gather(y_s, 'model', axis=0, tiled=True)]
    unnamed x46 -> x41, local copies, waits for them, and re-layouts: 24.8 us -> 18.6 us
  transfers between devices with their start and end apart: 4 -> 4, of which waited for: 3 -> 2; matrix products, arithmetic and copies ran while one was open for 6% -> 9% of each run, Pallas kernels for 12% -> 28%
where the time goes in v4:
time: 592 us; the launch traced here: 582 us
  Pallas kernels  389 us (66%)
  waiting for transfers between devices  88.8 us (15%)
  matrix products  48 us (8%)
  local copies, waits for them, and re-layouts  23 us (4%)
  other arithmetic  18.2 us (3%)
  between operations  14.4 us (2%)
    pallas_call x3, Pallas kernels, matmul_reduce_scatter(): pl.pallas_call(functools.partial(reduce_kernel, n, r_dim), out_shape=jax....  208 us
    pallas_call x1, Pallas kernels, gather_mlp(): pl.pallas_call(functools.partial(gather_mlp_kernel, n), out_shape=[jax.Sh...  61.1 us
    all_gather x1, waiting for transfers between devices, layer(): y_out = lax.all_gather(y_s, 'model', axis=0, tiled=True)  59.3 us
    pallas_call x3, Pallas kernels, exchange(): pl.pallas_call(functools.partial(exchange_kernel, n, src_of, dst_of), out...  50 us
    dot_general x6, matrix products, mm(): lax.dot_general(a, b, (((ca,), (cb,)), ((), ())), preferred_element_type=...  48 us
    all_gather x1, waiting for transfers between devices, layer(): d_resid = lax.all_gather(d_resid_s, 'model', axis=0, tiled=True)  27.9 us
    pallas_call x1, Pallas kernels, attention_backward(): pl.pallas_call(functools.partial(attn_bwd_kernel, bk), grid_spec=pltpu.Pr...  21.2 us
    pallas_call x1, Pallas kernels, ln_qkv(): pl.pallas_call(ln_qkv_kernel, grid=(t // bt,), in_specs=[row(h), pl.Block...  20.7 us
  transfers between devices with their start and end apart: 4, of which 2 were waited for; matrix products, arithmetic and copies ran while one was open for 9% of the time, Pallas kernels for 28%

profile of v4, /device:TPU:97, one launch (start us, length us, event | category | flops | bytes accessed | tf_op | source)
XLA Modules:
  0.0 581.7 jit_solution(4725476704539907522)
XLA Ops:
  8.0 1.3 reshape.414.g_ref
  9.3 1.3 convert_element_type.76
  11.8 1.5 add_select_fusion
  15.1 1.2 convert_reduce_fusion
  17.2 1.3 fusion.23
  19.2 20.7 %ln_qkv.1 = (bf16[4096,2048]{1,0:T(8,128)(2,1)}, bf16[4096,64]{1,0:T(8,128)(2,1)}, bf16[4096,64]{1,0:T(8,128)(2,1)}, bf16[4096,64]{1,0:T(8,128)(2,1)}, bf16[192,4096]{1,0:T(8,128)(2,1)}) custom-call(bf16[4096,2048]{1,0:T(8,128)(2,1)} %bitcast.118, bf16[1,2048]{1,0:T(2,128)(2,1)} %reshape.414.g_ref, bf16[192,2048]{1,0:T(8,128)(2,1)} %bitcast.109), custom_call_target="tpu_custom_call" | custom-call | flops 3388997632 | bytes 33554432 | tf_op jit(solution)/shard_map/ln_qkv/pallas_call | solution.py:47
  39.9 14.3 %attn_fwd.1 = (bf16[64,4096]{1,0:T(8,128)(2,1)}, f32[1,4096]{1,0:T(1,128)}) custom-call(s32[4,8]{1,0:T(4,128)} %pad_add_fusion.tab_ref, bf16[4096,64]{1,0:T(8,128)(2,1)} %get-tuple-element.22.k_ref, bf16[192,4096]{1,0:T(8,128)(2,1)} %get-tuple-element.23.qt_ref.vt_ref.t_ref, bf16[192,4096]{1,0:T(8,128)(2,1)} %get-tuple-element.23.qt_ref.vt_ref.t_ref, ...), custom_call_target="tpu_custom_call" | custom-call | flops 17179869184 | bytes 2097152 | tf_op jit(solution)/shard_map/attn_fwd/pallas_call | solution.py:126
  54.2 19.1 %shard_map.152 = bf16[32,64,128]{2,1,0:T(8,128)(2,1)} custom-call(bf16[64,4096]{1,0:T(8,128)(2,1)} %get-tuple-element.24.in_ref.ot_ref), custom_call_target="tpu_custom_call" | custom-call | flops 2000000000 | bytes 1048576 | tf_op jit(solution)/shard_map/pallas_call | solution.py:257
  73.9 4.9 fusion.36
  79.3 61.1 %gather_mlp.1 = (bf16[4,4,2,128,2048]{4,3,2,1,0:T(8,128)(2,1)}, bf16[8,512,256]{2,1,0:T(8,128)(2,1)}, bf16[8,512,256]{2,1,0:T(8,128)(2,1)}) custom-call(bf16[128,2048]{1,0:T(8,128)(2,1)S(1)} %multiply_convert_fusion.own_ref, bf16[2048,256]{1,0:T(8,128)(2,1)S(1)} %copy-done.2, bf16[256,2048]{1,0:T(8,128)(2,1)S(1)} %copy-done.3, bf16[8,512,2048]{2,1,0:T(8,128)(2,1)} %bitcast.115), custom_call_target="tpu_custom_call" | custom-call | flops 40000000000 | bytes 33554432 | tf_op jit(solution)/shard_map/gather_mlp/pallas_call | solution.py:637
  140.4 1.6 copy-done.5
  142.0 57.4 %shard_map.153 = bf16[128,2048]{1,0:T(8,128)(2,1)S(1)} custom-call(bf16[4,4,2,128,256]{4,3,2,1,0:T(8,128)(2,1)S(1)} %bitcast.111, bf16[2048,256]{1,0:T(8,128)(2,1)S(1)} %copy-done.2), custom_call_target="tpu_custom_call" | custom-call | flops 40000000000 | bytes 4194304 | tf_op jit(solution)/shard_map/pallas_call | solution.py:445
  199.9 1.6 fusion.31
  201.5 6.5 %fusion.8 = bf16[2048,128]{0,1:T(8,128)(2,1)S(1)} fusion(bf16[128,2048]{1,0:T(8,128)(2,1)S(1)} %fusion.31, bf16[2048,2048]{1,0:T(8,128)(2,1)} %bitcast.114), kind=kOutput, calls=%fused_computation.10 | convolution fusion | flops 1074003968 | bytes 9437184 | tf_op jit(solution)/shard_map/dot_general | solution.py:22
  208.9 16.6 %shard_map.156.dot_ref = bf16[64,4096]{1,0:T(8,128)(2,1)} custom-call(bf16[32,64,128]{2,1,0:T(8,128)(2,1)} %bitcast.121), custom_call_target="tpu_custom_call" | custom-call | flops 2000000000 | bytes 1048576 | tf_op jit(solution)/shard_map/pallas_call | solution.py:257
  225.5 21.2 %attn_bwd.1 = bf16[4096,192]{1,0:T(8,128)(2,1)} custom-call(s32[4,8]{1,0:T(4,128)} %pad_add_fusion.tab_ref, bf16[4096,64]{1,0:T(8,128)(2,1)} %get-tuple-element.29.q_ref, bf16[4096,64]{1,0:T(8,128)(2,1)} %get-tuple-element.22.k_ref, bf16[4096,64]{1,0:T(8,128)(2,1)} %get-tuple-element.30.v_ref, bf16[192,4096]{1,0:T(8,128)(2,1)} %get-tuple-element.23.qt_ref.vt_ref.t_ref, ...), custom_call_target="tpu_custom_call" | custom-call | flops 42949672960 | bytes 4194304 | tf_op jit(solution)/shard_map/attn_bwd/pallas_call | solution.py:201
  246.8 1.6 copy-done.7
  248.4 56.5 %shard_map.157 = bf16[128,2048]{1,0:T(8,128)(2,1)S(1)} custom-call(bf16[4,4,2,128,192]{4,3,2,1,0:T(8,128)(2,1)S(1)} %bitcast.113, bf16[192,2048]{1,0:T(8,128)(2,1)S(1)} %bitcast.110), custom_call_target="tpu_custom_call" | custom-call | flops 40000000000 | bytes 3145728 | tf_op jit(solution)/shard_map/pallas_call | solution.py:445
  304.9 1.5 fusion.30
  306.5 2.4 fusion.32
  309.8 1.2 copy-done.4
  311.0 94.1 %shard_map.154 = bf16[128,2048]{1,0:T(8,128)(2,1)S(1)} custom-call(bf16[4,4,2,128,256]{4,3,2,1,0:T(8,128)(2,1)S(1)} %bitcast.107, bf16[256,2048]{1,0:T(8,128)(2,1)S(1)} %copy-done.4), custom_call_target="tpu_custom_call" | custom-call | flops 40000000000 | bytes 4194304 | tf_op jit(solution)/shard_map/pallas_call | solution.py:445
  406.8 14.3 %shard_map.158 = f32[32,1,4096]{2,1,0:T(1,128)} custom-call(f32[1,4096]{1,0:T(1,128)} %bitcast.126), custom_call_target="tpu_custom_call" | custom-call | flops 2000000000 | bytes 16384 | tf_op jit(solution)/shard_map/pallas_call | solution.py:257
  421.1 1.4 reduce_sum.109
  423.1 11.1 %convolution_convert_fusion.1 = bf16[2048,192]{0,1:T(8,128)(2,1)} fusion(bf16[4096,2048]{1,0:T(8,128)(2,1)} %get-tuple-element.32, bf16[4096,192]{1,0:T(8,128)(2,1)} %attn_bwd.1), kind=kOutput, calls=%fused_computation.4 | convolution fusion | flops 3221618688 | bytes 19136512 | tf_op jit(solution)/shard_map/dot_general | solution.py:22
  434.2 10.6 %convolution_convert_fusion = bf16[2048,256]{1,0:T(8,128)(2,1)} fusion(bf16[4096,2048]{1,0:T(8,128)(2,1)} %bitcast.127, bf16[4096,256]{1,0:T(8,128)(2,1)S(1)} %bitcast.112), kind=kOutput, calls=%fused_computation.3 | convolution fusion | flops 4295491584 | bytes 19922944 | tf_op jit(solution)/shard_map/dot_general | solution.py:22
  444.8 5.5 fusion.2
  450.3 27.9 %all-gather.10.cloned.1.call-done = bf16[4096,2048]{1,0:T(8,128)(2,1)} async-done(((bf16[128,2048]{1,0:T(8,128)(2,1)}), bf16[4096,2048]{1,0:T(8,128)(2,1)}) %all-gather.10.cloned.1.call-update) | async-done | bytes 16777232 | tf_op jit(solution)/shard_map/all_gather | solution.py:720
  478.2 9.5 %fusion.9 = bf16[1,64,2048]{2,1,0:T(8,128)(2,1)} fusion(bf16[64,4096]{1,0:T(8,128)(2,1)S(1)} %copy-done.11, bf16[4096,2048]{1,0:T(8,128)(2,1)} %all-gather.10.cloned.1.call-done), kind=kOutput, calls=%fused_computation.12 | convolution fusion | flops 1073872896 | bytes 17563648 | tf_op jit(solution)/shard_map/dot_general | solution.py:22
  487.7 59.3 %all-gather.8.cloned.1.call-done.src_ref = bf16[4096,2048]{1,0:T(8,128)(2,1)} async-done(((bf16[128,2048]{1,0:T(8,128)(2,1)}), bf16[4096,2048]{1,0:T(8,128)(2,1)}) %all-gather.8.cloned.1.call-update) | async-done | bytes 16777232 | tf_op jit(solution)/shard_map/all_gather | solution.py:732
  547.0 13.8 %shard_map.155 = bf16[4096,2048]{1,0:T(8,128)(2,1)} custom-call(bf16[4096,2048]{1,0:T(8,128)(2,1)} %all-gather.8.cloned.1.call-done.src_ref), custom_call_target="tpu_custom_call" | custom-call | flops 10000000 | bytes 33554432 | tf_op jit(solution)/shard_map/pallas_call | solution.py:663
  560.8 14.2 %copy.37 = bf16[1,4096,2048]{2,1,0:T(8,128)(2,1)} copy(bf16[1,4096,2048]{2,1,0:T(8,128)(2,1)} %bitcast.119) | data formatting | bytes 33554432
  (78 shorter events, 11.0 us)
Async XLA Ops:
  7.2 66.7 %all-gather.6.cloned.1.call-start = ((), (), s32[]{:S(2)}) async-start(), calls=%async_computation | async-start | bytes 8650752 | tf_op jit(solution)/shard_map/all_gather | solution.py:701
  8.0 442.3 %all-gather.12.cloned.1.call-start = ((), (), s32[]{:S(2)}) async-start(), calls=%async_computation.3 | async-start | bytes 17301504 | tf_op jit(solution)/shard_map/all_gather | solution.py:740
  17.2 22.7 %copy-start.13 = (f32[128]{0:T(128)}, f32[128]{0:T(128)S(1)}, u32[]{:S(2)}) copy-start(f32[128]{0:T(128)S(1)} %broadcast_multiply_fusion.2) | copy-start | bytes 1540
  54.2 25.1 %copy-start.2 = (bf16[2048,256]{1,0:T(8,128)(2,1)S(1)}, bf16[2048,256]{1,0:T(8,128)(2,1)}, u32[]{:S(2)}) copy-start(bf16[2048,256]{1,0:T(8,128)(2,1)} %r_ref.2) | copy-start | bytes 3145732
  54.2 25.1 %copy-start.3 = (bf16[256,2048]{1,0:T(8,128)(2,1)S(1)}, bf16[256,2048]{1,0:T(8,128)(2,1)}, u32[]{:S(2)}) copy-start(bf16[256,2048]{1,0:T(8,128)(2,1)} %r_ref.3) | copy-start | bytes 3145732
  78.8 121.1 %copy-start.8 = (f32[128,2048]{1,0:T(8,128)}, f32[128,2048]{1,0:T(8,128)S(1)}, u32[]{:S(2)}) copy-start(f32[128,2048]{1,0:T(8,128)S(1)} %get-tuple-element.49) | copy-start | bytes 3145732
  140.4 1.6 copy-start.5
  201.5 105.0 %copy-start.10 = (bf16[128,2048]{1,0:T(8,128)(2,1)}, bf16[128,2048]{1,0:T(8,128)(2,1)S(1)}, u32[]{:S(2)}) copy-start(bf16[128,2048]{1,0:T(8,128)(2,1)S(1)} %fusion.31) | copy-start | bytes 1572868
  225.5 21.2 %copy-start.1 = (bf16[2048,192]{0,1:T(8,128)(2,1)S(1)}, bf16[2048,192]{0,1:T(8,128)(2,1)}, u32[]{:S(2)}) copy-start(bf16[2048,192]{0,1:T(8,128)(2,1)} %param.12) | copy-start | bytes 2359300
  246.8 1.6 copy-start.7
  248.4 56.6 %copy-start.12 = (f32[2048]{0:T(1024)S(1)}, f32[2048]{0:T(1024)}, u32[]{:S(2)}) copy-start(f32[2048]{0:T(1024)} %convert_element_type.76) | copy-start | bytes 24580
  248.4 56.6 %copy-start.14 = (f32[128]{0:T(128)S(1)}, f32[128]{0:T(128)}, u32[]{:S(2)}) copy-start(f32[128]{0:T(128)} %copy-done.13) | copy-start | bytes 1540
  248.4 56.6 %copy-start.15 = (f32[128]{0:T(128)S(1)}, f32[128]{0:T(128)}, u32[]{:S(2)}) copy-start(f32[128]{0:T(128)} %add_rsqrt_fusion) | copy-start | bytes 1540
  248.4 61.4 %copy-start = (bf16[8,512,256]{2,1,0:T(8,128)(2,1)S(1)}, bf16[8,512,256]{2,1,0:T(8,128)(2,1)}, u32[]{:S(2)}) copy-start(bf16[8,512,256]{2,1,0:T(8,128)(2,1)} %get-tuple-element.25) | copy-start | bytes 6291460
  308.9 169.2 %all-gather.10.cloned.1.call-start = ((), (), s32[]{:S(2)}) async-start(), calls=%async_computation.2 | async-start | bytes 17301504 | tf_op jit(solution)/shard_map/all_gather | solution.py:720
  309.7 237.3 %all-gather.8.cloned.1.call-start = ((), (), s32[]{:S(2)}) async-start(), calls=%async_computation.1 | async-start | bytes 17301504 | tf_op jit(solution)/shard_map/all_gather | solution.py:732
  309.8 1.2 copy-start.4
  311.0 94.1 %copy-start.9 = (f32[128,2048]{1,0:T(8,128)S(1)}, f32[128,2048]{1,0:T(8,128)}, u32[]{:S(2)}) copy-start(f32[128,2048]{1,0:T(8,128)} %copy-done.8) | copy-start | bytes 3145732
  422.5 11.7 %copy-start.6 = (bf16[8,512,256]{2,1,0:T(8,128)(2,1)S(1)}, bf16[8,512,256]{2,1,0:T(8,128)(2,1)}, u32[]{:S(2)}) copy-start(bf16[8,512,256]{2,1,0:T(8,128)(2,1)} %get-tuple-element.26) | copy-start | bytes 6291460
  423.1 21.7 %slice-start = ((s8[16777216]{0:T(1024)(128)(4,1)}), s8[4194304]{0:T(1024)(128)(4,1)S(1)}, s32[]{:S(2)}) async-start(s8[16777216]{0:T(1024)(128)(4,1)} %bitcast.116), calls=%async_computation.4 | async-start | bytes 8388608
  423.1 21.7 %slice-start.1 = ((s8[16777216]{0:T(1024)(128)(4,1)}), s8[4194304]{0:T(1024)(128)(4,1)S(1)}, s32[]{:S(2)}) async-start(s8[16777216]{0:T(1024)(128)(4,1)} %bitcast.116), calls=%async_computation.5 | async-start | bytes 8388608
  434.2 10.6 %slice-start.2 = ((s8[16777216]{0:T(1024)(128)(4,1)}), s8[4194304]{0:T(1024)(128)(4,1)S(1)}, s32[]{:S(2)}) async-start(s8[16777216]{0:T(1024)(128)(4,1)} %bitcast.116), calls=%async_computation.6 | async-start | bytes 8388608
  434.2 10.6 %slice-start.3 = ((s8[16777216]{0:T(1024)(128)(4,1)}), s8[4194304]{0:T(1024)(128)(4,1)S(1)}, s32[]{:S(2)}) async-start(s8[16777216]{0:T(1024)(128)(4,1)} %bitcast.116), calls=%async_computation.7 | async-start | bytes 8388608
  444.8 33.4 %copy-start.11 = (bf16[64,4096]{1,0:T(8,128)(2,1)S(1)}, bf16[64,4096]{1,0:T(8,128)(2,1)}, u32[]{:S(2)}) copy-start(bf16[64,4096]{1,0:T(8,128)(2,1)} %get-tuple-element.24.in_ref.ot_ref) | copy-start | bytes 1572868
Sparse Core Ops, SparseCore 0:
  10.1 51.9 all-gather.5
  309.1 99.9 all-gather.11
  411.1 66.9 all-gather.9
  480.1 66.8 all-gather.7

commit v5 on v4

--- a/solution.py
+++ b/solution.py
@@ -271,10 +271,6 @@
 
 def leading(ref, j):
     return ref.at[j]
-
-
-def whole_ref(ref, j):
-    return ref
 
 
 def ring_place(n, q):
@@ -653,17 +649,97 @@
 
 
 def copy_kernel(src_ref, dst_ref):
-    dst_ref[...] = src_ref[...]
-
-
-def copy_rows(value):
-    t, h = value.shape
-    bt = min(512, t)
-    row = pl.BlockSpec((bt, h), lambda i: (i, 0))
+    dst_ref[...] = src_ref[...].reshape(dst_ref.shape)
+
+
+def copy_half(pair, half):
+    n, _, tb, h = pair.shape
+    per = min(4, n)
     return pl.pallas_call(
-        copy_kernel, grid=(t // bt,), in_specs=[row], out_specs=row, out_shape=jax.ShapeDtypeStruct((t, h), value.dtype),
-        cost_estimate=pl.CostEstimate(flops=10_000_000, bytes_accessed=4 * t * h, transcendentals=0),
-    )(value)
+        copy_kernel, grid=(n // per,),
+        in_specs=[pl.BlockSpec((per, 1, tb, h), lambda i: (i, half, 0, 0))], out_specs=pl.BlockSpec((per * tb, h), lambda i: (i, 0)),
+        out_shape=jax.ShapeDtypeStruct((n * tb, h), pair.dtype),
+        cost_estimate=pl.CostEstimate(flops=10_000_000, bytes_accessed=4 * n * tb * h, transcendentals=0),
+    )(pair)
+
+
+def out_grad_kernel(ot_ref, src_ref, out_ref, acc):
+    i = pl.program_id(0)
+
+    @pl.when(i == 0)
+    def _():
+        acc[...] = jnp.zeros_like(acc)
+
+    h = src_ref.shape[-1]
+    acc[...] += mm(ot_ref[...], src_ref[...].reshape(-1, h), 1, 0)
+
+    @pl.when(i == pl.num_programs(0) - 1)
+    def _():
+        out_ref[...] = acc[...].astype(BF16)
+
+
+def out_grad(ot, pair, half):
+    n, _, tb, h = pair.shape
+    hd = ot.shape[0]
+    per = min(4, n)
+    return pl.pallas_call(
+        out_grad_kernel, grid=(n // per,),
+        in_specs=[pl.BlockSpec((hd, per * tb), lambda i: (0, i)), pl.BlockSpec((per, 1, tb, h), lambda i: (i, half, 0, 0))],
+        out_specs=pl.BlockSpec((hd, h), lambda i: (0, 0)),
+        out_shape=jax.ShapeDtypeStruct((hd, h), BF16),
+        scratch_shapes=[pltpu.VMEM((hd, h), F32)],
+        cost_estimate=pl.CostEstimate(flops=2 * n * tb * h * hd, bytes_accessed=2 * n * tb * h, transcendentals=0), name='out_grad',
+    )(ot, pair)
+
+
+def sum_kernel(n, in_ref, out_ref, land, mine, s_send, s_recv, b_send, b_recv):
+    me = lax.axis_index('model')
+    barrier = pltpu.get_barrier_semaphore()
+
+    def hello(off, _):
+        pl.semaphore_signal(barrier, inc=1, device_id={'model': lax.rem(me + off, n)}, device_id_type=MESH)
+        return 0
+
+    lax.fori_loop(1, n, hello, 0)
+    land[me] = in_ref[me]
+    pl.semaphore_wait(barrier, n - 1)
+
+    def scatter(off, slot):
+        to = lax.rem(me + off, n)
+        return pltpu.make_async_remote_copy(
+            in_ref.at[to], land.at[slot], s_send.at[off], s_recv.at[off], device_id={'model': to}, device_id_type=MESH)
+
+    def spread(off, slot):
+        return pltpu.make_async_remote_copy(
+            mine, out_ref.at[slot], b_send.at[off], b_recv.at[off], device_id={'model': lax.rem(me + off, n)}, device_id_type=MESH)
+
+    def each(body):
+        def step(off, _):
+            body(off, lax.rem(me - off + n, n))
+            return 0
+
+        lax.fori_loop(1, n, step, 0)
+
+    each(lambda off, come: scatter(off, me).start())
+    each(lambda off, come: scatter(off, come).wait())
+    mine[...] = jnp.sum(land[...], axis=0)
+    each(lambda off, come: spread(off, me).start())
+    out_ref[me] = mine[...]
+    each(lambda off, come: spread(off, come).wait())
+
+
+def sum_over_devices(n, value, collective_id):
+    piece = (1, value.size // n)
+    vmem = pl.BlockSpec(memory_space=pltpu.VMEM)
+    return pl.pallas_call(
+        functools.partial(sum_kernel, n),
+        out_shape=jax.ShapeDtypeStruct((n, *piece), F32),
+        in_specs=[vmem], out_specs=vmem,
+        scratch_shapes=[pltpu.VMEM((n, *piece), F32), pltpu.VMEM(piece, F32)] + [pltpu.SemaphoreType.DMA((n,))] * 4,
+        compiler_params=pltpu.CompilerParams(collective_id=collective_id, has_side_effects=True),
+        cost_estimate=pl.CostEstimate(flops=1_000_000_000, bytes_accessed=value.size * 8, transcendentals=0),
+        name='gain_sums',
+    )(value.reshape(n, *piece)).reshape(value.shape)
 
 
 def ln_rows(z, gain):
@@ -715,32 +791,29 @@
         b1_s, hat_two, rstd_two = ln_rows(resid, gain_two)
         b1, gelu_out, d_up = (z.reshape(t, z.shape[-1]) for z in gather_mlp(n, b1_s, w_up, w_down, dy, 6))
         d_b1 = matmul_reduce_scatter(n, d_up, w_up, 1, 3)
+        late_gelu, d_b1 = lax.optimization_barrier((gelu_out, d_b1))
         d_ln, d_gain_two = ln_back(d_b1, hat_two, rstd_two, gain_two)
         d_resid_s = dy_s + d_ln
-        d_resid = lax.all_gather(d_resid_s, 'model', axis=0, tiled=True)
-        late_gelu, _ = lax.optimization_barrier((gelu_out, d_resid_s))
         part_two = matmul_reduce_scatter(n, late_gelu, w_down, 0, 4)
         late_gelu, late_up, part_two = lax.optimization_barrier((late_gelu, d_up, part_two))
         d_w_down = mm(late_gelu, dy, 0, 0).astype(BF16)
         d_w_up = mm(b1, late_up, 0, 0).astype(BF16)
 
+        y_s = (resid.astype(F32) + part_two.astype(F32)).astype(BF16)
+        pair = lax.all_gather(jnp.stack([y_s, d_resid_s]), 'model', axis=0, tiled=True).reshape(n, 2, ts, h)
+        y_out = copy_half(pair, 0)[None]
         d_heads = mm(wo_full, d_resid_s, 1, 1).astype(BF16).reshape(n, hd, ts)
         dot = exchange(n, d_heads, (hd, t), leading, column_block(ts), 1)
 
         d_qkv = attention_backward(q, k, v, qkvt, ot, dot, lse, start_row, tab, bq, bk)
-        y_s = (resid.astype(F32) + part_two.astype(F32)).astype(BF16)
-        y_out = lax.all_gather(y_s, 'model', axis=0, tiled=True)
-        y_out = copy_rows(y_out)[None]
         d_norm = matmul_reduce_scatter(n, d_qkv, w_qkv.T, 0, 5)
         d_w_qkv = mm(a_full, d_qkv, 0, 0).astype(BF16)
-        d_w_out = mm(ot, d_resid, 1, 0).astype(BF16)
+        d_w_out = out_grad(ot, pair, 1)
 
         _, hat_one, rstd_one = ln_rows(x_s, gain_one)
         d_ln, d_gain_one = ln_back(d_norm, hat_one, rstd_one, gain_one)
         d_x = lax.all_gather((d_resid_s + d_ln)[None], 'model', axis=1, tiled=True)
-        gains = jnp.concatenate([d_gain_one, d_gain_two]).reshape(1, 2 * h)
-        gains = exchange(n, gains, (n, 1, 2 * h), whole_ref, leading, 2)
-        gains = jnp.sum(gains, axis=(0, 1)).astype(BF16)
+        gains = sum_over_devices(n, jnp.concatenate([d_gain_one, d_gain_two]), 2).astype(BF16)
         return (y_out, d_x, d_w_qkv, d_w_out.reshape(n_local, hd, h), d_w_up, d_w_down, gains[:h], gains[h:])
 
     in_specs = (P('data'), P('data'), P(), P(None, 'model'), P('model'), P(), P(None, 'model'), P('model'), P('data'))

time: 592 us -> 599 us (1.012)
  waiting for transfers between devices: 88.8 us -> 132 us
  Pallas kernels: 389 us -> 366 us
  matrix products: 48 us -> 34.1 us
    pallas_call x3, Pallas kernels: 208 us -> 172 us  [matmul_reduce_scatter(): pl.pallas_call(functools.partial(reduce_kernel, n, r_dim), out_shape=jax....]
    pallas_call x1 -> x3, Pallas kernels: 13.8 us -> 42 us  [the longest x1 17.9 us: sum_over_devices(): pl.pallas_call(functools.partial(sum_kernel, n), out_shape=jax.ShapeDtype...]
    all_gather x2 -> x1, waiting for transfers between devices: 87.2 us -> 110 us  [layer(): lax.all_gather(jnp.stack([y_s, d_resid_s]), 'model', axis=0, tiled=True)]
    all_gather x1, waiting for transfers between devices: 0.01 us -> 21 us  [layer(): d_x = lax.all_gather((d_resid_s + d_ln)[None], 'model', axis=1, tiled=True)]
    pallas_call x3 -> x2, Pallas kernels: 50 us -> 35.5 us  [exchange(): pl.pallas_call(functools.partial(exchange_kernel, n, src_of, dst_of), out...]
    dot_general x6 -> x5, matrix products: 48 us -> 34.1 us  [mm(): lax.dot_general(a, b, (((ca,), (cb,)), ((), ())), preferred_element_type=...]
    unnamed x41 -> x37, local copies, waits for them, and re-layouts: 18.6 us -> 17.4 us
  transfers between devices with their start and end apart: 4 -> 3, of which waited for: 2 -> 2; matrix products, arithmetic and copies ran while one was open for 9% -> 7% of each run, Pallas kernels for 28% -> 12%
where the time goes in v5:
time: 599 us; the launch traced here: 589 us
  Pallas kernels  366 us (61%)
  waiting for transfers between devices  132 us (22%)
  matrix products  34.1 us (6%)
  local copies, waits for them, and re-layouts  21.8 us (4%)
  other arithmetic  19.6 us (3%)
  between operations  14.4 us (2%)
    pallas_call x3, Pallas kernels, matmul_reduce_scatter(): pl.pallas_call(functools.partial(reduce_kernel, n, r_dim), out_shape=jax....  172 us
    all_gather x1, waiting for transfers between devices, layer(): lax.all_gather(jnp.stack([y_s, d_resid_s]), 'model', axis=0, tiled=True)  110 us
    pallas_call x1, Pallas kernels, gather_mlp(): pl.pallas_call(functools.partial(gather_mlp_kernel, n), out_shape=[jax.Sh...  61.1 us
    pallas_call x2, Pallas kernels, exchange(): pl.pallas_call(functools.partial(exchange_kernel, n, src_of, dst_of), out...  35.5 us
    dot_general x5, matrix products, mm(): lax.dot_general(a, b, (((ca,), (cb,)), ((), ())), preferred_element_type=...  34.1 us
    pallas_call x1, Pallas kernels, attention_backward(): pl.pallas_call(functools.partial(attn_bwd_kernel, bk), grid_spec=pltpu.Pr...  21.2 us
    all_gather x1, waiting for transfers between devices, layer(): d_x = lax.all_gather((d_resid_s + d_ln)[None], 'model', axis=1, tiled=True)  21 us
    pallas_call x1, Pallas kernels, ln_qkv(): pl.pallas_call(ln_qkv_kernel, grid=(t // bt,), in_specs=[row(h), pl.Block...  20.7 us
  transfers between devices with their start and end apart: 3, of which 2 were waited for; matrix products, arithmetic and copies ran while one was open for 7% of the time, Pallas kernels for 12%

profile of v5, /device:TPU:97, one launch (start us, length us, event | category | flops | bytes accessed | tf_op | source)
XLA Modules:
  0.0 588.6 jit_solution(3149001457260285398)
XLA Ops:
  8.0 1.3 convert_element_type.74
  9.3 1.3 reshape.421.g_ref
  12.5 1.5 add_select_fusion
  15.1 1.2 convert_reduce_fusion
  17.2 1.3 fusion.22
  19.2 20.7 %ln_qkv.1 = (bf16[4096,2048]{1,0:T(8,128)(2,1)}, bf16[4096,64]{1,0:T(8,128)(2,1)}, bf16[4096,64]{1,0:T(8,128)(2,1)}, bf16[4096,64]{1,0:T(8,128)(2,1)}, bf16[192,4096]{1,0:T(8,128)(2,1)}) custom-call(bf16[4096,2048]{1,0:T(8,128)(2,1)} %bitcast.126, bf16[1,2048]{1,0:T(2,128)(2,1)} %reshape.421.g_ref, bf16[192,2048]{1,0:T(8,128)(2,1)} %bitcast.113), custom_call_target="tpu_custom_call" | custom-call | flops 3388997632 | bytes 33554432 | tf_op jit(solution)/shard_map/ln_qkv/pallas_call | solution.py:47
  39.9 14.3 %attn_fwd.1 = (bf16[64,4096]{1,0:T(8,128)(2,1)}, f32[1,4096]{1,0:T(1,128)}) custom-call(s32[4,8]{1,0:T(4,128)} %pad_add_fusion.tab_ref, bf16[4096,64]{1,0:T(8,128)(2,1)} %get-tuple-element.23.k_ref, bf16[192,4096]{1,0:T(8,128)(2,1)} %get-tuple-element.24.qt_ref.vt_ref.t_ref, bf16[192,4096]{1,0:T(8,128)(2,1)} %get-tuple-element.24.qt_ref.vt_ref.t_ref, ...), custom_call_target="tpu_custom_call" | custom-call | flops 17179869184 | bytes 2097152 | tf_op jit(solution)/shard_map/attn_fwd/pallas_call | solution.py:126
  54.2 19.0 %shard_map.152 = bf16[32,64,128]{2,1,0:T(8,128)(2,1)} custom-call(bf16[64,4096]{1,0:T(8,128)(2,1)} %get-tuple-element.25.in_ref.ot_ref), custom_call_target="tpu_custom_call" | custom-call | flops 2000000000 | bytes 1048576 | tf_op jit(solution)/shard_map/pallas_call | solution.py:257
  73.7 5.1 fusion.35
  79.3 61.1 %gather_mlp.1 = (bf16[4,4,2,128,2048]{4,3,2,1,0:T(8,128)(2,1)}, bf16[8,512,256]{2,1,0:T(8,128)(2,1)}, bf16[8,512,256]{2,1,0:T(8,128)(2,1)}) custom-call(bf16[128,2048]{1,0:T(8,128)(2,1)S(1)} %multiply_convert_fusion.own_ref, bf16[2048,256]{1,0:T(8,128)(2,1)S(1)} %copy-done.2, bf16[256,2048]{1,0:T(8,128)(2,1)S(1)} %copy-done.3, bf16[8,512,2048]{2,1,0:T(8,128)(2,1)} %bitcast.123), custom_call_target="tpu_custom_call" | custom-call | flops 40000000000 | bytes 33554432 | tf_op jit(solution)/shard_map/gather_mlp/pallas_call | solution.py:633
  140.4 1.6 copy-done.5
  142.0 57.2 %shard_map.153 = bf16[128,2048]{1,0:T(8,128)(2,1)S(1)} custom-call(bf16[4,4,2,128,256]{4,3,2,1,0:T(8,128)(2,1)S(1)} %bitcast.115, bf16[2048,256]{1,0:T(8,128)(2,1)S(1)} %copy-done.2), custom_call_target="tpu_custom_call" | custom-call | flops 40000000000 | bytes 4194304 | tf_op jit(solution)/shard_map/pallas_call | solution.py:441
  199.2 58.4 %shard_map.154 = bf16[128,2048]{1,0:T(8,128)(2,1)S(1)} custom-call(bf16[4,4,2,128,256]{4,3,2,1,0:T(8,128)(2,1)S(1)} %bitcast.111, bf16[256,2048]{1,0:T(8,128)(2,1)S(1)} %copy-done.4), custom_call_target="tpu_custom_call" | custom-call | flops 40000000000 | bytes 4194304 | tf_op jit(solution)/shard_map/pallas_call | solution.py:441
  257.6 1.3 fusion.27
  258.9 1.5 fusion.31
  260.4 2.9 fusion.8
  264.3 16.5 %shard_map.156.dot_ref = bf16[64,4096]{1,0:T(8,128)(2,1)} custom-call(bf16[32,64,128]{2,1,0:T(8,128)(2,1)} %bitcast.130), custom_call_target="tpu_custom_call" | custom-call | flops 2000000000 | bytes 1048576 | tf_op jit(solution)/shard_map/pallas_call | solution.py:257
  280.8 21.2 %attn_bwd.1 = bf16[4096,192]{1,0:T(8,128)(2,1)} custom-call(s32[4,8]{1,0:T(4,128)} %pad_add_fusion.tab_ref, bf16[4096,64]{1,0:T(8,128)(2,1)} %get-tuple-element.31.q_ref, bf16[4096,64]{1,0:T(8,128)(2,1)} %get-tuple-element.23.k_ref, bf16[4096,64]{1,0:T(8,128)(2,1)} %get-tuple-element.32.v_ref, bf16[192,4096]{1,0:T(8,128)(2,1)} %get-tuple-element.24.qt_ref.vt_ref.t_ref, ...), custom_call_target="tpu_custom_call" | custom-call | flops 42949672960 | bytes 4194304 | tf_op jit(solution)/shard_map/attn_bwd/pallas_call | solution.py:201
  302.1 1.6 copy-done.7
  303.7 56.2 %shard_map.157 = bf16[128,2048]{1,0:T(8,128)(2,1)S(1)} custom-call(bf16[4,4,2,128,192]{4,3,2,1,0:T(8,128)(2,1)S(1)} %bitcast.117, bf16[192,2048]{1,0:T(8,128)(2,1)S(1)} %bitcast.114), custom_call_target="tpu_custom_call" | custom-call | flops 40000000000 | bytes 3145728 | tf_op jit(solution)/shard_map/pallas_call | solution.py:441
  359.8 1.5 fusion.29
  361.4 2.4 fusion.32
  363.9 2.1 pad_maximum_fusion
  366.8 17.9 %gain_sums.1 = f32[32,1,128]{2,1,0:T(1,128)} custom-call(f32[32,1,128]{2,1,0:T(1,128)} %pad_maximum_fusion.1.in_ref), custom_call_target="tpu_custom_call" | custom-call | flops 1000000000 | bytes 32768 | tf_op jit(solution)/shard_map/gain_sums/pallas_call | solution.py:734
  386.0 10.8 %convolution_convert_fusion.1 = bf16[2048,192]{0,1:T(8,128)(2,1)} fusion(bf16[4096,2048]{1,0:T(8,128)(2,1)} %get-tuple-element.34, bf16[4096,192]{1,0:T(8,128)(2,1)} %attn_bwd.1), kind=kOutput, calls=%fused_computation.4 | convolution fusion | flops 3221618688 | bytes 19136512 | tf_op jit(solution)/shard_map/dot_general | solution.py:22
  396.9 9.8 %convolution_convert_fusion = bf16[2048,256]{1,0:T(8,128)(2,1)} fusion(bf16[4096,2048]{1,0:T(8,128)(2,1)} %bitcast.140, bf16[4096,256]{1,0:T(8,128)(2,1)S(1)} %bitcast.116), kind=kOutput, calls=%fused_computation.3 | convolution fusion | flops 4295491584 | bytes 19922944 | tf_op jit(solution)/shard_map/dot_general | solution.py:22
  406.7 5.5 fusion.2
  412.3 21.0 %all-gather.9.cloned.1.call-done = bf16[4096,2048]{1,0:T(8,128)(2,1)} async-done(((bf16[128,2048]{1,0:T(8,128)(2,1)}), bf16[4096,2048]{1,0:T(8,128)(2,1)}) %all-gather.9.cloned.1.call-update) | async-done | bytes 16777232 | tf_op jit(solution)/shard_map/all_gather | solution.py:815
  433.2 110.2 %all-gather.7.cloned.1.call-done = bf16[64,128,2048]{2,1,0:T(8,128)(2,1)} async-done(((bf16[2,128,2048]{2,1,0:T(8,128)(2,1)}), bf16[64,128,2048]{2,1,0:T(8,128)(2,1)}) %all-gather.7.cloned.1.call-update) | async-done | bytes 33554448 | tf_op jit(solution)/shard_map/all_gather | solution.py:803
  543.4 10.3 %out_grad.1 = bf16[64,2048]{1,0:T(8,128)(2,1)} custom-call(bf16[64,4096]{1,0:T(8,128)(2,1)} %get-tuple-element.25.in_ref.ot_ref, bf16[32,2,128,2048]{3,2,1,0:T(8,128)(2,1)} %bitcast.118), custom_call_target="tpu_custom_call" | custom-call | flops 1073741824 | bytes 16777216 | tf_op jit(solution)/shard_map/out_grad/pallas_call | solution.py:685
  553.7 13.8 %shard_map.155 = bf16[4096,2048]{1,0:T(8,128)(2,1)} custom-call(bf16[32,2,128,2048]{3,2,1,0:T(8,128)(2,1)} %bitcast.119), custom_call_target="tpu_custom_call" | custom-call | flops 10000000 | bytes 33554432 | tf_op jit(solution)/shard_map/pallas_call | solution.py:658
  567.5 14.2 %copy.37 = bf16[1,4096,2048]{2,1,0:T(8,128)(2,1)} copy(bf16[1,4096,2048]{2,1,0:T(8,128)(2,1)} %bitcast.128) | data formatting | bytes 33554432
  (72 shorter events, 9.6 us)
Async XLA Ops:
  7.2 66.5 %all-gather.5.cloned.1.call-start = ((), (), s32[]{:S(2)}) async-start(), calls=%async_computation | async-start | bytes 8650752 | tf_op jit(solution)/shard_map/all_gather | solution.py:777
  8.0 425.3 %all-gather.9.cloned.1.call-start = ((), (), s32[]{:S(2)}) async-start(), calls=%async_computation.2 | async-start | bytes 17301504 | tf_op jit(solution)/shard_map/all_gather | solution.py:815
  17.2 22.7 %copy-start.9 = (f32[128]{0:T(128)}, f32[128]{0:T(128)S(1)}, u32[]{:S(2)}) copy-start(f32[128]{0:T(128)S(1)} %broadcast_multiply_fusion.2) | copy-start | bytes 1540
  73.7 5.6 copy-start.2
  73.7 5.6 copy-start.3
  140.4 1.6 copy-start.5
  142.0 57.2 %copy-start = (bf16[8,512,256]{2,1,0:T(8,128)(2,1)S(1)}, bf16[8,512,256]{2,1,0:T(8,128)(2,1)}, u32[]{:S(2)}) copy-start(bf16[8,512,256]{2,1,0:T(8,128)(2,1)} %get-tuple-element.26) | copy-start | bytes 6291460
  142.0 57.2 %copy-start.4 = (bf16[256,2048]{1,0:T(8,128)(2,1)S(1)}, bf16[256,2048]{1,0:T(8,128)(2,1)}, u32[]{:S(2)}) copy-start(bf16[256,2048]{1,0:T(8,128)(2,1)} %r_ref.3) | copy-start | bytes 3145732
  142.0 118.4 %slice-start = ((s8[8388608]{0:T(1024)(128)(4,1)}), s8[4194304]{0:T(1024)(128)(4,1)S(1)}, s32[]{:S(2)}) async-start(s8[8388608]{0:T(1024)(128)(4,1)} %bitcast.120), calls=%async_computation.3 | async-start | bytes 8388608
  199.2 61.2 %slice-start.1 = ((s8[8388608]{0:T(1024)(128)(4,1)}), s8[4194304]{0:T(1024)(128)(4,1)S(1)}, s32[]{:S(2)}) async-start(s8[8388608]{0:T(1024)(128)(4,1)} %bitcast.120), calls=%async_computation.4 | async-start | bytes 8388608
  280.8 21.2 %copy-start.1 = (bf16[2048,192]{0,1:T(8,128)(2,1)S(1)}, bf16[2048,192]{0,1:T(8,128)(2,1)}, u32[]{:S(2)}) copy-start(bf16[2048,192]{0,1:T(8,128)(2,1)} %param.12) | copy-start | bytes 2359300
  302.1 1.6 copy-start.7
  303.7 56.2 %copy-start.8 = (f32[2048]{0:T(1024)S(1)}, f32[2048]{0:T(1024)}, u32[]{:S(2)}) copy-start(f32[2048]{0:T(1024)} %convert_element_type.74) | copy-start | bytes 24580
  303.7 56.2 %copy-start.10 = (f32[128]{0:T(128)S(1)}, f32[128]{0:T(128)}, u32[]{:S(2)}) copy-start(f32[128]{0:T(128)} %copy-done.9) | copy-start | bytes 1540
  303.7 56.2 %copy-start.11 = (f32[128]{0:T(128)S(1)}, f32[128]{0:T(128)}, u32[]{:S(2)}) copy-start(f32[128]{0:T(128)} %add_rsqrt_fusion) | copy-start | bytes 1540
  363.9 179.5 %all-gather.7.cloned.1.call-start = ((), (), s32[]{:S(2)}) async-start(), calls=%async_computation.1 | async-start | bytes 34603008 | tf_op jit(solution)/shard_map/all_gather | solution.py:803
  386.0 10.9 %copy-start.6 = (bf16[8,512,256]{2,1,0:T(8,128)(2,1)S(1)}, bf16[8,512,256]{2,1,0:T(8,128)(2,1)}, u32[]{:S(2)}) copy-start(bf16[8,512,256]{2,1,0:T(8,128)(2,1)} %get-tuple-element.27) | copy-start | bytes 6291460
  386.0 20.7 %slice-start.2 = ((s8[16777216]{0:T(1024)(128)(4,1)}), s8[4194304]{0:T(1024)(128)(4,1)S(1)}, s32[]{:S(2)}) async-start(s8[16777216]{0:T(1024)(128)(4,1)} %bitcast.124), calls=%async_computation.5 | async-start | bytes 8388608
  386.0 20.7 %slice-start.3 = ((s8[16777216]{0:T(1024)(128)(4,1)}), s8[4194304]{0:T(1024)(128)(4,1)S(1)}, s32[]{:S(2)}) async-start(s8[16777216]{0:T(1024)(128)(4,1)} %bitcast.124), calls=%async_computation.6 | async-start | bytes 8388608
  396.9 9.8 %slice-start.4 = ((s8[16777216]{0:T(1024)(128)(4,1)}), s8[4194304]{0:T(1024)(128)(4,1)S(1)}, s32[]{:S(2)}) async-start(s8[16777216]{0:T(1024)(128)(4,1)} %bitcast.124), calls=%async_computation.7 | async-start | bytes 8388608
  396.9 9.8 %slice-start.5 = ((s8[16777216]{0:T(1024)(128)(4,1)}), s8[4194304]{0:T(1024)(128)(4,1)S(1)}, s32[]{:S(2)}) async-start(s8[16777216]{0:T(1024)(128)(4,1)} %bitcast.124), calls=%async_computation.8 | async-start | bytes 8388608
Sparse Core Ops, SparseCore 0:
  10.1 51.9 all-gather.4
  364.0 69.2 all-gather.8
  435.3 108.0 all-gather.6

commit v6 on v5

--- a/solution.py
+++ b/solution.py
@@ -20,6 +20,14 @@
 
 def mm(a, b, ca, cb):
     return lax.dot_general(a, b, (((ca,), (cb,)), ((), ())), preferred_element_type=F32)
+
+
+def cost(flops, moved):
+    return pl.CostEstimate(flops=flops, bytes_accessed=moved, transcendentals=0)
+
+
+def zero_map(*_):
+    return (0, 0)
 
 
 def ln_qkv_kernel(x_ref, g_ref, w_ref, a_ref, q_ref, k_ref, v_ref, t_ref):
@@ -47,11 +55,11 @@
     return pl.pallas_call(
         ln_qkv_kernel,
         grid=(t // bt,),
-        in_specs=[row(h), pl.BlockSpec((1, h), lambda i: (0, 0)), pl.BlockSpec((c, h), lambda i: (0, 0))],
+        in_specs=[row(h), pl.BlockSpec((1, h), zero_map), pl.BlockSpec((c, h), zero_map)],
         out_specs=[row(h), row(hd), row(hd), row(hd), pl.BlockSpec((c, bt), lambda i: (0, i))],
         out_shape=[jax.ShapeDtypeStruct((t, h), BF16)] + [jax.ShapeDtypeStruct((t, hd), BF16)] * 3 + [jax.ShapeDtypeStruct((c, t), BF16)],
         compiler_params=pltpu.CompilerParams(vmem_limit_bytes=VMEM_LIMIT),
-        cost_estimate=pl.CostEstimate(flops=2 * t * h * c + 20 * t * h, bytes_accessed=4 * t * h, transcendentals=0),
+        cost_estimate=cost(2 * t * h * c + 20 * t * h, 4 * t * h),
         name='ln_qkv',
     )(x, g.reshape(1, h), w)
 
@@ -129,7 +137,7 @@
             num_scalar_prefetch=1,
             grid=(t // bq,),
             in_specs=[
-                pl.BlockSpec((t, hd), lambda i, *_: (0, 0)),
+                pl.BlockSpec((t, hd), zero_map),
                 pl.BlockSpec((hd, bq), lambda i, *_: (0, i)),
                 pl.BlockSpec((hd, t), lambda i, *_: (2, 0)),
                 pl.BlockSpec((1, bq), lambda i, *_: (0, i)),
@@ -138,7 +146,7 @@
         ),
         out_shape=[jax.ShapeDtypeStruct((hd, t), BF16), jax.ShapeDtypeStruct((1, t), F32)],
         compiler_params=pltpu.CompilerParams(vmem_limit_bytes=VMEM_LIMIT),
-        cost_estimate=pl.CostEstimate(flops=16 * t * t * hd, bytes_accessed=8 * t * hd, transcendentals=t * t // 2),
+        cost_estimate=cost(16 * t * t * hd, 8 * t * hd),
         name='attn_fwd',
     )(tab, k, qkvt, qkvt, start)
 
@@ -196,7 +204,7 @@
 
 def attention_backward(q, k, v, qkvt, ot, dot, lse, start, tab, bq, bk):
     t, hd = k.shape
-    whole = lambda shape: pl.BlockSpec(shape, lambda i, *_: (0, 0))
+    whole = lambda shape: pl.BlockSpec(shape, zero_map)
     cols = lambda n: pl.BlockSpec((n, bq), lambda i, *_: (0, i))
     return pl.pallas_call(
         functools.partial(attn_bwd_kernel, bk),
@@ -212,7 +220,7 @@
         ),
         out_shape=jax.ShapeDtypeStruct((t, 3 * hd), BF16),
         compiler_params=pltpu.CompilerParams(vmem_limit_bytes=VMEM_LIMIT),
-        cost_estimate=pl.CostEstimate(flops=40 * t * t * hd, bytes_accessed=16 * t * hd, transcendentals=t * t // 2),
+        cost_estimate=cost(40 * t * t * hd, 16 * t * hd),
         name='attn_bwd',
     )(tab, q, k, v, qkvt, ot, dot, lse, start)
 
@@ -261,7 +269,7 @@
         out_specs=pl.BlockSpec(memory_space=pltpu.VMEM),
         scratch_shapes=[pltpu.SemaphoreType.DMA((n,)), pltpu.SemaphoreType.DMA((n,)), pltpu.SemaphoreType.DMA],
         compiler_params=pltpu.CompilerParams(collective_id=collective_id, has_side_effects=True),
-        cost_estimate=pl.CostEstimate(flops=2_000_000_000, bytes_accessed=2 * value.size * 2, transcendentals=0),
+        cost_estimate=cost(2_000_000_000, 2 * value.size * 2),
     )(value)
 
 
@@ -308,155 +316,174 @@
     pl.semaphore_wait(barrier, 5)
 
 
-def reduce_kernel(n, r_dim, l_ref, r_ref, out_ref, l_peer, r_peer, part, first, slot1, slot2, s_send, s_recv, p_send, p_recv, x_send, x_recv):
-    me = lax.axis_index('model')
-    my_core = lax.rem(me, 2)
-    side, _, _, tb, k = l_ref.shape
-    width = out_ref.shape[1] // 4
-    greet_neighbours(n)
-    peer = {'model': me + 1 - 2 * my_core}
-    swap = [
-        pltpu.make_async_remote_copy(src, dst, x_send.at[i], x_recv.at[i], device_id=peer, device_id_type=MESH)
-        for i, (src, dst) in enumerate([(r_ref, r_peer), (l_ref.at[:, :, 1 - my_core], l_peer)])
-    ]
-    for copy in swap:
-        copy.start()
-
-    def group(s, q):
-        _, _, sign, a, _, _ = ring_place(n, q)
-        at = lax.rem(a - sign * (1 + s) + 2 * side, side)
-        mine, other = (l_ref[:, at, my_core], l_peer[:, at]) if q < 2 else (l_ref[at, :, my_core], l_peer[at])
-        cols = pl.ds(q * width, width)
-        r_mine, r_other = (r_ref[:, cols], r_peer[:, cols]) if r_dim == 0 else (r_ref[cols, :], r_peer[cols, :])
-        total = mm(mine.reshape(side * tb, k), r_mine, 1, r_dim) + mm(other.reshape(side * tb, k), r_other, 1, r_dim)
-        part[lax.rem(s, 2), q] = total.reshape(side, tb, width)
-
-    def own_part(q, s, j):
-        _, _, sign, _, b, _ = ring_place(n, q)
-        return part[lax.rem(s, 2), q, lax.rem(b - sign * (1 + j) + 2 * side, side)]
-
-    def hop(q, s, j, src):
-        _, core, sign, a, b, chip_at = ring_place(n, q)
-        at = (q * (side - 1) + s) * side + j
+class Reduction:
+    def __init__(self, n, r_dim, l_ref, r_ref, out_ref, scratch):
+        self.n, self.r_dim, self.l_ref, self.r_ref, self.out_ref = n, r_dim, l_ref, r_ref, out_ref
+        (self.l_peer, self.r_peer, self.part, self.first, self.slot1, self.slot2,
+         self.s_send, self.s_recv, self.p_send, self.p_recv, self.x_send, self.x_recv) = scratch
+        self.side, _, _, self.tb, self.k = l_ref.shape
+        self.width = out_ref.shape[1] // 4
+        me = lax.axis_index('model')
+        self.my_core = lax.rem(me, 2)
+        peer = {'model': me + 1 - 2 * self.my_core}
+        pairs = [(r_ref, self.r_peer), (l_ref.at[:, :, 1 - self.my_core], self.l_peer)]
+        self.swap = [
+            pltpu.make_async_remote_copy(src, dst, self.x_send.at[i], self.x_recv.at[i], device_id=peer, device_id_type=MESH)
+            for i, (src, dst) in enumerate(pairs)
+        ]
+
+    def wrap(self, pos):
+        return lax.rem(pos + 2 * self.side, self.side)
+
+    def group(self, s, q):
+        _, _, sign, a, _, _ = ring_place(self.n, q)
+        at = self.wrap(a - sign * (1 + s))
+        l_ref, l_peer, core = self.l_ref, self.l_peer, self.my_core
+        mine, other = (l_ref[:, at, core], l_peer[:, at]) if q < 2 else (l_ref[at, :, core], l_peer[at])
+        cols = pl.ds(q * self.width, self.width)
+        at_r = (slice(None), cols) if self.r_dim == 0 else (cols, slice(None))
+        flat = (self.side * self.tb, self.k)
+        total = mm(mine.reshape(flat), self.r_ref[at_r], 1, self.r_dim) + mm(other.reshape(flat), self.r_peer[at_r], 1, self.r_dim)
+        self.part[lax.rem(s, 2), q] = total.reshape(self.side, self.tb, self.width)
+
+    def own_part(self, q, s, j):
+        _, _, sign, _, b, _ = ring_place(self.n, q)
+        return self.part[lax.rem(s, 2), q, self.wrap(b - sign * (1 + j))]
+
+    def hop(self, q, s, j, src):
+        _, core, sign, a, b, chip_at = ring_place(self.n, q)
+        at = self.arrived(q, s, j)
         return pltpu.make_async_remote_copy(
-            src, slot1.at[at], s_send.at[at], s_recv.at[at], device_id={'model': chip_at(a + sign, b) * 2 + core}, device_id_type=MESH)
-
-    def turn_hop(q, s, src):
-        _, core, sign, a, b, chip_at = ring_place(n, q)
-        at = q * (side - 1) + s
+            src, self.slot1.at[at], self.s_send.at[at], self.s_recv.at[at],
+            device_id={'model': chip_at(a + sign, b) * 2 + core}, device_id_type=MESH)
+
+    def turn_hop(self, q, s, src):
+        _, core, sign, a, b, chip_at = ring_place(self.n, q)
+        at = q * (self.side - 1) + s
         return pltpu.make_async_remote_copy(
-            src, slot2.at[at], p_send.at[at], p_recv.at[at], device_id={'model': chip_at(a, b + sign) * 2 + core}, device_id_type=MESH)
-
-    def arrived(q, s, j):
-        return (q * (side - 1) + s) * side + j
-
-    for copy in swap:
-        copy.wait()
-
-    def start_step(s, _):
+            src, self.slot2.at[at], self.p_send.at[at], self.p_recv.at[at],
+            device_id={'model': chip_at(a, b + sign) * 2 + core}, device_id_type=MESH)
+
+    def arrived(self, q, s, j):
+        return (q * (self.side - 1) + s) * self.side + j
+
+    def start_step(self, s):
         for q in range(4):
-            group(s, q)
+            self.group(s, q)
 
             @pl.when(s == 0)
             def _():
                 def start_round(j, _):
-                    at = q * side + j
-                    first[at] = own_part(q, 0, j).astype(BF16)
-                    hop(q, 0, j, first.at[at]).start()
+                    src = self.first.at[q * self.side + j]
+                    src[...] = self.own_part(q, 0, j).astype(BF16)
+                    self.hop(q, 0, j, src).start()
                     return 0
 
-                lax.fori_loop(0, side, start_round, 0)
-
-        return 0
-
-    lax.fori_loop(0, 2, start_step, 0)
-
-    def middle_round(t, _):
-        s, rest = 1 + t // (4 * side), lax.rem(t, 4 * side)
+                lax.fori_loop(0, self.side, start_round, 0)
+
+    def received(self, q, s, j):
+        slot = self.slot1.at[self.arrived(q, s - 1, j)]
+        self.hop(q, s - 1, j, slot).wait_recv()
+        return slot, slot[...].astype(F32) + self.own_part(q, s, j)
+
+    def middle_round(self, t):
+        s, rest = 1 + t // (4 * self.side), lax.rem(t, 4 * self.side)
         j, q = rest // 4, lax.rem(rest, 4)
-        at = arrived(q, s - 1, j)
-        hop(q, s - 1, j, slot1.at[at]).wait_recv()
-        slot1[at] = (slot1[at].astype(F32) + own_part(q, s, j)).astype(BF16)
-        hop(q, s, j, slot1.at[at]).start()
+        slot, total = self.received(q, s, j)
+        slot[...] = total.astype(BF16)
+        self.hop(q, s, j, slot).start()
         for ahead in range(4):
             @pl.when((q == 3) & (j == ahead))
             def _():
-                group(s + 1, ahead)
-
-        return 0
-
-    lax.fori_loop(0, 4 * side * (side - 2), middle_round, 0)
-
-    def last_sum(q, j):
-        at = arrived(q, side - 2, j)
-        hop(q, side - 2, j, slot1.at[at]).wait_recv()
-        return at, slot1[at].astype(F32) + own_part(q, side - 1, j)
-
-    def turn_first(q, _):
-        at, total = last_sum(q, 0)
-        slot1[at] = total.astype(BF16)
-        turn_hop(q, 0, slot1.at[at]).start()
-        return 0
-
-    lax.fori_loop(0, 4, turn_first, 0)
-
-    def turn_round(t, _):
+                self.group(s + 1, ahead)
+
+    def turn_first(self, q):
+        slot, total = self.received(q, self.side - 1, 0)
+        slot[...] = total.astype(BF16)
+        self.turn_hop(q, 0, slot).start()
+
+    def turned(self, q, s):
+        _, total = self.received(q, self.side - 1, s)
+        slot = self.slot2.at[q * (self.side - 1) + s - 1]
+        self.turn_hop(q, s - 1, slot).wait_recv()
+        return slot, slot[...].astype(F32) + total
+
+    def turn_round(self, t):
         s, q = 1 + t // 4, lax.rem(t, 4)
-        _, total = last_sum(q, s)
-        at = q * (side - 1) + s - 1
-        turn_hop(q, s - 1, slot2.at[at]).wait_recv()
-        slot2[at] = (slot2[at].astype(F32) + total).astype(BF16)
-        turn_hop(q, s, slot2.at[at]).start()
-        return 0
-
-    lax.fori_loop(0, 4 * (side - 2), turn_round, 0)
-
-    def turn_last(q, _):
-        _, total = last_sum(q, side - 1)
-        at = q * (side - 1) + side - 2
-        turn_hop(q, side - 2, slot2.at[at]).wait_recv()
-        out_ref[:, pl.ds(pl.multiple_of(q * width, width), width)] = (slot2[at].astype(F32) + total).astype(BF16)
-        return 0
-
-    lax.fori_loop(0, 4, turn_last, 0)
-
-    def drain(t, _):
-        q, s = t // (side - 1), lax.rem(t, side - 1)
-        turn_hop(q, s, slot2.at[t]).wait_send()
-        for j in range(side):
-            hop(q, s, j, slot1.at[t * side + j]).wait_send()
-        return 0
-
-    lax.fori_loop(0, 4 * (side - 1), drain, 0)
-
-
-def matmul_reduce_scatter(n, left, right, r_dim, collective_id):
-    t, k = left.shape
-    f = right.shape[1 - r_dim]
+        slot, total = self.turned(q, s)
+        slot[...] = total.astype(BF16)
+        self.turn_hop(q, s, slot).start()
+
+    def turn_last(self, q):
+        _, total = self.turned(q, self.side - 1)
+        self.out_ref[:, pl.ds(pl.multiple_of(q * self.width, self.width), self.width)] = total.astype(BF16)
+
+    def drain(self, t):
+        q, s = t // (self.side - 1), lax.rem(t, self.side - 1)
+        self.turn_hop(q, s, self.slot2.at[t]).wait_send()
+        for j in range(self.side):
+            self.hop(q, s, j, self.slot1.at[t * self.side + j]).wait_send()
+
+
+def reduce_kernel(n, r_dims, *refs):
+    m = len(r_dims)
+    lefts, rights, outs = refs[:m], refs[m:2 * m], refs[2 * m:3 * m]
+    rest = refs[3 * m:]
+    each = len(rest) // m
+    todo = [
+        Reduction(n, r_dims[i], lefts[i], rights[i], outs[i], rest[i * each:(i + 1) * each]) for i in range(m)
+    ]
+    side = todo[0].side
+    greet_neighbours(n)
+    for job in todo:
+        for copy in job.swap:
+            copy.start()
+    for job in todo:
+        for copy in job.swap:
+            copy.wait()
+        loop(2, [job.start_step])
+    loop(4 * side * (side - 2), [job.middle_round for job in todo])
+    loop(4, [job.turn_first for job in todo])
+    loop(4 * (side - 2), [job.turn_round for job in todo])
+    loop(4, [job.turn_last for job in todo])
+    loop(4 * (side - 1), [job.drain for job in todo])
+
+
+def loop(count, bodies):
+    def step(t, _):
+        for body in bodies:
+            body(t)
+        return 0
+
+    lax.fori_loop(0, count, step, 0)
+
+
+def matmul_reduce_scatter(n, jobs, collective_id):
     chips = n // 2
     side = math.isqrt(chips)
-    tb = t // n
     hops = 4 * (side - 1)
     vmem = pl.BlockSpec(memory_space=pltpu.VMEM)
+    lefts, rights, outs, scratch = [], [], [], []
+    for left, right, r_dim in jobs:
+        t, k = left.shape
+        f, tb = right.shape[1 - r_dim], t // n
+        lefts.append(left.reshape(side, side, 2, tb, k))
+        rights.append(right)
+        outs.append(jax.ShapeDtypeStruct((tb, f), BF16))
+        piece = (tb, f // 4)
+        scratch += [
+            pltpu.VMEM((side, side, tb, k), BF16), pltpu.VMEM(right.shape, BF16), pltpu.VMEM((2, 4, side, *piece), F32),
+            pltpu.VMEM((4 * side, *piece), BF16), pltpu.VMEM((hops * side, *piece), BF16), pltpu.VMEM((hops, *piece), BF16),
+        ] + [pltpu.SemaphoreType.DMA((c,)) for c in (hops * side, hops * side, hops, hops, 2, 2)]
     return pl.pallas_call(
-        functools.partial(reduce_kernel, n, r_dim),
-        out_shape=jax.ShapeDtypeStruct((tb, f), BF16),
-        in_specs=[vmem, vmem],
-        out_specs=vmem,
-        scratch_shapes=[
-            pltpu.VMEM((side, side, tb, k), BF16),
-            pltpu.VMEM(right.shape, BF16),
-            pltpu.VMEM((2, 4, side, tb, f // 4), F32),
-            pltpu.VMEM((4 * side, tb, f // 4), BF16),
-            pltpu.VMEM((hops * side, tb, f // 4), BF16),
-            pltpu.VMEM((hops, tb, f // 4), BF16),
-            pltpu.SemaphoreType.DMA((hops * side,)), pltpu.SemaphoreType.DMA((hops * side,)),
-            pltpu.SemaphoreType.DMA((hops,)), pltpu.SemaphoreType.DMA((hops,)),
-            pltpu.SemaphoreType.DMA((2,)), pltpu.SemaphoreType.DMA((2,)),
-        ],
-        compiler_params=pltpu.CompilerParams(collective_id=collective_id, has_side_effects=True, vmem_limit_bytes=48 * 1024 * 1024),
-        cost_estimate=pl.CostEstimate(flops=40_000_000_000, bytes_accessed=4 * t * k, transcendentals=0),
-    )(left.reshape(side, side, 2, tb, k), right)
+        functools.partial(reduce_kernel, n, [r_dim for _, _, r_dim in jobs]),
+        out_shape=outs,
+        in_specs=[vmem] * (2 * len(jobs)),
+        out_specs=[vmem] * len(jobs),
+        scratch_shapes=scratch,
+        compiler_params=pltpu.CompilerParams(collective_id=collective_id, has_side_effects=True, vmem_limit_bytes=VMEM_LIMIT),
+        cost_estimate=cost(40_000_000_000, 4 * t * k),
+    )(*lefts, *rights)
 
 
 def gelu_parts(up):
@@ -643,7 +670,7 @@
             *sems, pltpu.SemaphoreType.DMA,
         ],
         compiler_params=pltpu.CompilerParams(collective_id=collective_id, has_side_effects=True, vmem_limit_bytes=50 * 1024 * 1024),
-        cost_estimate=pl.CostEstimate(flops=40_000_000_000, bytes_accessed=4 * n * tb * h, transcendentals=0),
+        cost_estimate=cost(40_000_000_000, 4 * n * tb * h),
         name='gather_mlp',
     )(own, w_up, w_down, dy.reshape(n // 4, 4 * tb, h))
 
@@ -659,7 +686,7 @@
         copy_kernel, grid=(n // per,),
         in_specs=[pl.BlockSpec((per, 1, tb, h), lambda i: (i, half, 0, 0))], out_specs=pl.BlockSpec((per * tb, h), lambda i: (i, 0)),
         out_shape=jax.ShapeDtypeStruct((n * tb, h), pair.dtype),
-        cost_estimate=pl.CostEstimate(flops=10_000_000, bytes_accessed=4 * n * tb * h, transcendentals=0),
+        cost_estimate=cost(10_000_000, 4 * n * tb * h),
     )(pair)
 
 
@@ -685,10 +712,10 @@
     return pl.pallas_call(
         out_grad_kernel, grid=(n // per,),
         in_specs=[pl.BlockSpec((hd, per * tb), lambda i: (0, i)), pl.BlockSpec((per, 1, tb, h), lambda i: (i, half, 0, 0))],
-        out_specs=pl.BlockSpec((hd, h), lambda i: (0, 0)),
+        out_specs=pl.BlockSpec((hd, h), zero_map),
         out_shape=jax.ShapeDtypeStruct((hd, h), BF16),
         scratch_shapes=[pltpu.VMEM((hd, h), F32)],
-        cost_estimate=pl.CostEstimate(flops=2 * n * tb * h * hd, bytes_accessed=2 * n * tb * h, transcendentals=0), name='out_grad',
+        cost_estimate=cost(2 * n * tb * h * hd, 2 * n * tb * h), name='out_grad',
     )(ot, pair)
 
 
@@ -737,7 +764,7 @@
         in_specs=[vmem], out_specs=vmem,
         scratch_shapes=[pltpu.VMEM((n, *piece), F32), pltpu.VMEM(piece, F32)] + [pltpu.SemaphoreType.DMA((n,))] * 4,
         compiler_params=pltpu.CompilerParams(collective_id=collective_id, has_side_effects=True),
-        cost_estimate=pl.CostEstimate(flops=1_000_000_000, bytes_accessed=value.size * 8, transcendentals=0),
+        cost_estimate=cost(1_000_000_000, value.size * 8),
         name='gain_sums',
     )(value.reshape(n, *piece)).reshape(value.shape)
 
@@ -790,14 +817,11 @@
         resid = (x_s.astype(F32) + proj).astype(BF16)
         b1_s, hat_two, rstd_two = ln_rows(resid, gain_two)
         b1, gelu_out, d_up = (z.reshape(t, z.shape[-1]) for z in gather_mlp(n, b1_s, w_up, w_down, dy, 6))
-        d_b1 = matmul_reduce_scatter(n, d_up, w_up, 1, 3)
-        late_gelu, d_b1 = lax.optimization_barrier((gelu_out, d_b1))
+        d_b1, part_two = matmul_reduce_scatter(n, [(d_up, w_up, 1), (gelu_out, w_down, 0)], 3)
         d_ln, d_gain_two = ln_back(d_b1, hat_two, rstd_two, gain_two)
         d_resid_s = dy_s + d_ln
-        part_two = matmul_reduce_scatter(n, late_gelu, w_down, 0, 4)
-        late_gelu, late_up, part_two = lax.optimization_barrier((late_gelu, d_up, part_two))
-        d_w_down = mm(late_gelu, dy, 0, 0).astype(BF16)
-        d_w_up = mm(b1, late_up, 0, 0).astype(BF16)
+        d_w_down = mm(gelu_out, dy, 0, 0).astype(BF16)
+        d_w_up = mm(b1, d_up, 0, 0).astype(BF16)
 
         y_s = (resid.astype(F32) + part_two.astype(F32)).astype(BF16)
         pair = lax.all_gather(jnp.stack([y_s, d_resid_s]), 'model', axis=0, tiled=True).reshape(n, 2, ts, h)
@@ -806,7 +830,7 @@
         dot = exchange(n, d_heads, (hd, t), leading, column_block(ts), 1)
 
         d_qkv = attention_backward(q, k, v, qkvt, ot, dot, lse, start_row, tab, bq, bk)
-        d_norm = matmul_reduce_scatter(n, d_qkv, w_qkv.T, 0, 5)
+        (d_norm,) = matmul_reduce_scatter(n, [(d_qkv, w_qkv.T, 0)], 5)
         d_w_qkv = mm(a_full, d_qkv, 0, 0).astype(BF16)
         d_w_out = out_grad(ot, pair, 1)
 

time: 599 us -> 591 us (0.987)
  Pallas kernels: 366 us -> 357 us
    pallas_call x3 -> x2, Pallas kernels: 172 us -> 162 us  [matmul_reduce_scatter(): pl.pallas_call(functools.partial(reduce_kernel, n, [r_dim for _, _, r_dim...]
    unnamed x37 -> x25, local copies, waits for them, and re-layouts: 17.4 us -> 14.2 us
where the time goes in v6:
time: 591 us; the launch traced here: 581 us
  Pallas kernels  357 us (60%)
  waiting for transfers between devices  133 us (23%)
  matrix products  37.4 us (6%)
  other arithmetic  19.5 us (3%)
  local copies, waits for them, and re-layouts  18.6 us (3%)
  between operations  14.4 us (2%)
    pallas_call x2, Pallas kernels, matmul_reduce_scatter(): pl.pallas_call(functools.partial(reduce_kernel, n, [r_dim for _, _, r_dim...  162 us
    all_gather x1, waiting for transfers between devices, layer(): lax.all_gather(jnp.stack([y_s, d_resid_s]), 'model', axis=0, tiled=True)  110 us
    pallas_call x1, Pallas kernels, gather_mlp(): pl.pallas_call(functools.partial(gather_mlp_kernel, n), out_shape=[jax.Sh...  61 us
    dot_general x5, matrix products, mm(): lax.dot_general(a, b, (((ca,), (cb,)), ((), ())), preferred_element_type=...  37.4 us
    pallas_call x2, Pallas kernels, exchange(): pl.pallas_call(functools.partial(exchange_kernel, n, src_of, dst_of), out...  35.9 us
    all_gather x1, waiting for transfers between devices, layer(): d_x = lax.all_gather((d_resid_s + d_ln)[None], 'model', axis=1, tiled=True)  22.3 us
    pallas_call x1, Pallas kernels, attention_backward(): pl.pallas_call(functools.partial(attn_bwd_kernel, bk), grid_spec=pltpu.Pr...  21.1 us
    pallas_call x1, Pallas kernels, ln_qkv(): pl.pallas_call(ln_qkv_kernel, grid=(t // bt,), in_specs=[row(h), pl.Block...  20.7 us
  transfers between devices with their start and end apart: 3, of which 2 were waited for; matrix products, arithmetic and copies ran while one was open for 7% of the time, Pallas kernels for 12%

profile of v6, /device:TPU:97, one launch (start us, length us, event | category | flops | bytes accessed | tf_op | source)
XLA Modules:
  0.0 580.7 jit_solution(13251791471937151416)
XLA Ops:
  8.0 1.3 convert_element_type.74
  9.3 1.3 reshape.418.g_ref
  10.6 1.2 slice.33
  12.5 1.5 add_select_fusion
  15.1 1.2 convert_reduce_fusion
  17.2 1.3 fusion.22
  19.2 20.7 %ln_qkv.1 = (bf16[4096,2048]{1,0:T(8,128)(2,1)}, bf16[4096,64]{1,0:T(8,128)(2,1)}, bf16[4096,64]{1,0:T(8,128)(2,1)}, bf16[4096,64]{1,0:T(8,128)(2,1)}, bf16[192,4096]{1,0:T(8,128)(2,1)}) custom-call(bf16[4096,2048]{1,0:T(8,128)(2,1)} %bitcast.117, bf16[1,2048]{1,0:T(2,128)(2,1)} %reshape.418.g_ref, bf16[192,2048]{1,0:T(8,128)(2,1)} %bitcast.123), custom_call_target="tpu_custom_call" | custom-call | flops 3388997632 | bytes 33554432 | tf_op jit(solution)/shard_map/ln_qkv/pallas_call | solution.py:55
  39.9 14.3 %attn_fwd.1 = (bf16[64,4096]{1,0:T(8,128)(2,1)}, f32[1,4096]{1,0:T(1,128)}) custom-call(s32[4,8]{1,0:T(4,128)} %pad_add_fusion.tab_ref, bf16[4096,64]{1,0:T(8,128)(2,1)} %get-tuple-element.20.k_ref, bf16[192,4096]{1,0:T(8,128)(2,1)} %get-tuple-element.21.qt_ref.vt_ref.t_ref, bf16[192,4096]{1,0:T(8,128)(2,1)} %get-tuple-element.21.qt_ref.vt_ref.t_ref, ...), custom_call_target="tpu_custom_call" | custom-call | flops 17179869184 | bytes 2097152 | tf_op jit(solution)/shard_map/attn_fwd/pallas_call | solution.py:134
  54.2 19.0 %shard_map.152 = bf16[32,64,128]{2,1,0:T(8,128)(2,1)} custom-call(bf16[64,4096]{1,0:T(8,128)(2,1)} %get-tuple-element.22.in_ref.ot_ref), custom_call_target="tpu_custom_call" | custom-call | flops 2000000000 | bytes 1048576 | tf_op jit(solution)/shard_map/pallas_call | solution.py:265
  73.7 5.1 fusion.35
  79.3 61.0 %gather_mlp.1 = (bf16[4,4,2,128,2048]{4,3,2,1,0:T(8,128)(2,1)}, bf16[8,512,256]{2,1,0:T(8,128)(2,1)}, bf16[8,512,256]{2,1,0:T(8,128)(2,1)}) custom-call(bf16[128,2048]{1,0:T(8,128)(2,1)S(1)} %multiply_convert_fusion.own_ref, bf16[2048,256]{1,0:T(8,128)(2,1)S(1)} %copy-done, bf16[256,2048]{1,0:T(8,128)(2,1)S(1)} %copy-done.1, bf16[8,512,2048]{2,1,0:T(8,128)(2,1)} %bitcast.114), custom_call_target="tpu_custom_call" | custom-call | flops 40000000000 | bytes 33554432 | tf_op jit(solution)/shard_map/gather_mlp/pallas_call | solution.py:660
  140.3 103.6 %shard_map.153 = (bf16[128,2048]{1,0:T(8,128)(2,1)}, bf16[128,2048]{1,0:T(8,128)(2,1)}) custom-call(bf16[4,4,2,128,256]{4,3,2,1,0:T(8,128)(2,1)} %bitcast.136, bf16[4,4,2,128,256]{4,3,2,1,0:T(8,128)(2,1)} %bitcast.121, bf16[2048,256]{1,0:T(8,128)(2,1)} %refs_2_.1, bf16[256,2048]{1,0:T(8,128)(2,1)} %refs_3_.1), custom_call_target="tpu_custom_call" | custom-call | flops 40000000000 | bytes 4194304 | tf_op jit(solution)/shard_map/pallas_call | solution.py:478
  244.0 1.7 fusion.27
  245.7 1.7 fusion.31
  247.5 6.3 %fusion.8 = bf16[2048,128]{0,1:T(8,128)(2,1)S(1)} fusion(bf16[128,2048]{1,0:T(8,128)(2,1)S(1)} %fusion.31, bf16[2048,2048]{1,0:T(8,128)(2,1)} %bitcast.113), kind=kOutput, calls=%fused_computation.10 | convolution fusion | flops 1074003968 | bytes 9437184 | tf_op jit(solution)/shard_map/dot_general | solution.py:22
  253.7 1.0 copy.35
  254.7 17.0 %shard_map.155.dot_ref = bf16[64,4096]{1,0:T(8,128)(2,1)} custom-call(bf16[32,64,128]{2,1,0:T(8,128)(2,1)} %bitcast.125), custom_call_target="tpu_custom_call" | custom-call | flops 2000000000 | bytes 1048576 | tf_op jit(solution)/shard_map/pallas_call | solution.py:265
  271.7 21.1 %attn_bwd.1 = bf16[4096,192]{1,0:T(8,128)(2,1)} custom-call(s32[4,8]{1,0:T(4,128)} %pad_add_fusion.tab_ref, bf16[4096,64]{1,0:T(8,128)(2,1)} %get-tuple-element.27.q_ref, bf16[4096,64]{1,0:T(8,128)(2,1)} %get-tuple-element.20.k_ref, bf16[4096,64]{1,0:T(8,128)(2,1)} %get-tuple-element.28.v_ref, bf16[192,4096]{1,0:T(8,128)(2,1)} %get-tuple-element.21.qt_ref.vt_ref.t_ref, ...), custom_call_target="tpu_custom_call" | custom-call | flops 42949672960 | bytes 4194304 | tf_op jit(solution)/shard_map/attn_bwd/pallas_call | solution.py:209
  292.8 58.8 %shard_map.156 = bf16[128,2048]{1,0:T(8,128)(2,1)} custom-call(bf16[4,4,2,128,192]{4,3,2,1,0:T(8,128)(2,1)} %bitcast.138, bf16[192,2048]{1,0:T(8,128)(2,1)} %bitcast.124), custom_call_target="tpu_custom_call" | custom-call | flops 40000000000 | bytes 3145728 | tf_op jit(solution)/shard_map/pallas_call | solution.py:478
  351.7 1.7 fusion.29
  353.4 2.6 fusion.32
  356.1 1.1 pad_maximum_fusion
  357.8 17.7 %gain_sums.1 = f32[32,1,128]{2,1,0:T(1,128)} custom-call(f32[32,1,128]{2,1,0:T(1,128)} %pad_maximum_fusion.1.in_ref), custom_call_target="tpu_custom_call" | custom-call | flops 1000000000 | bytes 32768 | tf_op jit(solution)/shard_map/gain_sums/pallas_call | solution.py:761
  375.6 0.7 convert_element_type.79
  377.0 10.8 %convolution_convert_fusion.1 = bf16[2048,192]{0,1:T(8,128)(2,1)} fusion(bf16[4096,2048]{1,0:T(8,128)(2,1)} %get-tuple-element.30, bf16[4096,192]{1,0:T(8,128)(2,1)} %attn_bwd.1), kind=kOutput, calls=%fused_computation.4 | convolution fusion | flops 3221618688 | bytes 19136512 | tf_op jit(solution)/shard_map/dot_general | solution.py:22
  387.8 9.8 %convolution_convert_fusion = bf16[2048,256]{1,0:T(8,128)(2,1)} fusion(bf16[4096,2048]{1,0:T(8,128)(2,1)} %bitcast.135, bf16[4096,256]{1,0:T(8,128)(2,1)S(1)} %bitcast.137), kind=kOutput, calls=%fused_computation.3 | convolution fusion | flops 4295491584 | bytes 19922944 | tf_op jit(solution)/shard_map/dot_general | solution.py:22
  397.6 5.5 fusion.2
  403.1 22.3 %all-gather.9.cloned.1.call-done = bf16[4096,2048]{1,0:T(8,128)(2,1)} async-done(((bf16[128,2048]{1,0:T(8,128)(2,1)}), bf16[4096,2048]{1,0:T(8,128)(2,1)}) %all-gather.9.cloned.1.call-update) | async-done | bytes 16777232 | tf_op jit(solution)/shard_map/all_gather | solution.py:839
  425.4 110.1 %all-gather.7.cloned.1.call-done = bf16[64,128,2048]{2,1,0:T(8,128)(2,1)} async-done(((bf16[2,128,2048]{2,1,0:T(8,128)(2,1)}), bf16[64,128,2048]{2,1,0:T(8,128)(2,1)}) %all-gather.7.cloned.1.call-update) | async-done | bytes 33554448 | tf_op jit(solution)/shard_map/all_gather | solution.py:827
  535.5 10.3 %out_grad.1 = bf16[64,2048]{1,0:T(8,128)(2,1)} custom-call(bf16[64,4096]{1,0:T(8,128)(2,1)} %get-tuple-element.22.in_ref.ot_ref, bf16[32,2,128,2048]{3,2,1,0:T(8,128)(2,1)} %bitcast.111), custom_call_target="tpu_custom_call" | custom-call | flops 1073741824 | bytes 16777216 | tf_op jit(solution)/shard_map/out_grad/pallas_call | solution.py:712
  545.8 13.8 %shard_map.154 = bf16[4096,2048]{1,0:T(8,128)(2,1)} custom-call(bf16[32,2,128,2048]{3,2,1,0:T(8,128)(2,1)} %bitcast.112), custom_call_target="tpu_custom_call" | custom-call | flops 10000000 | bytes 33554432 | tf_op jit(solution)/shard_map/pallas_call | solution.py:685
  559.6 14.2 %copy.37 = bf16[1,4096,2048]{2,1,0:T(8,128)(2,1)} copy(bf16[1,4096,2048]{2,1,0:T(8,128)(2,1)} %bitcast.119) | data formatting | bytes 33554432
  (58 shorter events, 6.7 us)
Async XLA Ops:
  7.2 66.6 %all-gather.5.cloned.1.call-start = ((), (), s32[]{:S(2)}) async-start(), calls=%async_computation | async-start | bytes 8650752 | tf_op jit(solution)/shard_map/all_gather | solution.py:804
  8.0 417.4 %all-gather.9.cloned.1.call-start = ((), (), s32[]{:S(2)}) async-start(), calls=%async_computation.2 | async-start | bytes 17301504 | tf_op jit(solution)/shard_map/all_gather | solution.py:839
  17.2 22.7 %copy-start.4 = (f32[128]{0:T(128)}, f32[128]{0:T(128)S(1)}, u32[]{:S(2)}) copy-start(f32[128]{0:T(128)S(1)} %broadcast_multiply_fusion.2) | copy-start | bytes 1540
  73.7 5.6 copy-start
  73.7 5.6 copy-start.1
  292.8 58.8 %copy-start.3 = (f32[2048]{0:T(1024)S(1)}, f32[2048]{0:T(1024)}, u32[]{:S(2)}) copy-start(f32[2048]{0:T(1024)} %convert_element_type.74) | copy-start | bytes 24580
  292.8 58.9 %copy-start.5 = (f32[128]{0:T(128)S(1)}, f32[128]{0:T(128)}, u32[]{:S(2)}) copy-start(f32[128]{0:T(128)} %copy-done.4) | copy-start | bytes 1540
  292.8 58.9 %copy-start.6 = (f32[128]{0:T(128)S(1)}, f32[128]{0:T(128)}, u32[]{:S(2)}) copy-start(f32[128]{0:T(128)} %add_rsqrt_fusion) | copy-start | bytes 1540
  356.0 179.6 %all-gather.7.cloned.1.call-start = ((), (), s32[]{:S(2)}) async-start(), calls=%async_computation.1 | async-start | bytes 34603008 | tf_op jit(solution)/shard_map/all_gather | solution.py:827
  377.0 10.9 %copy-start.7 = (bf16[8,512,256]{2,1,0:T(8,128)(2,1)S(1)}, bf16[8,512,256]{2,1,0:T(8,128)(2,1)}, u32[]{:S(2)}) copy-start(bf16[8,512,256]{2,1,0:T(8,128)(2,1)} %get-tuple-element.23) | copy-start | bytes 6291460
  377.0 20.7 %slice-start = ((s8[16777216]{0:T(1024)(128)(4,1)}), s8[4194304]{0:T(1024)(128)(4,1)S(1)}, s32[]{:S(2)}) async-start(s8[16777216]{0:T(1024)(128)(4,1)} %bitcast.115), calls=%async_computation.3 | async-start | bytes 8388608
  377.0 20.7 %slice-start.1 = ((s8[16777216]{0:T(1024)(128)(4,1)}), s8[4194304]{0:T(1024)(128)(4,1)S(1)}, s32[]{:S(2)}) async-start(s8[16777216]{0:T(1024)(128)(4,1)} %bitcast.115), calls=%async_computation.4 | async-start | bytes 8388608
  387.8 9.8 %slice-start.2 = ((s8[16777216]{0:T(1024)(128)(4,1)}), s8[4194304]{0:T(1024)(128)(4,1)S(1)}, s32[]{:S(2)}) async-start(s8[16777216]{0:T(1024)(128)(4,1)} %bitcast.115), calls=%async_computation.5 | async-start | bytes 8388608
  387.8 9.8 %slice-start.3 = ((s8[16777216]{0:T(1024)(128)(4,1)}), s8[4194304]{0:T(1024)(128)(4,1)S(1)}, s32[]{:S(2)}) async-start(s8[16777216]{0:T(1024)(128)(4,1)} %bitcast.115), calls=%async_computation.6 | async-start | bytes 8388608
  387.8 9.8 %copy-start.2 = (bf16[8,512,256]{2,1,0:T(8,128)(2,1)S(1)}, bf16[8,512,256]{2,1,0:T(8,128)(2,1)}, u32[]{:S(2)}) copy-start(bf16[8,512,256]{2,1,0:T(8,128)(2,1)} %get-tuple-element.24) | copy-start | bytes 6291460
Sparse Core Ops, SparseCore 0:
  10.1 51.9 all-gather.4
  356.1 69.2 all-gather.8
  427.5 108.0 all-gather.6

commit v7 on v6

--- a/solution.py
+++ b/solution.py
@@ -50,7 +50,7 @@
     t, h = x.shape
     c = w.shape[0]
     hd = c // 3
-    bt = min(512, t)
+    bt = min(256, t)
     row = lambda n: pl.BlockSpec((bt, n), lambda i: (i, 0))
     return pl.pallas_call(
         ln_qkv_kernel,
@@ -367,31 +367,27 @@
     def arrived(self, q, s, j):
         return (q * (self.side - 1) + s) * self.side + j
 
-    def start_step(self, s):
-        for q in range(4):
-            self.group(s, q)
-
-            @pl.when(s == 0)
-            def _():
-                def start_round(j, _):
-                    src = self.first.at[q * self.side + j]
-                    src[...] = self.own_part(q, 0, j).astype(BF16)
-                    self.hop(q, 0, j, src).start()
-                    return 0
-
-                lax.fori_loop(0, self.side, start_round, 0)
-
     def received(self, q, s, j):
         slot = self.slot1.at[self.arrived(q, s - 1, j)]
         self.hop(q, s - 1, j, slot).wait_recv()
         return slot, slot[...].astype(F32) + self.own_part(q, s, j)
 
     def middle_round(self, t):
-        s, rest = 1 + t // (4 * self.side), lax.rem(t, 4 * self.side)
+        s, rest = t // (4 * self.side) - 1, lax.rem(t, 4 * self.side)
         j, q = rest // 4, lax.rem(rest, 4)
-        slot, total = self.received(q, s, j)
-        slot[...] = total.astype(BF16)
-        self.hop(q, s, j, slot).start()
+
+        @pl.when(s == 0)
+        def _():
+            src = self.first.at[q * self.side + j]
+            src[...] = self.own_part(q, s, j).astype(BF16)
+            self.hop(q, s, j, src).start()
+
+        @pl.when(s > 0)
+        def _():
+            slot, total = self.received(q, s, j)
+            slot[...] = total.astype(BF16)
+            self.hop(q, s, j, slot).start()
+
         for ahead in range(4):
             @pl.when((q == 3) & (j == ahead))
             def _():
@@ -441,8 +437,7 @@
     for job in todo:
         for copy in job.swap:
             copy.wait()
-        loop(2, [job.start_step])
-    loop(4 * side * (side - 2), [job.middle_round for job in todo])
+    loop(4 * side * side, [job.middle_round for job in todo])
     loop(4, [job.turn_first for job in todo])
     loop(4 * (side - 2), [job.turn_round for job in todo])
     loop(4, [job.turn_last for job in todo])
@@ -594,7 +589,7 @@
             def _():
                 along_a(q, j, src).start()
 
-        @pl.when(s > 0)
+        @pl.when((s > 0) & (s < side))
         def _():
             along_b(q, r - side, src).wait_recv()
 
@@ -602,21 +597,22 @@
         def _():
             along_b(q, r, src).start()
 
-        across(q, r, src, my_core).start()
+        @pl.when(s < side)
+        def _():
+            across(q, r, src, my_core).start()
+
         for late in range(4):
             @pl.when((q == 3) & (j == late) & (s > 0))
             def _():
                 take_step(s - 1, late)
 
-        @pl.when((q == 1) & (lax.rem(r, 2) == 1))
+        @pl.when((q == 1) & (lax.rem(r, 2) == 1) & (s < side))
         def _():
             back_proj(r // 2)
 
         return 0
 
-    lax.fori_loop(4, 4 * rounds, main_round, 0)
-    for q in range(4):
-        take_step(jnp.int32(side - 1), q)
+    lax.fori_loop(4, 4 * (rounds + side), main_round, 0)
 
     def activate(t, _):
         chip, core = t // 2, lax.rem(t, 2)
@@ -681,7 +677,7 @@
 
 def copy_half(pair, half):
     n, _, tb, h = pair.shape
-    per = min(4, n)
+    per = min(2, n)
     return pl.pallas_call(
         copy_kernel, grid=(n // per,),
         in_specs=[pl.BlockSpec((per, 1, tb, h), lambda i: (i, half, 0, 0))], out_specs=pl.BlockSpec((per * tb, h), lambda i: (i, 0)),
@@ -708,7 +704,7 @@
 def out_grad(ot, pair, half):
     n, _, tb, h = pair.shape
     hd = ot.shape[0]
-    per = min(4, n)
+    per = min(2, n)
     return pl.pallas_call(
         out_grad_kernel, grid=(n // per,),
         in_specs=[pl.BlockSpec((hd, per * tb), lambda i: (0, i)), pl.BlockSpec((per, 1, tb, h), lambda i: (i, half, 0, 0))],

time: 591 us -> 602 us (1.019); the launches traced: 581 us -> 600 us
  Pallas kernels: 357 us -> 377 us
    pallas_call x2, Pallas kernels: 162 us -> 170 us  [matmul_reduce_scatter(): pl.pallas_call(functools.partial(reduce_kernel, n, [r_dim for _, _, r_dim...]
  transfers between devices with their start and end apart: 3 -> 3, of which waited for: 2 -> 2; matrix products, arithmetic and copies ran while one was open for 7% -> 7% of each run, Pallas kernels for 12% -> 13%
where the time goes in v7:
time: 602 us; the launch traced here: 600 us
  Pallas kernels  377 us (63%)
  waiting for transfers between devices  133 us (22%)
  matrix products  37.4 us (6%)
  other arithmetic  19.5 us (3%)
  local copies, waits for them, and re-layouts  18.6 us (3%)
  between operations  14 us (2%)
    pallas_call x2, Pallas kernels, matmul_reduce_scatter(): pl.pallas_call(functools.partial(reduce_kernel, n, [r_dim for _, _, r_dim...  170 us
    all_gather x1, waiting for transfers between devices, layer(): lax.all_gather(jnp.stack([y_s, d_resid_s]), 'model', axis=0, tiled=True)  110 us
    pallas_call x1, Pallas kernels, gather_mlp(): pl.pallas_call(functools.partial(gather_mlp_kernel, n), out_shape=[jax.Sh...  62.4 us
    dot_general x5, matrix products, mm(): lax.dot_general(a, b, (((ca,), (cb,)), ((), ())), preferred_element_type=...  37.4 us
    pallas_call x2, Pallas kernels, exchange(): pl.pallas_call(functools.partial(exchange_kernel, n, src_of, dst_of), out...  35.7 us
    pallas_call x1, Pallas kernels, ln_qkv(): pl.pallas_call(ln_qkv_kernel, grid=(t // bt,), in_specs=[row(h), pl.Block...  24.6 us
    all_gather x1, waiting for transfers between devices, layer(): d_x = lax.all_gather((d_resid_s + d_ln)[None], 'model', axis=1, tiled=True)  22.4 us
    pallas_call x1, Pallas kernels, attention_backward(): pl.pallas_call(functools.partial(attn_bwd_kernel, bk), grid_spec=pltpu.Pr...  21.1 us
  transfers between devices with their start and end apart: 3, of which 2 were waited for; matrix products, arithmetic and copies ran while one was open for 7% of the time, Pallas kernels for 13%

profile of v7, /device:TPU:97, one launch (start us, length us, event | category | flops | bytes accessed | tf_op | source)
XLA Modules:
  0.0 599.9 jit_solution(17809598035132800971)
XLA Ops:
  8.0 1.3 convert_element_type.74
  9.3 1.3 reshape.418.g_ref
  10.6 1.2 slice.33
  12.5 1.5 add_select_fusion
  15.1 1.2 convert_reduce_fusion
  17.2 1.3 fusion.22
  19.2 24.6 %ln_qkv.1 = (bf16[4096,2048]{1,0:T(8,128)(2,1)}, bf16[4096,64]{1,0:T(8,128)(2,1)}, bf16[4096,64]{1,0:T(8,128)(2,1)}, bf16[4096,64]{1,0:T(8,128)(2,1)}, bf16[192,4096]{1,0:T(8,128)(2,1)}) custom-call(bf16[4096,2048]{1,0:T(8,128)(2,1)} %bitcast.117, bf16[1,2048]{1,0:T(2,128)(2,1)} %reshape.418.g_ref, bf16[192,2048]{1,0:T(8,128)(2,1)} %bitcast.123), custom_call_target="tpu_custom_call" | custom-call | flops 3388997632 | bytes 33554432 | tf_op jit(solution)/shard_map/ln_qkv/pallas_call | solution.py:55
  43.8 14.5 %attn_fwd.1 = (bf16[64,4096]{1,0:T(8,128)(2,1)}, f32[1,4096]{1,0:T(1,128)}) custom-call(s32[4,8]{1,0:T(4,128)} %pad_add_fusion.tab_ref, bf16[4096,64]{1,0:T(8,128)(2,1)} %get-tuple-element.20.k_ref, bf16[192,4096]{1,0:T(8,128)(2,1)} %get-tuple-element.21.qt_ref.vt_ref.t_ref, bf16[192,4096]{1,0:T(8,128)(2,1)} %get-tuple-element.21.qt_ref.vt_ref.t_ref, ...), custom_call_target="tpu_custom_call" | custom-call | flops 17179869184 | bytes 2097152 | tf_op jit(solution)/shard_map/attn_fwd/pallas_call | solution.py:134
  58.3 18.9 %shard_map.152 = bf16[32,64,128]{2,1,0:T(8,128)(2,1)} custom-call(bf16[64,4096]{1,0:T(8,128)(2,1)} %get-tuple-element.22.in_ref.ot_ref), custom_call_target="tpu_custom_call" | custom-call | flops 2000000000 | bytes 1048576 | tf_op jit(solution)/shard_map/pallas_call | solution.py:265
  77.7 5.1 fusion.35
  83.3 62.4 %gather_mlp.1 = (bf16[4,4,2,128,2048]{4,3,2,1,0:T(8,128)(2,1)}, bf16[8,512,256]{2,1,0:T(8,128)(2,1)}, bf16[8,512,256]{2,1,0:T(8,128)(2,1)}) custom-call(bf16[128,2048]{1,0:T(8,128)(2,1)S(1)} %multiply_convert_fusion.own_ref, bf16[2048,256]{1,0:T(8,128)(2,1)S(1)} %copy-done, bf16[256,2048]{1,0:T(8,128)(2,1)S(1)} %copy-done.1, bf16[8,512,2048]{2,1,0:T(8,128)(2,1)} %bitcast.114), custom_call_target="tpu_custom_call" | custom-call | flops 40000000000 | bytes 33554432 | tf_op jit(solution)/shard_map/gather_mlp/pallas_call | solution.py:656
  145.7 110.1 %shard_map.153 = (bf16[128,2048]{1,0:T(8,128)(2,1)}, bf16[128,2048]{1,0:T(8,128)(2,1)}) custom-call(bf16[4,4,2,128,256]{4,3,2,1,0:T(8,128)(2,1)} %bitcast.136, bf16[4,4,2,128,256]{4,3,2,1,0:T(8,128)(2,1)} %bitcast.121, bf16[2048,256]{1,0:T(8,128)(2,1)} %refs_2_.1, bf16[256,2048]{1,0:T(8,128)(2,1)} %refs_3_.1), custom_call_target="tpu_custom_call" | custom-call | flops 40000000000 | bytes 4194304 | tf_op jit(solution)/shard_map/pallas_call | solution.py:473
  255.9 1.7 fusion.27
  257.6 1.7 fusion.31
  259.3 6.3 %fusion.8 = bf16[2048,128]{0,1:T(8,128)(2,1)S(1)} fusion(bf16[128,2048]{1,0:T(8,128)(2,1)S(1)} %fusion.31, bf16[2048,2048]{1,0:T(8,128)(2,1)} %bitcast.113), kind=kOutput, calls=%fused_computation.10 | convolution fusion | flops 1074003968 | bytes 9437184 | tf_op jit(solution)/shard_map/dot_general | solution.py:22
  265.6 1.0 copy.35
  266.6 16.8 %shard_map.155.dot_ref = bf16[64,4096]{1,0:T(8,128)(2,1)} custom-call(bf16[32,64,128]{2,1,0:T(8,128)(2,1)} %bitcast.125), custom_call_target="tpu_custom_call" | custom-call | flops 2000000000 | bytes 1048576 | tf_op jit(solution)/shard_map/pallas_call | solution.py:265
  283.5 21.1 %attn_bwd.1 = bf16[4096,192]{1,0:T(8,128)(2,1)} custom-call(s32[4,8]{1,0:T(4,128)} %pad_add_fusion.tab_ref, bf16[4096,64]{1,0:T(8,128)(2,1)} %get-tuple-element.27.q_ref, bf16[4096,64]{1,0:T(8,128)(2,1)} %get-tuple-element.20.k_ref, bf16[4096,64]{1,0:T(8,128)(2,1)} %get-tuple-element.28.v_ref, bf16[192,4096]{1,0:T(8,128)(2,1)} %get-tuple-element.21.qt_ref.vt_ref.t_ref, ...), custom_call_target="tpu_custom_call" | custom-call | flops 42949672960 | bytes 4194304 | tf_op jit(solution)/shard_map/attn_bwd/pallas_call | solution.py:209
  304.6 59.7 %shard_map.156 = bf16[128,2048]{1,0:T(8,128)(2,1)} custom-call(bf16[4,4,2,128,192]{4,3,2,1,0:T(8,128)(2,1)} %bitcast.138, bf16[192,2048]{1,0:T(8,128)(2,1)} %bitcast.124), custom_call_target="tpu_custom_call" | custom-call | flops 40000000000 | bytes 3145728 | tf_op jit(solution)/shard_map/pallas_call | solution.py:473
  364.3 1.7 fusion.29
  366.0 2.6 fusion.32
  368.7 1.1 pad_maximum_fusion
  370.4 17.2 %gain_sums.1 = f32[32,1,128]{2,1,0:T(1,128)} custom-call(f32[32,1,128]{2,1,0:T(1,128)} %pad_maximum_fusion.1.in_ref), custom_call_target="tpu_custom_call" | custom-call | flops 1000000000 | bytes 32768 | tf_op jit(solution)/shard_map/gain_sums/pallas_call | solution.py:757
  387.7 0.7 convert_element_type.79
  389.1 10.8 %convolution_convert_fusion.1 = bf16[2048,192]{0,1:T(8,128)(2,1)} fusion(bf16[4096,2048]{1,0:T(8,128)(2,1)} %get-tuple-element.30, bf16[4096,192]{1,0:T(8,128)(2,1)} %attn_bwd.1), kind=kOutput, calls=%fused_computation.4 | convolution fusion | flops 3221618688 | bytes 19136512 | tf_op jit(solution)/shard_map/dot_general | solution.py:22
  399.9 9.8 %convolution_convert_fusion = bf16[2048,256]{1,0:T(8,128)(2,1)} fusion(bf16[4096,2048]{1,0:T(8,128)(2,1)} %bitcast.135, bf16[4096,256]{1,0:T(8,128)(2,1)S(1)} %bitcast.137), kind=kOutput, calls=%fused_computation.3 | convolution fusion | flops 4295491584 | bytes 19922944 | tf_op jit(solution)/shard_map/dot_general | solution.py:22
  409.7 5.5 fusion.2
  415.2 22.4 %all-gather.9.cloned.1.call-done = bf16[4096,2048]{1,0:T(8,128)(2,1)} async-done(((bf16[128,2048]{1,0:T(8,128)(2,1)}), bf16[4096,2048]{1,0:T(8,128)(2,1)}) %all-gather.9.cloned.1.call-update) | async-done | bytes 16777232 | tf_op jit(solution)/shard_map/all_gather | solution.py:835
  437.6 110.1 %all-gather.7.cloned.1.call-done = bf16[64,128,2048]{2,1,0:T(8,128)(2,1)} async-done(((bf16[2,128,2048]{2,1,0:T(8,128)(2,1)}), bf16[64,128,2048]{2,1,0:T(8,128)(2,1)}) %all-gather.7.cloned.1.call-update) | async-done | bytes 33554448 | tf_op jit(solution)/shard_map/all_gather | solution.py:823
  547.7 14.1 %out_grad.1 = bf16[64,2048]{1,0:T(8,128)(2,1)} custom-call(bf16[64,4096]{1,0:T(8,128)(2,1)} %get-tuple-element.22.in_ref.ot_ref, bf16[32,2,128,2048]{3,2,1,0:T(8,128)(2,1)} %bitcast.111), custom_call_target="tpu_custom_call" | custom-call | flops 1073741824 | bytes 16777216 | tf_op jit(solution)/shard_map/out_grad/pallas_call | solution.py:708
  561.8 17.4 %shard_map.154 = bf16[4096,2048]{1,0:T(8,128)(2,1)} custom-call(bf16[32,2,128,2048]{3,2,1,0:T(8,128)(2,1)} %bitcast.112), custom_call_target="tpu_custom_call" | custom-call | flops 10000000 | bytes 33554432 | tf_op jit(solution)/shard_map/pallas_call | solution.py:681
  579.2 14.2 %copy.37 = bf16[1,4096,2048]{2,1,0:T(8,128)(2,1)} copy(bf16[1,4096,2048]{2,1,0:T(8,128)(2,1)} %bitcast.119) | data formatting | bytes 33554432
  (58 shorter events, 6.7 us)
Async XLA Ops:
  7.2 70.5 %all-gather.5.cloned.1.call-start = ((), (), s32[]{:S(2)}) async-start(), calls=%async_computation | async-start | bytes 8650752 | tf_op jit(solution)/shard_map/all_gather | solution.py:800
  8.0 429.6 %all-gather.9.cloned.1.call-start = ((), (), s32[]{:S(2)}) async-start(), calls=%async_computation.2 | async-start | bytes 17301504 | tf_op jit(solution)/shard_map/all_gather | solution.py:835
  17.2 26.6 %copy-start.4 = (f32[128]{0:T(128)}, f32[128]{0:T(128)S(1)}, u32[]{:S(2)}) copy-start(f32[128]{0:T(128)S(1)} %broadcast_multiply_fusion.2) | copy-start | bytes 1540
  77.7 5.6 copy-start
  77.7 5.6 copy-start.1
  304.6 59.7 %copy-start.3 = (f32[2048]{0:T(1024)S(1)}, f32[2048]{0:T(1024)}, u32[]{:S(2)}) copy-start(f32[2048]{0:T(1024)} %convert_element_type.74) | copy-start | bytes 24580
  304.6 59.7 %copy-start.5 = (f32[128]{0:T(128)S(1)}, f32[128]{0:T(128)}, u32[]{:S(2)}) copy-start(f32[128]{0:T(128)} %copy-done.4) | copy-start | bytes 1540
  304.6 59.7 %copy-start.6 = (f32[128]{0:T(128)S(1)}, f32[128]{0:T(128)}, u32[]{:S(2)}) copy-start(f32[128]{0:T(128)} %add_rsqrt_fusion) | copy-start | bytes 1540
  368.6 179.1 %all-gather.7.cloned.1.call-start = ((), (), s32[]{:S(2)}) async-start(), calls=%async_computation.1 | async-start | bytes 34603008 | tf_op jit(solution)/shard_map/all_gather | solution.py:823
  389.1 10.9 %copy-start.7 = (bf16[8,512,256]{2,1,0:T(8,128)(2,1)S(1)}, bf16[8,512,256]{2,1,0:T(8,128)(2,1)}, u32[]{:S(2)}) copy-start(bf16[8,512,256]{2,1,0:T(8,128)(2,1)} %get-tuple-element.23) | copy-start | bytes 6291460
  389.1 20.6 %slice-start = ((s8[16777216]{0:T(1024)(128)(4,1)}), s8[4194304]{0:T(1024)(128)(4,1)S(1)}, s32[]{:S(2)}) async-start(s8[16777216]{0:T(1024)(128)(4,1)} %bitcast.115), calls=%async_computation.3 | async-start | bytes 8388608
  389.1 20.6 %slice-start.1 = ((s8[16777216]{0:T(1024)(128)(4,1)}), s8[4194304]{0:T(1024)(128)(4,1)S(1)}, s32[]{:S(2)}) async-start(s8[16777216]{0:T(1024)(128)(4,1)} %bitcast.115), calls=%async_computation.4 | async-start | bytes 8388608
  399.9 9.8 %slice-start.2 = ((s8[16777216]{0:T(1024)(128)(4,1)}), s8[4194304]{0:T(1024)(128)(4,1)S(1)}, s32[]{:S(2)}) async-start(s8[16777216]{0:T(1024)(128)(4,1)} %bitcast.115), calls=%async_computation.5 | async-start | bytes 8388608
  399.9 9.8 %slice-start.3 = ((s8[16777216]{0:T(1024)(128)(4,1)}), s8[4194304]{0:T(1024)(128)(4,1)S(1)}, s32[]{:S(2)}) async-start(s8[16777216]{0:T(1024)(128)(4,1)} %bitcast.115), calls=%async_computation.6 | async-start | bytes 8388608
  399.9 9.8 %copy-start.2 = (bf16[8,512,256]{2,1,0:T(8,128)(2,1)S(1)}, bf16[8,512,256]{2,1,0:T(8,128)(2,1)}, u32[]{:S(2)}) copy-start(bf16[8,512,256]{2,1,0:T(8,128)(2,1)} %get-tuple-element.24) | copy-start | bytes 6291460
Sparse Core Ops, SparseCore 0:
  10.1 51.9 all-gather.4
  368.7 68.7 all-gather.8
  439.7 108.0 all-gather.6
